TPU v7x, 8 devices: a whole 2x2x1 slice. The times are simulated.
8 devices in a mesh: sys: 2 (over z, y), row: 4 (over x, core).
Axes of the slice: x: 2, y: 2, z: 1, core: 2. Of those that a mesh axis runs over, the one named last changes fastest.
Arguments:
- positions: bfloat16 [16384, 768], P(('sys', 'row')), parts along dimension 0
- charges: float32 [16384], P(('sys', 'row')), parts along dimension 0
- counts: int32 [8], P(('sys', 'row')), parts along dimension 0
Outputs:
- output 1: float32 [16384, 768], P(('sys', 'row')), parts along dimension 0
- output 2: float32 [2], P('sys'), parts along dimension 0
There are 2 independent parts. A program takes and returns all parts, laid end to end along the dimension named above; each array names one.
All inputs are finite; a program needn't handle non-finite values.
Results may differ from a plain program's by a relative error of at most 0.001.
Values are sent between devices in bfloat16 or wider.
A program may use at most 1 GiB of HBM per device.

v0:
```python
import jax
import jax.numpy as jnp
from jax import lax
from jax.sharding import PartitionSpec as P


def sq_norm(block_pos):
    pos_f32 = block_pos.astype(jnp.float32)
    return jnp.sum(pos_f32 * pos_f32, axis=1)


def pair_weight(row_pos, row_q, col_pos, col_q, neg_scale):
    gram_mat = jnp.einsum('id,jd->ij', row_pos, col_pos, preferred_element_type=jnp.float32)
    dist_sq = jnp.maximum(sq_norm(row_pos)[:, None] + sq_norm(col_pos)[None, :] - 2.0 * gram_mat, 0.0)
    return row_q[:, None] * col_q[None, :] * jnp.exp(dist_sq * neg_scale)


def row_force(weight, w_low, row_pos, col_pos, inv_len2):
    pulled = jnp.dot(w_low, col_pos, preferred_element_type=jnp.float32)
    return (jnp.sum(weight, axis=1)[:, None] * row_pos.astype(jnp.float32) - pulled) * inv_len2


def col_force(weight, w_low, row_pos, col_pos, inv_len2):
    pushed = jnp.einsum('ij,id->jd', w_low, row_pos, preferred_element_type=jnp.float32)
    return (jnp.sum(weight, axis=0)[:, None] * col_pos.astype(jnp.float32) - pushed) * inv_len2


def solution(mesh):
    num_blocks = mesh.shape['row']
    half_way = num_blocks // 2
    next_perm = [(src, (src + 1) % num_blocks) for src in range(num_blocks)]
    home_perm = [(src, (src - half_way) % num_blocks) for src in range(num_blocks)]

    def per_device(positions, charges, counts):
        block_rows, width = positions.shape
        half_rows = block_rows // 2
        neg_scale = -0.5 / width
        inv_len2 = 1.0 / width
        live_q = jnp.where(jnp.arange(block_rows) < counts[0], charges, 0.0)
        diag_mask = jnp.arange(block_rows)[:, None] == jnp.arange(block_rows)[None, :]
        own_w = jnp.where(diag_mask, 0.0, pair_weight(positions, live_q, positions, live_q, neg_scale))
        own_force = row_force(own_w, own_w.astype(jnp.bfloat16), positions, positions, inv_len2)
        energy = 0.5 * jnp.sum(own_w)
        vis_pos = lax.ppermute(positions, 'row', next_perm)
        vis_q = lax.ppermute(live_q, 'row', next_perm)
        vis_react = jnp.zeros((block_rows, width), jnp.float32)

        def full_step(step_idx, loop_state):
            vis_pos, vis_q, vis_react, own_force, energy = loop_state
            weight = pair_weight(positions, live_q, vis_pos, vis_q, neg_scale)
            w_low = weight.astype(jnp.bfloat16)
            own_force = own_force + row_force(weight, w_low, positions, vis_pos, inv_len2)
            vis_react = vis_react + col_force(weight, w_low, positions, vis_pos, inv_len2)
            energy = energy + jnp.sum(weight)
            vis_pos = lax.ppermute(vis_pos, 'row', next_perm)
            vis_q = lax.ppermute(vis_q, 'row', next_perm)
            vis_react = lax.ppermute(vis_react, 'row', next_perm)
            return vis_pos, vis_q, vis_react, own_force, energy

        loop_state = lax.fori_loop(0, half_way - 1, full_step, (vis_pos, vis_q, vis_react, own_force, energy))
        vis_pos, vis_q, vis_react, own_force, energy = loop_state
        is_lower = lax.axis_index('row') < half_way
        a_pos = jnp.where(is_lower, positions[:half_rows], vis_pos[half_rows:])
        a_q = jnp.where(is_lower, live_q[:half_rows], vis_q[half_rows:])
        b_pos = jnp.where(is_lower, vis_pos, positions)
        b_q = jnp.where(is_lower, vis_q, live_q)
        weight = pair_weight(a_pos, a_q, b_pos, b_q, neg_scale)
        w_low = weight.astype(jnp.bfloat16)
        a_force = row_force(weight, w_low, a_pos, b_pos, inv_len2)
        b_force = col_force(weight, w_low, a_pos, b_pos, inv_len2)
        zero_half = jnp.zeros((half_rows, width), jnp.float32)
        own_force = own_force + jnp.where(is_lower, jnp.concatenate([a_force, zero_half], axis=0), b_force)
        vis_react = vis_react + jnp.where(is_lower, b_force, jnp.concatenate([zero_half, a_force], axis=0))
        energy = energy + jnp.sum(weight)
        own_force = own_force + lax.ppermute(vis_react, 'row', home_perm)
        energy = lax.psum(energy, 'row')
        return own_force, energy.reshape(1)

    row_spec = P(('sys', 'row'), None)
    vec_spec = P(('sys', 'row'))
    return jax.shard_map(per_device, mesh=mesh, in_specs=(row_spec, vec_spec, vec_spec), out_specs=(row_spec, P('sys')), check_vma=False)
```

profile of v0, /device:TPU:0, one launch (start us, length us, event | category | flops | bytes accessed | tf_op | source)
XLA Modules:
  0.0 369.3 jit_solution(2870127891763802544)
XLA Ops:
  0.6 0.9 collective-permute-start.1
  1.5 36.9 %collective-permute-done.1 = bf16[2048,768]{1,0:T(8,128)(2,1)S(1)} collective-permute-done((bf16[2048,768]{1,0:T(8,128)(2,1)}, bf16[2048,768]{1,0:T(8,128)(2,1)S(1)}, u32[]{:S(2)}, u32[]{:S(2)}) %collective-permute-start.1) | collective-permute-done | bytes 3145760 | tf_op jit(solution)/shard_map/ppermute | solution.py:44
  38.4 0.0 copy-start.3
  38.4 0.0 collective-permute-start.3
  39.0 0.7 fusion.28
  39.8 2.4 collective-permute-start
  42.2 0.0 copy-start.1
  42.2 0.7 fusion.2
  42.9 0.0 copy-done.3
  42.9 32.2 %collective-permute-done.3 = bf16[2048,768]{1,0:T(8,128)(2,1)} collective-permute-done((bf16[2048,768]{1,0:T(8,128)(2,1)S(1)}, bf16[2048,768]{1,0:T(8,128)(2,1)}, u32[]{:S(2)}, u32[]{:S(2)}) %collective-permute-start.3) | collective-permute-done | bytes 3145760 | tf_op jit(solution)/shard_map/while/body/eval_jaxpr/ppermute | solution.py:55
  75.1 0.0 copy-start.4
  75.1 5.5 %fusion.5 = (f32[2048]{0:T(1024)S(1)}, bf16[2048,768]{1,0:T(8,128)(2,1)S(1)}, f32[2048]{0:T(1024)S(1)}) fusion(bf16[2048,768]{1,0:T(8,128)(2,1)} %collective-permute-done.3, bf16[2048,768]{1,0:T(8,128)(2,1)} %param.3, pred[]{:T(512)S(6)} %lt.12), kind=kLoop, calls=%fused_computation.16 | loop fusion | flops 11005952 | bytes 9453569 | tf_op jit(solution)/shard_map/reduce_sum | solution.py:9
  80.6 0.0 collective-permute-done
  80.6 0.0 copy-done.1
  80.6 0.0 copy-done.4
  80.6 12.3 %fusion.29 = (f32[]{:T(128)}, f32[2048]{0:T(1024)S(1)}, f32[2048]{0:T(1024)S(1)}, bf16[2048,2048]{0,1:T(8,128)(2,1)S(1)}) fusion(bf16[2048,768]{1,0:T(8,128)(2,1)S(1)} %copy-done.1, bf16[2048,768]{1,0:T(8,128)(2,1)S(1)} %copy-done.4, f32[2048]{0:T(1024)S(1)} %fusion.2, f32[2048]{0:T(1024)S(1)} %get-tuple-element.38, f32[2048]{0:T(1024)S(1)} %collective-permute-done, ...), kind=kOutput, calls=%fused_computation.46 | convolution fusion | flops 6488584192 | bytes 14729220 | tf_op jit(solution)/shard_map/while/body/eval_jaxpr/id,jd->ij/dot_general | solution.py:13
  92.9 0.0 copy-start.7
  92.9 3.2 copy-done.7
  96.2 0.0 copy-start.6
  96.2 8.5 %fusion.4 = f32[2048,768]{1,0:T(8,128)} fusion(bf16[2048,768]{1,0:T(8,128)(2,1)S(1)} %copy-done.4, f32[2048]{0:T(1024)S(1)} %get-tuple-element.19, bf16[2048,768]{1,0:T(8,128)(2,1)S(1)} %copy-done.1, bf16[2048,2048]{0,1:T(8,128)(2,1)S(1)} %get-tuple-element.39), kind=kOutput, calls=%fused_computation.15 | convolution fusion | flops 6448742400 | bytes 20979712 | tf_op jit(solution)/shard_map/while/body/eval_jaxpr/ij,id->jd/dot_general | solution.py:24
  104.7 0.0 collective-permute-start.4
  104.7 1.6 collective-permute-start.2
  106.3 68.9 %collective-permute-done.2 = f32[2048]{0:T(1024)S(1)} collective-permute-done((f32[2048]{0:T(1024)S(1)}, f32[2048]{0:T(1024)S(1)}, u32[]{:S(2)}, u32[]{:S(2)}) %collective-permute-start.2) | collective-permute-done | bytes 8224 | tf_op jit(solution)/shard_map/while/body/eval_jaxpr/ppermute | solution.py:56
  175.2 0.0 copy-done.6
  175.2 2.0 fusion.19
  177.2 6.6 %fusion.31 = (f32[]{:T(128)}, f32[2048]{0:T(1024)S(1)}, f32[1024]{0:T(1024)S(1)}, bf16[1024,2048]{1,0:T(8,128)(2,1)S(1)}) fusion(bf16[1024,768]{1,0:T(8,128)(2,1)S(1)} %get-tuple-element.35, bf16[2048,768]{1,0:T(8,128)(2,1)S(1)} %get-tuple-element.37, f32[2048]{0:T(1024)S(1)} %get-tuple-element.36, f32[1024]{0:T(1024)S(1)} %get-tuple-element.34, ...), kind=kOutput, calls=%fused_computation.48 | convolution fusion | flops 3244291072 | bytes 8949764 | tf_op jit(solution)/shard_map/id,jd->ij/dot_general | solution.py:13
  183.8 3.7 fusion.22
  187.5 0.0 copy-start
  187.5 3.4 fusion.21
  191.0 0.0 copy-start.2
  191.0 0.0 collective-permute-done.4
  191.0 0.0 copy-done
  191.0 3.7 %select_add_fusion = f32[2048,768]{1,0:T(8,128)} fusion(f32[2048,768]{1,0:T(8,128)S(1)} %collective-permute-done.4, f32[1024,768]{1,0:T(8,128)S(1)} %fusion.21, f32[2048,768]{1,0:T(8,128)S(1)} %fusion.22, bf16[2048,768]{1,0:T(8,128)(2,1)S(1)} %get-tuple-element.37, f32[2048]{0:T(1024)S(1)} %get-tuple-element.32, pred[]{:T(512)S(6)} %lt.12), kind=kLoop, calls=%fused_computation.26 | loop fusion | flops 9437184 | bytes 25174016 | tf_op jit(solution)/shard_map/add | solution.py:73
  194.7 0.0 copy-done.2
  194.7 1.5 collective-permute-start.5
  196.2 15.1 %fusion.30 = (f32[]{:T(128)}, f32[2048]{0:T(1024)S(1)}, bf16[2048,2048]{0,1:T(8,128)(2,1)}) fusion(bf16[2048,768]{1,0:T(8,128)(2,1)S(1)} %copy-done.1, f32[2048]{0:T(1024)S(1)} %get-tuple-element.38, f32[2048]{0:T(1024)S(1)} %fusion.28), kind=kOutput, calls=%fused_computation.47 | convolution fusion | flops 6492780544 | bytes 11558916 | tf_op jit(solution)/shard_map/id,jd->ij/dot_general | solution.py:13
  213.2 120.2 %psum.7 = f32[1]{0:T(128)} all-reduce(f32[1]{0:T(128)} %bitcast.1), channel_id=1, replica_groups=mesh['sys'=2,'row'=4] {'row'}, use_global_device_ids=true, to_apply=%region_12.13 | all-reduce | flops 1 | bytes 8 | tf_op jit(solution)/shard_map/psum | solution.py:76
  333.5 0.0 copy-start.5
  333.5 0.0 slice-start
  333.5 12.0 %fusion = f32[2048,768]{1,0:T(8,128)} fusion(bf16[2048,768]{1,0:T(8,128)(2,1)} %param.3, bf16[2048,2048]{0,1:T(8,128)(2,1)} %get-tuple-element.41), kind=kOutput, calls=%fused_computation.7 | convolution fusion | flops 6442450944 | bytes 17825792 | tf_op jit(solution)/shard_map/dot_general | solution.py:19
  345.4 0.0 copy-done.5
  345.4 0.0 slice-start.1
  345.5 11.2 %fusion.17 = f32[2048,768]{1,0:T(8,128)} fusion(bf16[2048,768]{1,0:T(8,128)(2,1)S(1)} %copy-done.5, bf16[2048,2048]{0,1:T(8,128)(2,1)} %copy-done.7), kind=kOutput, calls=%fused_computation.29 | convolution fusion | flops 6442450944 | bytes 17825792 | tf_op jit(solution)/shard_map/while/body/eval_jaxpr/dot_general | solution.py:19
  356.7 0.0 collective-permute-done.5
  356.7 0.0 slice-done
  356.7 0.0 slice-done.1
  356.7 12.7 %fusion.13 = f32[2048,768]{1,0:T(8,128)} fusion(f32[2048,768]{1,0:T(8,128)} %collective-permute-done.5, f32[2048,768]{1,0:T(8,128)} %fusion, bf16[2048,768]{1,0:T(8,128)(2,1)} %param.3, f32[2048,768]{1,0:T(8,128)} %fusion.17, f32[1024,768]{1,0:T(8,128)} %copy-done.2, f32[2048,768]{1,0:T(8,128)S(1)} %bitcast.21, bf16[2048,768]{1,0:T(8,128)(2,1)S(1)} %get-tuple-element.37, ...), kind=kLoop, calls=%fused_computation.24 | loop fusion | flops 22020096 | bytes 40919040 | tf_op jit(solution)/shard_map/add | solution.py:75
  (3 shorter events, 0.0 us)
Async XLA Ops:
  0.6 37.8 %collective-permute-start.1 = (bf16[2048,768]{1,0:T(8,128)(2,1)}, bf16[2048,768]{1,0:T(8,128)(2,1)S(1)}, u32[]{:S(2)}, u32[]{:S(2)}) collective-permute-start(bf16[2048,768]{1,0:T(8,128)(2,1)} %param.3), channel_id=1, source_target_pairs={{0,1},{1,2},{2,3},{3,0},{4,5},{5,6},{6,7},{7,4}} | collective-permute-start | bytes 9437192 | tf_op jit(solution)/shard_map/ppermute | solution.py:44
  38.4 4.5 %copy-start.3 = (bf16[2048,768]{1,0:T(8,128)(2,1)}, bf16[2048,768]{1,0:T(8,128)(2,1)S(1)}, u32[]{:S(2)}) copy-start(bf16[2048,768]{1,0:T(8,128)(2,1)S(1)} %collective-permute-done.1) | copy-start | bytes 9437188
  38.4 36.7 %collective-permute-start.3 = (bf16[2048,768]{1,0:T(8,128)(2,1)S(1)}, bf16[2048,768]{1,0:T(8,128)(2,1)}, u32[]{:S(2)}, u32[]{:S(2)}) collective-permute-start(bf16[2048,768]{1,0:T(8,128)(2,1)S(1)} %collective-permute-done.1), channel_id=1, source_target_pairs={{0,1},{1,2},{2,3},{3,0},{4,5},{5,6},{6,7},{7,4}} | collective-permute-start | bytes 9437192 | tf_op jit(solution)/shard_map/while/body/eval_jaxpr/ppermute | solution.py:55
  39.8 40.8 %collective-permute-start = (f32[2048]{0:T(1024)S(1)}, f32[2048]{0:T(1024)S(1)}, u32[]{:S(2)}, u32[]{:S(2)}) collective-permute-start(f32[2048]{0:T(1024)S(1)} %fusion.28), channel_id=1, source_target_pairs={{0,1},{1,2},{2,3},{3,0},{4,5},{5,6},{6,7},{7,4}} | collective-permute-start | bytes 24584 | tf_op jit(solution)/shard_map/ppermute | solution.py:45
  42.2 38.4 %copy-start.1 = (bf16[2048,768]{1,0:T(8,128)(2,1)S(1)}, bf16[2048,768]{1,0:T(8,128)(2,1)}, u32[]{:S(2)}) copy-start(bf16[2048,768]{1,0:T(8,128)(2,1)} %param.3) | copy-start | bytes 9437188
  75.1 5.5 %copy-start.4 = (bf16[2048,768]{1,0:T(8,128)(2,1)S(1)}, bf16[2048,768]{1,0:T(8,128)(2,1)}, u32[]{:S(2)}) copy-start(bf16[2048,768]{1,0:T(8,128)(2,1)} %copy-done.3) | copy-start | bytes 9437188
  92.9 3.2 copy-start.7
  96.2 79.0 %copy-start.6 = (f32[2048]{0:T(1024)S(1)}, f32[2048]{0:T(1024)}, u32[]{:S(2)}) copy-start(f32[2048]{0:T(1024)} %param.4) | copy-start | bytes 24580
  104.7 86.3 %collective-permute-start.4 = (f32[2048,768]{1,0:T(8,128)}, f32[2048,768]{1,0:T(8,128)S(1)}, u32[]{:S(2)}, u32[]{:S(2)}) collective-permute-start(f32[2048,768]{1,0:T(8,128)} %fusion.4), channel_id=1, source_target_pairs={{0,1},{1,2},{2,3},{3,0},{4,5},{5,6},{6,7},{7,4}} | collective-permute-start | bytes 18874376 | tf_op jit(solution)/shard_map/while/body/eval_jaxpr/ppermute | solution.py:57
  104.7 70.5 %collective-permute-start.2 = (f32[2048]{0:T(1024)S(1)}, f32[2048]{0:T(1024)S(1)}, u32[]{:S(2)}, u32[]{:S(2)}) collective-permute-start(f32[2048]{0:T(1024)S(1)} %collective-permute-done), channel_id=1, source_target_pairs={{0,1},{1,2},{2,3},{3,0},{4,5},{5,6},{6,7},{7,4}} | collective-permute-start | bytes 24584 | tf_op jit(solution)/shard_map/while/body/eval_jaxpr/ppermute | solution.py:56
  187.5 3.5 copy-start
  191.0 3.7 %copy-start.2 = (f32[1024,768]{1,0:T(8,128)}, f32[1024,768]{1,0:T(8,128)S(1)}, u32[]{:S(2)}) copy-start(f32[1024,768]{1,0:T(8,128)S(1)} %fusion.21) | copy-start | bytes 9437188
  194.7 162.0 %collective-permute-start.5 = (f32[2048,768]{1,0:T(8,128)}, f32[2048,768]{1,0:T(8,128)}, u32[]{:S(2)}, u32[]{:S(2)}) collective-permute-start(f32[2048,768]{1,0:T(8,128)} %select_add_fusion), channel_id=1, source_target_pairs={{0,2},{1,3},{2,0},{3,1},{4,6},{5,7},{6,4},{7,5}} | collective-permute-start | bytes 18874376 | tf_op jit(solution)/shard_map/ppermute | solution.py:75
  333.5 12.0 %copy-start.5 = (bf16[2048,768]{1,0:T(8,128)(2,1)S(1)}, bf16[2048,768]{1,0:T(8,128)(2,1)}, u32[]{:S(2)}) copy-start(bf16[2048,768]{1,0:T(8,128)(2,1)} %copy-done.3) | copy-start | bytes 9437188
  333.5 23.2 %slice-start = ((s8[6291456]{0:T(1024)(128)(4,1)}), s8[4194304]{0:T(1024)(128)(4,1)S(1)}, s32[]{:S(2)}) async-start(s8[6291456]{0:T(1024)(128)(4,1)} %bitcast.20), calls=%async_computation | async-start | bytes 8388608
  345.4 11.2 %slice-start.1 = ((s8[6291456]{0:T(1024)(128)(4,1)}), s8[2097152]{0:T(1024)(128)(4,1)S(1)}, s32[]{:S(2)}) async-start(s8[6291456]{0:T(1024)(128)(4,1)} %bitcast.20), calls=%async_computation.1 | async-start | bytes 4194304
where the time goes:
time: 370 us; the launch traced here: 369 us
  waiting for transfers between devices  138 us (37%)
  blocking collectives  120 us (32%)
  matrix products  72.9 us (20%)
  other arithmetic  25.3 us (7%)
  starting transfers between devices  6.42 us (2%)
    psum x1, blocking collectives, per_device(): energy = lax.psum(energy, 'row')  120 us
    ppermute x1, waiting for transfers between devices, full_step(): vis_q = lax.ppermute(vis_q, 'row', next_perm)  68.9 us
    ppermute x1, waiting for transfers between devices, per_device(): vis_pos = lax.ppermute(positions, 'row', next_perm)  36.9 us
    dot_general x3, matrix products, pair_weight(): jnp.einsum('id,jd->ij', row_pos, col_pos, preferred_element_type=jnp.floa...  34.1 us
    ppermute x1, waiting for transfers between devices, full_step(): vis_pos = lax.ppermute(vis_pos, 'row', next_perm)  32.2 us
    dot_general x3, matrix products, row_force(): pulled = jnp.dot(w_low, col_pos, preferred_element_type=jnp.float32)  26.6 us
    add x1, other arithmetic, per_device(): own_force = own_force + lax.ppermute(vis_react, 'row', home_perm)  12.7 us
    dot_general x2, matrix products, col_force(): jnp.einsum('ij,id->jd', w_low, row_pos, preferred_element_type=jnp.float32)  12.2 us
  transfers between devices with their start and end apart: 6, of which 3 were waited for; matrix products, arithmetic and copies ran while one was open for 16% of the time, Pallas kernels for 0%

commit v1 on v0

v1 whole, which is shorter than its diff:
```python
import functools

import jax
import jax.numpy as jnp
from jax import lax
from jax.experimental import pallas as pl
from jax.experimental.pallas import tpu as pltpu
from jax.sharding import PartitionSpec as P


CHUNK = 128
ROW_TILE = 1024
LOG2E = 1.4426950408889634
F32 = jnp.float32
MESH = pl.DeviceIdType.MESH
VMEM_SPEC = pl.BlockSpec(memory_space=pltpu.VMEM)
HBM_SPEC = pl.BlockSpec(memory_space=pl.ANY)


def to_all(mine_ref, all_ref, local_sem, send_sems, recv_sems):
    me = lax.axis_index('row')
    n = all_ref.shape[0]
    barrier = pltpu.get_barrier_semaphore()
    for d in range(1, n):
        pl.semaphore_signal(barrier, inc=1, device_id={'row': lax.rem(me + d, n)}, device_id_type=MESH)
    pl.semaphore_wait(barrier, n - 1)
    local = pltpu.make_async_copy(mine_ref, all_ref.at[me], local_sem)
    local.start()
    sends = []
    for d in range(1, n):
        copy = pltpu.make_async_remote_copy(
            src_ref=mine_ref, dst_ref=all_ref.at[me], send_sem=send_sems.at[d - 1], recv_sem=recv_sems.at[d - 1],
            device_id={'row': lax.rem(me + d, n)}, device_id_type=MESH)
        copy.start()
        sends.append(copy)
    for d in range(1, n):
        src = lax.rem(me + n - d, n)
        pltpu.make_async_remote_copy(
            src_ref=mine_ref, dst_ref=all_ref.at[src], send_sem=send_sems.at[d - 1], recv_sem=recv_sems.at[d - 1],
            device_id={'row': src}, device_id_type=MESH).wait_recv()
    for copy in sends:
        copy.wait_send()
    local.wait()


def sems(n):
    return [pltpu.SemaphoreType.DMA, pltpu.SemaphoreType.DMA((n - 1,)), pltpu.SemaphoreType.DMA((n - 1,))]


def energy_kernel(mine_ref, out_ref, all_ref, local_sem, send_sems, recv_sems):
    to_all(mine_ref, all_ref, local_sem, send_sems, recv_sems)
    total = all_ref[0]
    for k in range(1, all_ref.shape[0]):
        total = total + all_ref[k]
    total = jnp.sum(total, axis=1, keepdims=True)
    out_ref[...] = 0.5 * jnp.sum(total, axis=0, keepdims=True)


def energy_call(mine, n):
    return pl.pallas_call(
        energy_kernel,
        out_shape=jax.ShapeDtypeStruct((1, 1), F32),
        in_specs=[VMEM_SPEC], out_specs=VMEM_SPEC,
        scratch_shapes=[pltpu.VMEM((n,) + mine.shape, mine.dtype)] + sems(n),
        compiler_params=pltpu.CompilerParams(collective_id=2, has_side_effects=True),
        name='energy',
    )(mine)


def count_of(info_ref):
    return jnp.max(info_ref[info_ref.shape[0] - 8:, :]).astype(jnp.int32)


def step_kernel(cfg, *refs):
    start, num, tile_chunks, first, last, diag, kappa, inv_len2 = cfg
    refs = list(refs)
    xv, rowv, my_info = refs[:3]
    refs = refs[3:]
    cols, src_info = xv, my_info
    if not diag:
        src_info, cols = refs[:2]
        refs = refs[2:]
    if not first:
        t_in, s_in = refs[:2]
        refs = refs[2:]
    if last:
        forces, part, out_sems = refs
        tv, sv = t_in, s_in
    else:
        tv, sv = refs
    rows, width = xv.shape
    block_chunks = rows // CHUNK
    num_rt = rows // ROW_TILE
    col_tile = tile_chunks * CHUNK
    live_rt = (count_of(my_info) + ROW_TILE - 1) // ROW_TILE
    live = jnp.clip((count_of(src_info) + CHUNK - 1) // CHUNK - start, 0, num)
    tiles = (live + tile_chunks - 1) // tile_chunks

    def tile(rt, ct):
        r0 = pl.multiple_of(rt * ROW_TILE, ROW_TILE)
        c0 = pl.multiple_of(ct * col_tile, col_tile)
        rsl = pl.ds(r0, ROW_TILE)
        s_sum = sv[rsl, :]
        row_a = rowv[0, rsl, :]
        row_c = rowv[1, rsl, :]
        parts = []
        for q in range(tile_chunks // 2):
            gram = lax.dot_general(xv[rsl, :], cols[pl.ds(c0 + q * 256, 256), :], (((1,), (1,)), ((), ())),
                                   preferred_element_type=F32)
            for h in range(2):
                k = 2 * q + h
                cid = start + ct * tile_chunks + k
                col_a = src_info[pl.ds(cid, 1), :]
                col_c = src_info[pl.ds(block_chunks + cid, 1), :]
                expo = jnp.minimum(gram[:, h * 128:(h + 1) * 128] * (2.0 * kappa) + row_a + col_a, 0.0)
                w = jnp.exp2(expo) * (row_c * col_c)
                if diag:
                    delta = lax.broadcasted_iota(jnp.int32, w.shape, 0) - lax.broadcasted_iota(jnp.int32, w.shape, 1)
                    w = jnp.where(delta == c0 + k * CHUNK - r0, 0.0, w)
                s_sum = s_sum + w
                parts.append(w.astype(jnp.bfloat16))
        sv[rsl, :] = s_sum
        w_all = jnp.concatenate(parts, axis=1)
        tv[rsl, :] += jnp.dot(w_all, cols[pl.ds(c0, col_tile), :], preferred_element_type=F32)

    if first:
        def clear(i, _):
            sl = pl.ds(pl.multiple_of(i * 64, 64), 64)
            tv[sl, :] = jnp.zeros((64, width), F32)
            sv[sl, :] = jnp.zeros((64, 128), F32)
            return 0

        lax.fori_loop(0, rows // 64, clear, 0)
    if last:
        part[...] = jnp.zeros_like(part)

    def row_tile(rt, _):
        def one(ct, _):
            tile(rt, ct)
            return 0

        lax.fori_loop(0, tiles, one, 0)
        if last:
            def finish(i, acc):
                base = rt * ROW_TILE + i * 64
                sl = pl.ds(pl.multiple_of(base, 64), 64)
                sums = sv[sl, :]
                total = jnp.sum(sums, axis=1, keepdims=True)
                tv[sl, :] = (total * xv[sl, :].astype(F32) - tv[sl, :]) * inv_len2
                for g in range(8):
                    acc = acc + sums[g * 8:(g + 1) * 8]
                return acc

            part[...] += lax.fori_loop(0, ROW_TILE // 64, finish, jnp.zeros((8, 128), F32))
            sl = pl.ds(pl.multiple_of(rt * ROW_TILE, ROW_TILE), ROW_TILE)
            pltpu.make_async_copy(tv.at[sl], forces.at[sl], out_sems.at[rt]).start()
        return 0

    lax.fori_loop(0, live_rt, row_tile, 0)

    if last:
        for rt in range(num_rt):
            sl = pl.ds(rt * ROW_TILE, ROW_TILE)

            @pl.when(rt >= live_rt)
            def _():
                tv[sl, :] = jnp.zeros((ROW_TILE, width), F32)
                pltpu.make_async_copy(tv.at[sl], forces.at[sl], out_sems.at[rt]).start()
        for rt in range(num_rt):
            sl = pl.ds(rt * ROW_TILE, ROW_TILE)
            pltpu.make_async_copy(tv.at[sl], forces.at[sl], out_sems.at[rt]).wait()


VMEM_LIMIT = 24 * 1024 * 1024


def step(x, rowf, my_info, src_info, cols, start, num, tile_chunks, carry, last):
    rows, width = x.shape
    first, diag = carry is None, cols is None
    cfg = (start, num, tile_chunks, first, last, diag, LOG2E * 0.5 / width, 1.0 / width)
    ins = [x, rowf, my_info] + ([] if diag else [src_info, cols]) + ([] if first else list(carry))
    in_specs = [VMEM_SPEC] * len(ins)
    num_rt = rows // ROW_TILE
    flops = int(4 * rows * num * CHUNK * width * 0.6)
    common = dict(
        in_specs=in_specs,
        compiler_params=pltpu.CompilerParams(vmem_limit_bytes=VMEM_LIMIT),
        cost_estimate=pl.CostEstimate(flops=flops, bytes_accessed=rows * width, transcendentals=0),
        name='step_%d_%d' % (start, num))
    kernel = functools.partial(step_kernel, cfg)
    if last:
        return pl.pallas_call(
            kernel,
            out_shape=(jax.ShapeDtypeStruct((rows, width), F32), jax.ShapeDtypeStruct((8, 128), F32)),
            out_specs=(HBM_SPEC, VMEM_SPEC),
            scratch_shapes=[pltpu.SemaphoreType.DMA((num_rt,))], **common)(*ins)
    return pl.pallas_call(
        kernel,
        out_shape=(pltpu.VMEM((rows, width), F32), pltpu.VMEM((rows, 128), F32)),
        out_specs=(VMEM_SPEC, VMEM_SPEC),
        input_output_aliases={} if first else {len(ins) - 2: 0, len(ins) - 1: 1}, **common)(*ins)


PIECES = (256, 512, 512, 512, 256)


def after(value, *others):
    return lax.optimization_barrier((value,) + others)[0]


def solution(mesh):
    num_blocks = mesh.shape['row']
    cross_perm = [(src, src ^ 2) for src in range(num_blocks)]
    pair_perm = [(src, src ^ 1) for src in range(num_blocks)]

    def per_device(positions, charges, counts):
        rows, width = positions.shape
        chunks = rows // CHUNK
        kappa = LOG2E * 0.5 / width
        head = positions[:PIECES[0]]
        arrived = [lax.ppermute(head, 'row', cross_perm)]
        positions = after(positions, head)
        pos_f32 = positions.astype(F32)
        row_a = -kappa * jnp.sum(pos_f32 * pos_f32, axis=1)
        live_q = jnp.where(jnp.arange(rows) < counts[0], charges, 0.0)
        info = jnp.concatenate([row_a.reshape(chunks, CHUNK), live_q.reshape(chunks, CHUNK),
                                jnp.broadcast_to(counts.astype(F32)[0], (8, CHUNK))], axis=0)
        info_cross = lax.ppermute(info, 'row', cross_perm)
        info_pair = lax.ppermute(info, 'row', pair_perm)
        x = pltpu.with_memory_space_constraint(positions, pltpu.VMEM)
        off = PIECES[0]
        for size in PIECES[1:]:
            arrived.append(lax.ppermute(positions[off:off + size], 'row', cross_perm))
            off += size
        partner = lax.ppermute(positions, 'row', pair_perm)
        rowf = jnp.stack([jnp.broadcast_to(row_a[:, None], (rows, 128)), jnp.broadcast_to(live_q[:, None], (rows, 128))])
        rowf = pltpu.with_memory_space_constraint(rowf, pltpu.VMEM)

        carry = step(x, rowf, info, None, None, 0, chunks, 4, None, False)
        partner, *carry = lax.optimization_barrier((partner, *carry))
        carry = step(x, rowf, info, info_pair, partner, 0, chunks, 4, carry, False)
        info_cross, *carry = lax.optimization_barrier((info_cross, *carry))
        info_diag = lax.ppermute(info_cross, 'row', pair_perm)
        off = 0
        for k, piece in enumerate(arrived):
            num = PIECES[k] // CHUNK
            piece, *carry = lax.optimization_barrier((piece, *carry))
            relay = lax.ppermute(piece, 'row', pair_perm)
            carry = step(x, rowf, info, info_cross, piece, off, num, min(4, num), carry, False)
            carry = step(x, rowf, info, info_diag, relay, off, num, min(4, num), carry, k == len(PIECES) - 1)
            off += num
        forces, part = carry
        return forces, energy_call(part, num_blocks).reshape(1)

    row_spec = P(('sys', 'row'), None)
    vec_spec = P(('sys', 'row'))
    return jax.shard_map(per_device, mesh=mesh, in_specs=(row_spec, vec_spec, vec_spec), out_specs=(row_spec, P('sys')), check_vma=False)
```

time: 370 us -> 121 us (0.33)
  the two profiles are of different devices: /device:TPU:0 before, /device:TPU:5 now
where the time goes in v1:
time: 121 us
  Pallas kernels  66 us (55%)
  waiting for transfers between devices  36.2 us (30%)
  starting transfers between devices  7.57 us (6%)
  local copies, waits for them, and re-layouts  4.14 us (3%)
  other arithmetic  3.65 us (3%)
  between operations  3.3 us (3%)
    pallas_call x11, Pallas kernels, step(): pl.pallas_call(kernel, out_shape=(pltpu.VMEM((rows, width), F32), pltpu.V...  52.8 us
    ppermute x4, waiting for transfers between devices, per_device(): arrived.append(lax.ppermute(positions[off:off + size], 'row', cross_perm))  30 us
    pallas_call x1, Pallas kernels, step(): pl.pallas_call(kernel, out_shape=(jax.ShapeDtypeStruct((rows, width), F32...  8.52 us
    ppermute x5, waiting for transfers between devices, per_device(): relay = lax.ppermute(piece, 'row', pair_perm)  6.18 us
    pallas_call x1, Pallas kernels, energy_call(): pl.pallas_call(energy_kernel, out_shape=jax.ShapeDtypeStruct((1, 1), F32)...  4.69 us
    ppermute x5, starting transfers between devices, per_device(): relay = lax.ppermute(piece, 'row', pair_perm)  4.1 us
    reduce_sum x1, other arithmetic, per_device(): row_a = -kappa * jnp.sum(pos_f32 * pos_f32, axis=1)  2.57 us
  transfers between devices with their start and end apart: 14, of which 7 were waited for; matrix products, arithmetic and copies ran while one was open for 5% of the time, Pallas kernels for 44%

profile of v1, /device:TPU:5, one launch (start us, length us, event | category | flops | bytes accessed | tf_op | source)
XLA Modules:
  0.0 120.9 jit_solution(17895616535874164557)
XLA Ops:
  0.6 0.0 copy-start.2
  0.6 1.0 slice.15
  1.7 0.7 collective-permute-start.2
  3.0 0.1 pad.2.clone
  3.1 2.6 %multiply_reduce_fusion = f32[2048]{0:T(1024)S(1)} fusion(bf16[2048,768]{1,0:T(8,128)(2,1)} %refs_0_.11), kind=kLoop, calls=%fused_computation | loop fusion | flops 4716544 | bytes 3153920 | tf_op jit(solution)/shard_map/reduce_sum | solution.py:224
  5.7 0.0 copy-start
  5.7 0.9 fusion.3
  6.6 0.1 maximum_maximum_fusion.refs_2_
  6.6 0.0 collective-permute-start.1
  6.6 1.2 %collective-permute-start = (f32[40,128]{1,0:T(8,128)S(1)}, f32[40,128]{1,0:T(8,128)S(1)}, u32[]{:S(2)}, u32[]{:S(2)}) collective-permute-start(f32[40,128]{1,0:T(8,128)S(1)} %maximum_maximum_fusion.refs_2_), channel_id=1, source_target_pairs={{0,2},{1,3},{2,0},{3,1},{4,6},{5,7},{6,4},{7,5}} | collective-permute-start | bytes 61448 | tf_op jit(solution)/shard_map/ppermute | solution.py:228
  7.9 0.3 collective-permute-start.8
  8.1 1.8 %fusion.2 = (bf16[512,768]{1,0:T(8,128)(2,1)S(1)}, bf16[512,768]{1,0:T(8,128)(2,1)S(1)}, bf16[512,768]{1,0:T(8,128)(2,1)S(1)}) fusion(bf16[2048,768]{1,0:T(8,128)(2,1)} %refs_0_.11), kind=kLoop, calls=%fused_computation.7 | loop fusion | bytes 4718592 | tf_op jit(solution)/shard_map/slice | solution.py:233
  9.9 1.2 %collective-permute-start.7 = (bf16[512,768]{1,0:T(8,128)(2,1)S(1)}, bf16[512,768]{1,0:T(8,128)(2,1)S(1)}, u32[]{:S(2)}, u32[]{:S(2)}) collective-permute-start(bf16[512,768]{1,0:T(8,128)(2,1)S(1)} %get-tuple-element.94), channel_id=1, source_target_pairs={{0,2},{1,3},{2,0},{3,1},{4,6},{5,7},{6,4},{7,5}} | collective-permute-start | bytes 2359304 | tf_op jit(solution)/shard_map/ppermute | solution.py:233
  11.1 0.3 stack_broadcast_in_dim.4
  11.4 0.3 stack_broadcast_in_dim.5
  11.8 0.1 pad_maximum_fusion.refs_1_
  11.9 18.9 %step_0_16.2 = (f32[2048,768]{1,0:T(8,128)S(1)}, f32[2048,128]{1,0:T(8,128)S(1)}) custom-call(bf16[2048,768]{1,0:T(8,128)(2,1)S(1)} %copy-done, f32[2,2048,128]{2,1,0:T(8,128)S(1)} %pad_maximum_fusion.refs_1_, f32[40,128]{1,0:T(8,128)S(1)} %maximum_maximum_fusion.refs_2_), custom_call_target="tpu_custom_call" | custom-call | flops 7730940928 | bytes 1572864 | tf_op jit(solution)/shard_map/step_0_16/pallas_call | solution.py:197
  30.9 0.0 collective-permute-done.1.refs_3_
  30.9 12.7 %step_0_16.3 = (f32[2048,768]{1,0:T(8,128)S(1)}, f32[2048,128]{1,0:T(8,128)S(1)}) custom-call(bf16[2048,768]{1,0:T(8,128)(2,1)S(1)} %copy-done, f32[2,2048,128]{2,1,0:T(8,128)S(1)} %pad_maximum_fusion.refs_1_, f32[40,128]{1,0:T(8,128)S(1)} %maximum_maximum_fusion.refs_2_, ...), custom_call_target="tpu_custom_call", output_to_operand_aliasing={{0}: (5, {}), {1}: (6, {})} | custom-call | flops 7730940928 | bytes 1572864 | tf_op jit(solution)/shard_map/step_0_16/pallas_call | solution.py:197
  43.6 0.0 collective-permute-done.refs_3_
  43.6 1.0 collective-permute-start.9
  44.6 0.0 collective-permute-start.3
  44.7 3.6 %step_0_2.2 = (f32[2048,768]{1,0:T(8,128)S(1)}, f32[2048,128]{1,0:T(8,128)S(1)}) custom-call(bf16[2048,768]{1,0:T(8,128)(2,1)S(1)} %copy-done, f32[2,2048,128]{2,1,0:T(8,128)S(1)} %pad_maximum_fusion.refs_1_, f32[40,128]{1,0:T(8,128)S(1)} %maximum_maximum_fusion.refs_2_, ...), custom_call_target="tpu_custom_call", output_to_operand_aliasing={{0}: (5, {}), {1}: (6, {})} | custom-call | flops 966367616 | bytes 1572864 | tf_op jit(solution)/shard_map/step_0_2/pallas_call | solution.py:197
  48.3 0.0 collective-permute-done.9.refs_4_
  48.3 3.6 %step_0_2.3 = (f32[2048,768]{1,0:T(8,128)S(1)}, f32[2048,128]{1,0:T(8,128)S(1)}) custom-call(bf16[2048,768]{1,0:T(8,128)(2,1)S(1)} %copy-done, f32[2,2048,128]{2,1,0:T(8,128)S(1)} %pad_maximum_fusion.refs_1_, f32[40,128]{1,0:T(8,128)S(1)} %maximum_maximum_fusion.refs_2_, ...), custom_call_target="tpu_custom_call", output_to_operand_aliasing={{0}: (5, {}), {1}: (6, {})} | custom-call | flops 966367616 | bytes 1572864 | tf_op jit(solution)/shard_map/step_0_2/pallas_call | solution.py:197
  51.9 0.0 collective-permute-done.7.refs_4_
  52.0 0.5 collective-permute-start.10
  52.5 0.2 step_2_4.2
  52.6 1.7 %collective-permute-done.10.refs_4_ = bf16[512,768]{1,0:T(8,128)(2,1)S(1)} collective-permute-done((bf16[512,768]{1,0:T(8,128)(2,1)S(1)}, bf16[512,768]{1,0:T(8,128)(2,1)S(1)}, u32[]{:S(2)}, u32[]{:S(2)}) %collective-permute-start.10) | collective-permute-done | bytes 786464 | tf_op jit(solution)/shard_map/ppermute | solution.py:248
  54.4 4.4 %step_2_4.3 = (f32[2048,768]{1,0:T(8,128)S(1)}, f32[2048,128]{1,0:T(8,128)S(1)}) custom-call(bf16[2048,768]{1,0:T(8,128)(2,1)S(1)} %copy-done, f32[2,2048,128]{2,1,0:T(8,128)S(1)} %pad_maximum_fusion.refs_1_, f32[40,128]{1,0:T(8,128)S(1)} %maximum_maximum_fusion.refs_2_, ...), custom_call_target="tpu_custom_call", output_to_operand_aliasing={{0}: (5, {}), {1}: (6, {})} | custom-call | flops 1932735232 | bytes 1572864 | tf_op jit(solution)/shard_map/step_2_4/pallas_call | solution.py:197
  58.7 12.8 %collective-permute-done.6.refs_4_ = bf16[512,768]{1,0:T(8,128)(2,1)S(1)} collective-permute-done((bf16[512,768]{1,0:T(8,128)(2,1)S(1)}, bf16[512,768]{1,0:T(8,128)(2,1)S(1)}, u32[]{:S(2)}, u32[]{:S(2)}) %collective-permute-start.6) | collective-permute-done | bytes 786464 | tf_op jit(solution)/shard_map/ppermute | solution.py:233
  71.5 0.9 collective-permute-start.11
  72.4 0.3 step_6_4.2
  72.8 1.6 %collective-permute-done.11.refs_4_ = bf16[512,768]{1,0:T(8,128)(2,1)S(1)} collective-permute-done((bf16[512,768]{1,0:T(8,128)(2,1)S(1)}, bf16[512,768]{1,0:T(8,128)(2,1)S(1)}, u32[]{:S(2)}, u32[]{:S(2)}) %collective-permute-start.11) | collective-permute-done | bytes 786464 | tf_op jit(solution)/shard_map/ppermute | solution.py:248
  74.3 4.4 %step_6_4.3 = (f32[2048,768]{1,0:T(8,128)S(1)}, f32[2048,128]{1,0:T(8,128)S(1)}) custom-call(bf16[2048,768]{1,0:T(8,128)(2,1)S(1)} %copy-done, f32[2,2048,128]{2,1,0:T(8,128)S(1)} %pad_maximum_fusion.refs_1_, f32[40,128]{1,0:T(8,128)S(1)} %maximum_maximum_fusion.refs_2_, ...), custom_call_target="tpu_custom_call", output_to_operand_aliasing={{0}: (5, {}), {1}: (6, {})} | custom-call | flops 1932735232 | bytes 1572864 | tf_op jit(solution)/shard_map/step_6_4/pallas_call | solution.py:197
  78.7 12.8 %collective-permute-done.5.refs_4_ = bf16[512,768]{1,0:T(8,128)(2,1)S(1)} collective-permute-done((bf16[512,768]{1,0:T(8,128)(2,1)S(1)}, bf16[512,768]{1,0:T(8,128)(2,1)S(1)}, u32[]{:S(2)}, u32[]{:S(2)}) %collective-permute-start.5) | collective-permute-done | bytes 786464 | tf_op jit(solution)/shard_map/ppermute | solution.py:233
  91.5 0.9 collective-permute-start.12
  92.4 0.0 collective-permute-start.4
  92.4 0.2 step_10_4.2
  92.6 1.7 %collective-permute-done.12.refs_4_ = bf16[512,768]{1,0:T(8,128)(2,1)S(1)} collective-permute-done((bf16[512,768]{1,0:T(8,128)(2,1)S(1)}, bf16[512,768]{1,0:T(8,128)(2,1)S(1)}, u32[]{:S(2)}, u32[]{:S(2)}) %collective-permute-start.12) | collective-permute-done | bytes 786464 | tf_op jit(solution)/shard_map/ppermute | solution.py:248
  94.3 4.3 %step_10_4.3 = (f32[2048,768]{1,0:T(8,128)S(1)}, f32[2048,128]{1,0:T(8,128)S(1)}) custom-call(bf16[2048,768]{1,0:T(8,128)(2,1)S(1)} %copy-done, f32[2,2048,128]{2,1,0:T(8,128)S(1)} %pad_maximum_fusion.refs_1_, f32[40,128]{1,0:T(8,128)S(1)} %maximum_maximum_fusion.refs_2_, ...), custom_call_target="tpu_custom_call", output_to_operand_aliasing={{0}: (5, {}), {1}: (6, {})} | custom-call | flops 1932735232 | bytes 1572864 | tf_op jit(solution)/shard_map/step_10_4/pallas_call | solution.py:197
  98.6 4.5 %collective-permute-done.4.refs_4_ = bf16[256,768]{1,0:T(8,128)(2,1)S(1)} collective-permute-done((bf16[256,768]{1,0:T(8,128)(2,1)S(1)}, bf16[256,768]{1,0:T(8,128)(2,1)S(1)}, u32[]{:S(2)}, u32[]{:S(2)}) %collective-permute-start.4) | collective-permute-done | bytes 393248 | tf_op jit(solution)/shard_map/ppermute | solution.py:233
  103.1 0.9 collective-permute-start.13
  103.9 0.2 step_14_2.2
  104.1 1.2 collective-permute-done.13.refs_4_
  105.3 8.5 %step_14_2.3 = (f32[2048,768]{1,0:T(8,128)}, f32[8,128]{1,0:T(8,128)S(1)}) custom-call(bf16[2048,768]{1,0:T(8,128)(2,1)S(1)} %copy-done, f32[2,2048,128]{2,1,0:T(8,128)S(1)} %pad_maximum_fusion.refs_1_, f32[40,128]{1,0:T(8,128)S(1)} %maximum_maximum_fusion.refs_2_, f32[40,128]{1,0:T(8,128)S(1)} %collective-permute-done.3.refs_3_, ...), custom_call_target="tpu_custom_call" | custom-call | flops 966367616 | bytes 1572864 | tf_op jit(solution)/shard_map/step_14_2/pallas_call | solution.py:192
  113.8 0.6 copy-done.1
  114.4 4.7 %energy.1 = f32[1,1]{1,0:T(1,128)} custom-call(f32[8,128]{1,0:T(8,128)} %copy-done.1), custom_call_target="tpu_custom_call" | custom-call | tf_op jit(solution)/shard_map/energy/pallas_call | solution.py:60
  (12 shorter events, 0.1 us)
Async XLA Ops:
  0.6 10.5 %copy-start.2 = (f32[2048]{0:T(1024)S(1)}, f32[2048]{0:T(1024)}, u32[]{:S(2)}) copy-start(f32[2048]{0:T(1024)} %param.4) | copy-start | bytes 24580
  1.7 29.2 %collective-permute-start.2 = (bf16[2048,768]{1,0:T(8,128)(2,1)}, bf16[2048,768]{1,0:T(8,128)(2,1)S(1)}, u32[]{:S(2)}, u32[]{:S(2)}) collective-permute-start(bf16[2048,768]{1,0:T(8,128)(2,1)} %refs_0_.11), channel_id=1, source_target_pairs={{0,1},{1,0},{2,3},{3,2},{4,5},{5,4},{6,7},{7,6}} | collective-permute-start | bytes 9437192 | tf_op jit(solution)/shard_map/ppermute | solution.py:235
  5.7 6.2 %copy-start = (bf16[2048,768]{1,0:T(8,128)(2,1)S(1)}, bf16[2048,768]{1,0:T(8,128)(2,1)}, u32[]{:S(2)}) copy-start(bf16[2048,768]{1,0:T(8,128)(2,1)} %refs_0_.11) | copy-start | bytes 9437188
  6.6 24.3 %collective-permute-start.1 = (f32[40,128]{1,0:T(8,128)S(1)}, f32[40,128]{1,0:T(8,128)S(1)}, u32[]{:S(2)}, u32[]{:S(2)}) collective-permute-start(f32[40,128]{1,0:T(8,128)S(1)} %maximum_maximum_fusion.refs_2_), channel_id=1, source_target_pairs={{0,1},{1,0},{2,3},{3,2},{4,5},{5,4},{6,7},{7,6}} | collective-permute-start | bytes 61448 | tf_op jit(solution)/shard_map/ppermute | solution.py:229
  6.6 37.0 %collective-permute-start = (f32[40,128]{1,0:T(8,128)S(1)}, f32[40,128]{1,0:T(8,128)S(1)}, u32[]{:S(2)}, u32[]{:S(2)}) collective-permute-start(f32[40,128]{1,0:T(8,128)S(1)} %maximum_maximum_fusion.refs_2_), channel_id=1, source_target_pairs={{0,2},{1,3},{2,0},{3,1},{4,6},{5,7},{6,4},{7,5}} | collective-permute-start | bytes 61448 | tf_op jit(solution)/shard_map/ppermute | solution.py:228
  7.9 35.8 %collective-permute-start.8 = (bf16[256,768]{1,0:T(8,128)(2,1)S(1)}, bf16[256,768]{1,0:T(8,128)(2,1)S(1)}, u32[]{:S(2)}, u32[]{:S(2)}) collective-permute-start(bf16[256,768]{1,0:T(8,128)(2,1)S(1)} %slice.15), channel_id=1, source_target_pairs={{0,2},{1,3},{2,0},{3,1},{4,6},{5,7},{6,4},{7,5}} | collective-permute-start | bytes 1179656 | tf_op jit(solution)/shard_map/ppermute | solution.py:221
  9.9 42.1 %collective-permute-start.7 = (bf16[512,768]{1,0:T(8,128)(2,1)S(1)}, bf16[512,768]{1,0:T(8,128)(2,1)S(1)}, u32[]{:S(2)}, u32[]{:S(2)}) collective-permute-start(bf16[512,768]{1,0:T(8,128)(2,1)S(1)} %get-tuple-element.94), channel_id=1, source_target_pairs={{0,2},{1,3},{2,0},{3,1},{4,6},{5,7},{6,4},{7,5}} | collective-permute-start | bytes 2359304 | tf_op jit(solution)/shard_map/ppermute | solution.py:233
  43.6 4.7 %collective-permute-start.9 = (bf16[256,768]{1,0:T(8,128)(2,1)S(1)}, bf16[256,768]{1,0:T(8,128)(2,1)S(1)}, u32[]{:S(2)}, u32[]{:S(2)}) collective-permute-start(bf16[256,768]{1,0:T(8,128)(2,1)S(1)} %collective-permute-done.8.refs_4_), channel_id=1, source_target_pairs={{0,1},{1,0},{2,3},{3,2},{4,5},{5,4},{6,7},{7,6}} | collective-permute-start | bytes 1179656 | tf_op jit(solution)/shard_map/ppermute | solution.py:248
  44.6 3.7 %collective-permute-start.3 = (f32[40,128]{1,0:T(8,128)S(1)}, f32[40,128]{1,0:T(8,128)S(1)}, u32[]{:S(2)}, u32[]{:S(2)}) collective-permute-start(f32[40,128]{1,0:T(8,128)S(1)} %collective-permute-done.refs_3_), channel_id=1, source_target_pairs={{0,1},{1,0},{2,3},{3,2},{4,5},{5,4},{6,7},{7,6}} | collective-permute-start | bytes 61448 | tf_op jit(solution)/shard_map/ppermute | solution.py:243
  52.0 2.4 %collective-permute-start.10 = (bf16[512,768]{1,0:T(8,128)(2,1)S(1)}, bf16[512,768]{1,0:T(8,128)(2,1)S(1)}, u32[]{:S(2)}, u32[]{:S(2)}) collective-permute-start(bf16[512,768]{1,0:T(8,128)(2,1)S(1)} %collective-permute-done.7.refs_4_), channel_id=1, source_target_pairs={{0,1},{1,0},{2,3},{3,2},{4,5},{5,4},{6,7},{7,6}} | collective-permute-start | bytes 2359304 | tf_op jit(solution)/shard_map/ppermute | solution.py:248
  52.4 19.1 %collective-permute-start.6 = (bf16[512,768]{1,0:T(8,128)(2,1)S(1)}, bf16[512,768]{1,0:T(8,128)(2,1)S(1)}, u32[]{:S(2)}, u32[]{:S(2)}) collective-permute-start(bf16[512,768]{1,0:T(8,128)(2,1)S(1)} %get-tuple-element.95), channel_id=1, source_target_pairs={{0,2},{1,3},{2,0},{3,1},{4,6},{5,7},{6,4},{7,5}} | collective-permute-start | bytes 2359304 | tf_op jit(solution)/shard_map/ppermute | solution.py:233
  71.5 2.8 %collective-permute-start.11 = (bf16[512,768]{1,0:T(8,128)(2,1)S(1)}, bf16[512,768]{1,0:T(8,128)(2,1)S(1)}, u32[]{:S(2)}, u32[]{:S(2)}) collective-permute-start(bf16[512,768]{1,0:T(8,128)(2,1)S(1)} %collective-permute-done.6.refs_4_), channel_id=1, source_target_pairs={{0,1},{1,0},{2,3},{3,2},{4,5},{5,4},{6,7},{7,6}} | collective-permute-start | bytes 2359304 | tf_op jit(solution)/shard_map/ppermute | solution.py:248
  72.4 19.1 %collective-permute-start.5 = (bf16[512,768]{1,0:T(8,128)(2,1)S(1)}, bf16[512,768]{1,0:T(8,128)(2,1)S(1)}, u32[]{:S(2)}, u32[]{:S(2)}) collective-permute-start(bf16[512,768]{1,0:T(8,128)(2,1)S(1)} %get-tuple-element.96), channel_id=1, source_target_pairs={{0,2},{1,3},{2,0},{3,1},{4,6},{5,7},{6,4},{7,5}} | collective-permute-start | bytes 2359304 | tf_op jit(solution)/shard_map/ppermute | solution.py:233
  91.5 2.8 %collective-permute-start.12 = (bf16[512,768]{1,0:T(8,128)(2,1)S(1)}, bf16[512,768]{1,0:T(8,128)(2,1)S(1)}, u32[]{:S(2)}, u32[]{:S(2)}) collective-permute-start(bf16[512,768]{1,0:T(8,128)(2,1)S(1)} %collective-permute-done.5.refs_4_), channel_id=1, source_target_pairs={{0,1},{1,0},{2,3},{3,2},{4,5},{5,4},{6,7},{7,6}} | collective-permute-start | bytes 2359304 | tf_op jit(solution)/shard_map/ppermute | solution.py:248
  92.4 10.7 %collective-permute-start.4 = (bf16[256,768]{1,0:T(8,128)(2,1)S(1)}, bf16[256,768]{1,0:T(8,128)(2,1)S(1)}, u32[]{:S(2)}, u32[]{:S(2)}) collective-permute-start(bf16[256,768]{1,0:T(8,128)(2,1)S(1)} %slice.16), channel_id=1, source_target_pairs={{0,2},{1,3},{2,0},{3,1},{4,6},{5,7},{6,4},{7,5}} | collective-permute-start | bytes 1179656 | tf_op jit(solution)/shard_map/ppermute | solution.py:233
  103.1 2.2 %collective-permute-start.13 = (bf16[256,768]{1,0:T(8,128)(2,1)S(1)}, bf16[256,768]{1,0:T(8,128)(2,1)S(1)}, u32[]{:S(2)}, u32[]{:S(2)}) collective-permute-start(bf16[256,768]{1,0:T(8,128)(2,1)S(1)} %collective-permute-done.4.refs_4_), channel_id=1, source_target_pairs={{0,1},{1,0},{2,3},{3,2},{4,5},{5,4},{6,7},{7,6}} | collective-permute-start | bytes 1179656 | tf_op jit(solution)/shard_map/ppermute | solution.py:248
  113.8 0.6 copy-start.1

commit v2 on v1

v2 whole, which is shorter than its diff:
```python
import functools

import jax
import jax.numpy as jnp
from jax import lax
from jax.experimental import pallas as pl
from jax.experimental.pallas import tpu as pltpu
from jax.sharding import PartitionSpec as P


CHUNK = 128
ROW_TILE = 1024
LOG2E = 1.4426950408889634
F32 = jnp.float32
VMEM_SPEC = pl.BlockSpec(memory_space=pltpu.VMEM)
HBM_SPEC = pl.BlockSpec(memory_space=pl.ANY)
FINISH_TILE = 128


def prep_kernel(kappa, x_hbm, q_ref, count_ref, xv, rowv, info, sems):
    rows = xv.shape[0]
    chunks = rows // CHUNK
    part = rows // 4
    for k in range(4):
        pltpu.make_async_copy(x_hbm.at[pl.ds(k * part, part)], xv.at[pl.ds(k * part, part)], sems.at[k]).start()
    eye = lax.broadcasted_iota(jnp.int32, (CHUNK, CHUNK), 0) == lax.broadcasted_iota(jnp.int32, (CHUNK, CHUNK), 1)
    lane = lax.broadcasted_iota(jnp.int32, (1, CHUNK), 1)
    count = count_ref[0]
    info[2 * chunks:, :] = jnp.full((8, CHUNK), count, jnp.int32).astype(F32)
    for k in range(4):
        pltpu.make_async_copy(x_hbm.at[pl.ds(k * part, part)], xv.at[pl.ds(k * part, part)], sems.at[k]).wait()

        def one(c, _):
            sl = pl.ds(pl.multiple_of(c * CHUNK, CHUNK), CHUNK)
            block = xv[sl, :].astype(F32)
            col_s = -kappa * jnp.sum(block * block, axis=1, keepdims=True)
            rowv[0, sl, :] = jnp.broadcast_to(col_s, (CHUNK, CHUNK))
            info[pl.ds(c, 1), :] = jnp.sum(jnp.where(eye, col_s, 0.0), axis=0, keepdims=True)
            live = jnp.where(lane + c * CHUNK < count, q_ref[pl.ds(c, 1), :], 0.0)
            info[pl.ds(chunks + c, 1), :] = live
            rowv[1, sl, :] = jnp.broadcast_to(jnp.sum(jnp.where(eye, live, 0.0), axis=1, keepdims=True), (CHUNK, CHUNK))
            return 0
        lax.fori_loop(k * chunks // 4, (k + 1) * chunks // 4, one, 0)


def prep(positions, charges, counts):
    rows, width = positions.shape
    chunks = rows // CHUNK
    return pl.pallas_call(
        functools.partial(prep_kernel, LOG2E * 0.5 / width),
        out_shape=[pltpu.VMEM((rows, width), positions.dtype), pltpu.VMEM((2, rows, CHUNK), F32),
                   jax.ShapeDtypeStruct((2 * chunks + 8, CHUNK), F32)],
        in_specs=[HBM_SPEC, VMEM_SPEC, pl.BlockSpec(memory_space=pltpu.SMEM)], out_specs=[VMEM_SPEC] * 3,
        scratch_shapes=[pltpu.SemaphoreType.DMA((4,))],
        compiler_params=pltpu.CompilerParams(vmem_limit_bytes=VMEM_LIMIT),
        name='prep')(positions, charges.reshape(chunks, CHUNK), counts)


def count_of(info_ref):
    return jnp.max(info_ref[info_ref.shape[0] - 8:, :]).astype(jnp.int32)


def step_kernel(cfg, *refs):
    start, num, tile_chunks, first, last, diag, kappa = cfg
    refs = list(refs)
    xv, rowv, my_info = refs[:3]
    refs = refs[3:]
    cols, src_info = xv, my_info
    if not diag:
        src_info, cols = refs[:2]
        refs = refs[2:]
    if not first:
        refs = refs[2:]
    tv, sv = refs[:2]
    rows, width = xv.shape
    block_chunks = rows // CHUNK
    col_tile = tile_chunks * CHUNK
    live_rt = (count_of(my_info) + ROW_TILE - 1) // ROW_TILE
    live = jnp.clip((count_of(src_info) + CHUNK - 1) // CHUNK - start, 0, num)
    tiles = (live + tile_chunks - 1) // tile_chunks

    def tile(rt, ct):
        r0 = pl.multiple_of(rt * ROW_TILE, ROW_TILE)
        c0 = pl.multiple_of(ct * col_tile, col_tile)
        rsl = pl.ds(r0, ROW_TILE)
        s_sum = sv[rsl, :]
        row_a = rowv[0, rsl, :]
        row_c = rowv[1, rsl, :]
        parts = []
        for q in range(tile_chunks // 2):
            gram = lax.dot_general(xv[rsl, :], cols[pl.ds(c0 + q * 256, 256), :], (((1,), (1,)), ((), ())),
                                   preferred_element_type=F32)
            for h in range(2):
                k = 2 * q + h
                cid = start + ct * tile_chunks + k
                col_a = src_info[pl.ds(cid, 1), :]
                col_c = src_info[pl.ds(block_chunks + cid, 1), :]
                expo = jnp.minimum(gram[:, h * 128:(h + 1) * 128] * (2.0 * kappa) + row_a + col_a, 0.0)
                w = jnp.exp2(expo) * (row_c * col_c)
                if diag:
                    delta = lax.broadcasted_iota(jnp.int32, w.shape, 0) - lax.broadcasted_iota(jnp.int32, w.shape, 1)
                    w = jnp.where(delta == c0 + k * CHUNK - r0, 0.0, w)
                s_sum = s_sum + w
                parts.append(w.astype(jnp.bfloat16))
        sv[rsl, :] = s_sum
        w_all = jnp.concatenate(parts, axis=1)
        tv[rsl, :] += jnp.dot(w_all, cols[pl.ds(c0, col_tile), :], preferred_element_type=F32)

    if first:
        def clear(i, _):
            sl = pl.ds(pl.multiple_of(i * 64, 64), 64)
            tv[sl, :] = jnp.zeros((64, width), F32)
            sv[sl, :] = jnp.zeros((64, 128), F32)
            return 0
        lax.fori_loop(0, rows // 64, clear, 0)
    def row_tile(rt, _):
        def one(ct, _):
            tile(rt, ct)
            return 0
        lax.fori_loop(0, tiles, one, 0)
        return 0
    lax.fori_loop(0, live_rt, row_tile, 0)

    if last:
        def add(i, acc):
            sums = sv[pl.ds(pl.multiple_of(i * 128, 128), 128), :]
            for g in range(16):
                acc = acc + sums[g * 8:(g + 1) * 8]
            return acc
        refs[2][...] = lax.fori_loop(0, rows // 128, add, jnp.zeros((8, 128), F32))


def finish_kernel(inv_len2, xv, tv, sv, forces, buf, out_sems):
    num = xv.shape[0] // FINISH_TILE

    def out(i):
        return pltpu.make_async_copy(
            buf.at[lax.rem(i, 4)], forces.at[pl.ds(pl.multiple_of(i * FINISH_TILE, FINISH_TILE), FINISH_TILE)], out_sems.at[lax.rem(i, 4)])

    def one(i, _):
        @pl.when(i >= 4)
        def _():
            out(i - 4).wait()
        sl = pl.ds(pl.multiple_of(i * FINISH_TILE, FINISH_TILE), FINISH_TILE)
        total = jnp.sum(sv[sl, :], axis=1, keepdims=True)
        buf[lax.rem(i, 4)] = (total * xv[sl, :].astype(F32) - tv[sl, :]) * inv_len2
        out(i).start()
        return 0
    lax.fori_loop(0, num, one, 0)
    for i in range(num - 4, num):
        out(i).wait()


def finish(x, tv, sv):
    rows, width = x.shape
    return pl.pallas_call(
        functools.partial(finish_kernel, 1.0 / width),
        out_shape=jax.ShapeDtypeStruct((rows, width), F32),
        in_specs=[VMEM_SPEC] * 3, out_specs=HBM_SPEC,
        scratch_shapes=[pltpu.VMEM((4, FINISH_TILE, width), F32), pltpu.SemaphoreType.DMA((4,))],
        compiler_params=pltpu.CompilerParams(vmem_limit_bytes=VMEM_LIMIT),
        cost_estimate=pl.CostEstimate(flops=rows * width * 1000, bytes_accessed=rows * width * 4, transcendentals=0),
        name='finish')(x, tv, sv)


VMEM_LIMIT = 24 * 1024 * 1024


def step(x, rowf, my_info, src_info, cols, start, num, tile_chunks, carry, last):
    rows, width = x.shape
    first, diag = carry is None, cols is None
    cfg = (start, num, tile_chunks, first, last, diag, LOG2E * 0.5 / width)
    ins = [x, rowf, my_info] + ([] if diag else [src_info, cols]) + ([] if first else list(carry))
    in_specs = [VMEM_SPEC] * len(ins)
    flops = int(4 * rows * num * CHUNK * width * 0.6)
    common = dict(
        in_specs=in_specs,
        compiler_params=pltpu.CompilerParams(vmem_limit_bytes=VMEM_LIMIT),
        cost_estimate=pl.CostEstimate(flops=flops, bytes_accessed=rows * width, transcendentals=0),
        name='step_%d_%d' % (start, num))
    kernel = functools.partial(step_kernel, cfg)
    part_shape = [jax.ShapeDtypeStruct((8, 128), F32)] if last else []
    return pl.pallas_call(
        kernel,
        out_shape=[pltpu.VMEM((rows, width), F32), pltpu.VMEM((rows, 128), F32)] + part_shape,
        out_specs=[VMEM_SPEC] * (2 + len(part_shape)),
        input_output_aliases={} if first else {len(ins) - 2: 0, len(ins) - 1: 1}, **common)(*ins)


PIECES = (256, 512, 512, 512, 256)


def after(value, *others):
    return lax.optimization_barrier((value,) + others)[0]


def solution(mesh):
    num_blocks = mesh.shape['row']
    cross_perm = [(src, src ^ 2) for src in range(num_blocks)]
    pair_perm = [(src, src ^ 1) for src in range(num_blocks)]
    diag_perm = [(src, src ^ 3) for src in range(num_blocks)]

    def per_device(positions, charges, counts):
        rows, _ = positions.shape
        chunks = rows // CHUNK
        head = positions[:PIECES[0]]
        arrived = [lax.ppermute(head, 'row', cross_perm)]
        positions = after(positions, head)
        x, rowf, info = prep(positions, charges, counts)
        info_cross = lax.ppermute(info, 'row', cross_perm)
        info_pair = lax.ppermute(info, 'row', pair_perm)
        off = PIECES[0]
        for size in PIECES[1:]:
            arrived.append(lax.ppermute(positions[off:off + size], 'row', cross_perm))
            off += size
        partner = lax.ppermute(positions, 'row', pair_perm)
        carry = step(x, rowf, info, None, None, 0, chunks, 4, None, False)
        partner, *carry = lax.optimization_barrier((partner, *carry))
        carry = step(x, rowf, info, info_pair, partner, 0, chunks, 4, carry, False)
        info_cross, *carry = lax.optimization_barrier((info_cross, *carry))
        info_diag = lax.ppermute(info_cross, 'row', pair_perm)
        off = 0
        for k, piece in enumerate(arrived):
            num = PIECES[k] // CHUNK
            piece, *carry = lax.optimization_barrier((piece, *carry))
            relay = lax.ppermute(piece, 'row', pair_perm)
            carry = step(x, rowf, info, info_cross, piece, off, num, min(4, num), carry, False)
            carry = step(x, rowf, info, info_diag, relay, off, num, min(4, num), carry, k == len(PIECES) - 1)
            off += num
        t_sum, s_sum, part = carry
        total = part
        for perm in (cross_perm, pair_perm, diag_perm):
            total = total + lax.ppermute(part, 'row', perm)
        forces = finish(x, t_sum, s_sum)
        return forces, (0.5 * jnp.sum(total)).reshape(1)

    row_spec = P(('sys', 'row'), None)
    vec_spec = P(('sys', 'row'))
    return jax.shard_map(per_device, mesh=mesh, in_specs=(row_spec, vec_spec, vec_spec), out_specs=(row_spec, P('sys')), check_vma=False)
```

time: 121 us -> 118 us (0.975)
  other arithmetic: 3.65 us -> 0.6 us
  starting transfers between devices: 7.57 us -> 9.46 us
  Pallas kernels: 66 us -> 64.2 us
    unnamed x6 -> x4, local copies, waits for them, and re-layouts: 0.6 us -> 2.58 us
    reduce_sum x1, other arithmetic: 2.57 us -> 0.6 us  [per_device(): return (forces, (0.5 * jnp.sum(total)).reshape(1))]
    ppermute x0 -> x3, starting transfers between devices: none -> 1.87 us  [per_device(): total = total + lax.ppermute(part, 'row', perm)]
    pallas_call x13 -> x14, Pallas kernels: 66 us -> 64.2 us  [the longest x12 57.9 us: step(): pl.pallas_call(kernel, out_shape=[pltpu.VMEM((rows, width), F32), pltpu.V...]
    slice x2, local copies, waits for them, and re-layouts: 1.78 us -> 0.18 us  [per_device(): arrived.append(lax.ppermute(positions[off:off + size], 'row', cross_perm))]
  transfers between devices with their start and end apart: 14 -> 17, of which waited for: 7 -> 7; matrix products, arithmetic and copies ran while one was open for 5% -> 0% of each run, Pallas kernels for 44% -> 51%
where the time goes in v2:
time: 118 us; the launch traced here: 117 us
  Pallas kernels  64.2 us (54%)
  waiting for transfers between devices  36 us (31%)
  starting transfers between devices  9.46 us (8%)
  local copies, waits for them, and re-layouts  3.78 us (3%)
  between operations  3.29 us (3%)
    pallas_call x12, Pallas kernels, step(): pl.pallas_call(kernel, out_shape=[pltpu.VMEM((rows, width), F32), pltpu.V...  57.9 us
    ppermute x4, waiting for transfers between devices, per_device(): arrived.append(lax.ppermute(positions[off:off + size], 'row', cross_perm))  29.8 us
    ppermute x5, waiting for transfers between devices, per_device(): relay = lax.ppermute(piece, 'row', pair_perm)  6.18 us
    ppermute x5, starting transfers between devices, per_device(): relay = lax.ppermute(piece, 'row', pair_perm)  4.07 us
    pallas_call x1, Pallas kernels, finish(): pl.pallas_call(functools.partial(finish_kernel, 1.0 / width), out_shape=j...  3.91 us
    unnamed x4, local copies, waits for them, and re-layouts  2.58 us
    pallas_call x1, Pallas kernels, prep(): pl.pallas_call(functools.partial(prep_kernel, LOG2E * 0.5 / width), out_s...  2.41 us
  transfers between devices with their start and end apart: 17, of which 7 were waited for; matrix products, arithmetic and copies ran while one was open for 0% of the time, Pallas kernels for 51%

profile of v2, /device:TPU:5, one launch (start us, length us, event | category | flops | bytes accessed | tf_op | source)
XLA Modules:
  0.0 117.3 jit_solution(14195947536945545494)
XLA Ops:
  0.6 1.0 slice.15
  1.7 0.7 collective-permute-start.2
  3.0 1.9 %copy-done = bf16[2048,768]{1,0:T(8,128)(2,1)S(1)} copy-done((bf16[2048,768]{1,0:T(8,128)(2,1)S(1)}, bf16[2048,768]{1,0:T(8,128)(2,1)}, u32[]{:S(2)}) %copy-start) | copy-done | bytes 3145752
  4.9 0.7 copy-done.1
  5.6 2.4 %prep.1 = (bf16[2048,768]{1,0:T(8,128)(2,1)S(1)}, f32[2,2048,128]{2,1,0:T(8,128)S(1)}, f32[40,128]{1,0:T(8,128)S(1)}) custom-call(bf16[2048,768]{1,0:T(8,128)(2,1)S(1)} %copy-done, f32[16,128]{1,0:T(8,128)S(1)} %bitcast.2, s32[1]{0:T(128)S(6)} %copy.49.count_ref), custom_call_target="tpu_custom_call" | custom-call | tf_op jit(solution)/shard_map/prep/pallas_call | solution.py:49
  8.0 0.0 collective-permute-start.1
  8.0 1.2 %collective-permute-start = (f32[40,128]{1,0:T(8,128)S(1)}, f32[40,128]{1,0:T(8,128)S(1)}, u32[]{:S(2)}, u32[]{:S(2)}) collective-permute-start(f32[40,128]{1,0:T(8,128)S(1)} %get-tuple-element.55.refs_2_), channel_id=1, source_target_pairs={{0,2},{1,3},{2,0},{3,1},{4,6},{5,7},{6,4},{7,5}} | collective-permute-start | bytes 61448 | tf_op jit(solution)/shard_map/ppermute | solution.py:210
  9.3 0.3 collective-permute-start.8
  9.5 0.2 fusion
  9.7 1.2 %collective-permute-start.7 = (bf16[512,768]{1,0:T(8,128)(2,1)S(1)}, bf16[512,768]{1,0:T(8,128)(2,1)S(1)}, u32[]{:S(2)}, u32[]{:S(2)}) collective-permute-start(bf16[512,768]{1,0:T(8,128)(2,1)S(1)} %get-tuple-element.102), channel_id=1, source_target_pairs={{0,2},{1,3},{2,0},{3,1},{4,6},{5,7},{6,4},{7,5}} | collective-permute-start | bytes 2359304 | tf_op jit(solution)/shard_map/ppermute | solution.py:214
  10.9 19.5 %step_0_16.2 = (f32[2048,768]{1,0:T(8,128)S(1)}, f32[2048,128]{1,0:T(8,128)S(1)}) custom-call(bf16[2048,768]{1,0:T(8,128)(2,1)S(1)} %get-tuple-element.53.refs_0_.xv, f32[2,2048,128]{2,1,0:T(8,128)S(1)} %get-tuple-element.54.refs_1_, f32[40,128]{1,0:T(8,128)S(1)} %get-tuple-element.55.refs_2_), custom_call_target="tpu_custom_call" | custom-call | flops 7730940928 | bytes 1572864 | tf_op jit(solution)/shard_map/step_0_16/pallas_call | solution.py:183
  30.4 0.0 collective-permute-done.1.refs_3_
  30.4 13.1 %step_0_16.3 = (f32[2048,768]{1,0:T(8,128)S(1)}, f32[2048,128]{1,0:T(8,128)S(1)}) custom-call(bf16[2048,768]{1,0:T(8,128)(2,1)S(1)} %get-tuple-element.53.refs_0_.xv, f32[2,2048,128]{2,1,0:T(8,128)S(1)} %get-tuple-element.54.refs_1_, f32[40,128]{1,0:T(8,128)S(1)} %get-tuple-element.55.refs_2_, ...), custom_call_target="tpu_custom_call", output_to_operand_aliasing={{0}: (5, {}), {1}: (6, {})} | custom-call | flops 7730940928 | bytes 1572864 | tf_op jit(solution)/shard_map/step_0_16/pallas_call | solution.py:183
  43.5 0.0 collective-permute-done.refs_3_
  43.6 0.0 collective-permute-done.8.refs_4_
  43.6 1.0 collective-permute-start.9
  44.5 0.0 collective-permute-start.3
  44.6 3.6 %step_0_2.2 = (f32[2048,768]{1,0:T(8,128)S(1)}, f32[2048,128]{1,0:T(8,128)S(1)}) custom-call(bf16[2048,768]{1,0:T(8,128)(2,1)S(1)} %get-tuple-element.53.refs_0_.xv, f32[2,2048,128]{2,1,0:T(8,128)S(1)} %get-tuple-element.54.refs_1_, f32[40,128]{1,0:T(8,128)S(1)} %get-tuple-element.55.refs_2_, ...), custom_call_target="tpu_custom_call", output_to_operand_aliasing={{0}: (5, {}), {1}: (6, {})} | custom-call | flops 966367616 | bytes 1572864 | tf_op jit(solution)/shard_map/step_0_2/pallas_call | solution.py:183
  48.2 3.6 %step_0_2.3 = (f32[2048,768]{1,0:T(8,128)S(1)}, f32[2048,128]{1,0:T(8,128)S(1)}) custom-call(bf16[2048,768]{1,0:T(8,128)(2,1)S(1)} %get-tuple-element.53.refs_0_.xv, f32[2,2048,128]{2,1,0:T(8,128)S(1)} %get-tuple-element.54.refs_1_, f32[40,128]{1,0:T(8,128)S(1)} %get-tuple-element.55.refs_2_, ...), custom_call_target="tpu_custom_call", output_to_operand_aliasing={{0}: (5, {}), {1}: (6, {})} | custom-call | flops 966367616 | bytes 1572864 | tf_op jit(solution)/shard_map/step_0_2/pallas_call | solution.py:183
  51.9 0.0 collective-permute-done.7.refs_4_
  51.9 0.5 collective-permute-start.10
  52.4 0.0 collective-permute-start.6
  52.4 0.2 step_2_4.2
  52.5 1.7 %collective-permute-done.10.refs_4_ = bf16[512,768]{1,0:T(8,128)(2,1)S(1)} collective-permute-done((bf16[512,768]{1,0:T(8,128)(2,1)S(1)}, bf16[512,768]{1,0:T(8,128)(2,1)S(1)}, u32[]{:S(2)}, u32[]{:S(2)}) %collective-permute-start.10) | collective-permute-done | bytes 786464 | tf_op jit(solution)/shard_map/ppermute | solution.py:226
  54.3 4.4 %step_2_4.3 = (f32[2048,768]{1,0:T(8,128)S(1)}, f32[2048,128]{1,0:T(8,128)S(1)}) custom-call(bf16[2048,768]{1,0:T(8,128)(2,1)S(1)} %get-tuple-element.53.refs_0_.xv, f32[2,2048,128]{2,1,0:T(8,128)S(1)} %get-tuple-element.54.refs_1_, f32[40,128]{1,0:T(8,128)S(1)} %get-tuple-element.55.refs_2_, ...), custom_call_target="tpu_custom_call", output_to_operand_aliasing={{0}: (5, {}), {1}: (6, {})} | custom-call | flops 1932735232 | bytes 1572864 | tf_op jit(solution)/shard_map/step_2_4/pallas_call | solution.py:183
  58.7 12.7 %collective-permute-done.6.refs_4_ = bf16[512,768]{1,0:T(8,128)(2,1)S(1)} collective-permute-done((bf16[512,768]{1,0:T(8,128)(2,1)S(1)}, bf16[512,768]{1,0:T(8,128)(2,1)S(1)}, u32[]{:S(2)}, u32[]{:S(2)}) %collective-permute-start.6) | collective-permute-done | bytes 786464 | tf_op jit(solution)/shard_map/ppermute | solution.py:214
  71.4 0.9 collective-permute-start.11
  72.3 0.3 step_6_4.2
  72.7 1.6 %collective-permute-done.11.refs_4_ = bf16[512,768]{1,0:T(8,128)(2,1)S(1)} collective-permute-done((bf16[512,768]{1,0:T(8,128)(2,1)S(1)}, bf16[512,768]{1,0:T(8,128)(2,1)S(1)}, u32[]{:S(2)}, u32[]{:S(2)}) %collective-permute-start.11) | collective-permute-done | bytes 786464 | tf_op jit(solution)/shard_map/ppermute | solution.py:226
  74.2 4.4 %step_6_4.3 = (f32[2048,768]{1,0:T(8,128)S(1)}, f32[2048,128]{1,0:T(8,128)S(1)}) custom-call(bf16[2048,768]{1,0:T(8,128)(2,1)S(1)} %get-tuple-element.53.refs_0_.xv, f32[2,2048,128]{2,1,0:T(8,128)S(1)} %get-tuple-element.54.refs_1_, f32[40,128]{1,0:T(8,128)S(1)} %get-tuple-element.55.refs_2_, ...), custom_call_target="tpu_custom_call", output_to_operand_aliasing={{0}: (5, {}), {1}: (6, {})} | custom-call | flops 1932735232 | bytes 1572864 | tf_op jit(solution)/shard_map/step_6_4/pallas_call | solution.py:183
  78.7 12.7 %collective-permute-done.5.refs_4_ = bf16[512,768]{1,0:T(8,128)(2,1)S(1)} collective-permute-done((bf16[512,768]{1,0:T(8,128)(2,1)S(1)}, bf16[512,768]{1,0:T(8,128)(2,1)S(1)}, u32[]{:S(2)}, u32[]{:S(2)}) %collective-permute-start.5) | collective-permute-done | bytes 786464 | tf_op jit(solution)/shard_map/ppermute | solution.py:214
  91.4 0.9 collective-permute-start.12
  92.3 0.0 collective-permute-start.4
  92.3 0.2 step_10_4.2
  92.5 1.7 %collective-permute-done.12.refs_4_ = bf16[512,768]{1,0:T(8,128)(2,1)S(1)} collective-permute-done((bf16[512,768]{1,0:T(8,128)(2,1)S(1)}, bf16[512,768]{1,0:T(8,128)(2,1)S(1)}, u32[]{:S(2)}, u32[]{:S(2)}) %collective-permute-start.12) | collective-permute-done | bytes 786464 | tf_op jit(solution)/shard_map/ppermute | solution.py:226
  94.2 4.4 %step_10_4.3 = (f32[2048,768]{1,0:T(8,128)S(1)}, f32[2048,128]{1,0:T(8,128)S(1)}) custom-call(bf16[2048,768]{1,0:T(8,128)(2,1)S(1)} %get-tuple-element.53.refs_0_.xv, f32[2,2048,128]{2,1,0:T(8,128)S(1)} %get-tuple-element.54.refs_1_, f32[40,128]{1,0:T(8,128)S(1)} %get-tuple-element.55.refs_2_, ...), custom_call_target="tpu_custom_call", output_to_operand_aliasing={{0}: (5, {}), {1}: (6, {})} | custom-call | flops 1932735232 | bytes 1572864 | tf_op jit(solution)/shard_map/step_10_4/pallas_call | solution.py:183
  98.6 4.4 %collective-permute-done.4.refs_4_ = bf16[256,768]{1,0:T(8,128)(2,1)S(1)} collective-permute-done((bf16[256,768]{1,0:T(8,128)(2,1)S(1)}, bf16[256,768]{1,0:T(8,128)(2,1)S(1)}, u32[]{:S(2)}, u32[]{:S(2)}) %collective-permute-start.4) | collective-permute-done | bytes 393248 | tf_op jit(solution)/shard_map/ppermute | solution.py:214
  103.0 0.9 collective-permute-start.13
  103.9 0.2 step_14_2.2
  104.0 1.2 %collective-permute-done.13.refs_4_ = bf16[256,768]{1,0:T(8,128)(2,1)S(1)} collective-permute-done((bf16[256,768]{1,0:T(8,128)(2,1)S(1)}, bf16[256,768]{1,0:T(8,128)(2,1)S(1)}, u32[]{:S(2)}, u32[]{:S(2)}) %collective-permute-start.13) | collective-permute-done | bytes 393248 | tf_op jit(solution)/shard_map/ppermute | solution.py:226
  105.2 3.9 %step_14_2.3 = (f32[2048,768]{1,0:T(8,128)S(1)}, f32[2048,128]{1,0:T(8,128)S(1)}, f32[8,128]{1,0:T(8,128)S(1)}) custom-call(bf16[2048,768]{1,0:T(8,128)(2,1)S(1)} %get-tuple-element.53.refs_0_.xv, f32[2,2048,128]{2,1,0:T(8,128)S(1)} %get-tuple-element.54.refs_1_, ...), custom_call_target="tpu_custom_call", output_to_operand_aliasing={{0}: (5, {}), {1}: (6, {})} | custom-call | flops 966367616 | bytes 1572864 | tf_op jit(solution)/shard_map/step_14_2/pallas_call | solution.py:183
  109.1 0.0 collective-permute-start.14
  109.2 0.6 collective-permute-start.15
  109.8 1.2 %collective-permute-start.16 = (f32[8,128]{1,0:T(8,128)S(1)}, f32[8,128]{1,0:T(8,128)S(1)}, u32[]{:S(2)}, u32[]{:S(2)}) collective-permute-start(f32[8,128]{1,0:T(8,128)S(1)} %get-tuple-element.101), channel_id=1, source_target_pairs={{0,3},{1,2},{2,1},{3,0},{4,7},{5,6},{6,5},{7,4}} | collective-permute-start | bytes 12296 | tf_op jit(solution)/shard_map/ppermute | solution.py:233
  111.0 3.9 %finish.1 = f32[2048,768]{1,0:T(8,128)} custom-call(bf16[2048,768]{1,0:T(8,128)(2,1)S(1)} %get-tuple-element.53.refs_0_.xv, f32[2048,768]{1,0:T(8,128)S(1)} %get-tuple-element.99.tv, f32[2048,128]{1,0:T(8,128)S(1)} %get-tuple-element.100.sv), custom_call_target="tpu_custom_call" | custom-call | flops 1572864000 | bytes 6291456 | tf_op jit(solution)/shard_map/finish/pallas_call | solution.py:156
  114.9 0.0 collective-permute-done.14
  115.0 0.0 collective-permute-done.16
  115.0 0.6 add_reduce_fusion
  (8 shorter events, 0.0 us)
Async XLA Ops:
  1.7 28.8 %collective-permute-start.2 = (bf16[2048,768]{1,0:T(8,128)(2,1)}, bf16[2048,768]{1,0:T(8,128)(2,1)S(1)}, u32[]{:S(2)}, u32[]{:S(2)}) collective-permute-start(bf16[2048,768]{1,0:T(8,128)(2,1)} %x_hbm), channel_id=1, source_target_pairs={{0,1},{1,0},{2,3},{3,2},{4,5},{5,4},{6,7},{7,6}} | collective-permute-start | bytes 9437192 | tf_op jit(solution)/shard_map/ppermute | solution.py:216
  3.0 1.9 %copy-start = (bf16[2048,768]{1,0:T(8,128)(2,1)S(1)}, bf16[2048,768]{1,0:T(8,128)(2,1)}, u32[]{:S(2)}) copy-start(bf16[2048,768]{1,0:T(8,128)(2,1)} %x_hbm) | copy-start | bytes 9437188
  4.9 0.7 copy-start.1
  8.0 22.4 %collective-permute-start.1 = (f32[40,128]{1,0:T(8,128)S(1)}, f32[40,128]{1,0:T(8,128)S(1)}, u32[]{:S(2)}, u32[]{:S(2)}) collective-permute-start(f32[40,128]{1,0:T(8,128)S(1)} %get-tuple-element.55.refs_2_), channel_id=1, source_target_pairs={{0,1},{1,0},{2,3},{3,2},{4,5},{5,4},{6,7},{7,6}} | collective-permute-start | bytes 61448 | tf_op jit(solution)/shard_map/ppermute | solution.py:211
  8.0 35.5 %collective-permute-start = (f32[40,128]{1,0:T(8,128)S(1)}, f32[40,128]{1,0:T(8,128)S(1)}, u32[]{:S(2)}, u32[]{:S(2)}) collective-permute-start(f32[40,128]{1,0:T(8,128)S(1)} %get-tuple-element.55.refs_2_), channel_id=1, source_target_pairs={{0,2},{1,3},{2,0},{3,1},{4,6},{5,7},{6,4},{7,5}} | collective-permute-start | bytes 61448 | tf_op jit(solution)/shard_map/ppermute | solution.py:210
  9.3 34.3 %collective-permute-start.8 = (bf16[256,768]{1,0:T(8,128)(2,1)S(1)}, bf16[256,768]{1,0:T(8,128)(2,1)S(1)}, u32[]{:S(2)}, u32[]{:S(2)}) collective-permute-start(bf16[256,768]{1,0:T(8,128)(2,1)S(1)} %slice.15), channel_id=1, source_target_pairs={{0,2},{1,3},{2,0},{3,1},{4,6},{5,7},{6,4},{7,5}} | collective-permute-start | bytes 1179656 | tf_op jit(solution)/shard_map/ppermute | solution.py:207
  9.7 42.2 %collective-permute-start.7 = (bf16[512,768]{1,0:T(8,128)(2,1)S(1)}, bf16[512,768]{1,0:T(8,128)(2,1)S(1)}, u32[]{:S(2)}, u32[]{:S(2)}) collective-permute-start(bf16[512,768]{1,0:T(8,128)(2,1)S(1)} %get-tuple-element.102), channel_id=1, source_target_pairs={{0,2},{1,3},{2,0},{3,1},{4,6},{5,7},{6,4},{7,5}} | collective-permute-start | bytes 2359304 | tf_op jit(solution)/shard_map/ppermute | solution.py:214
  43.6 4.6 %collective-permute-start.9 = (bf16[256,768]{1,0:T(8,128)(2,1)S(1)}, bf16[256,768]{1,0:T(8,128)(2,1)S(1)}, u32[]{:S(2)}, u32[]{:S(2)}) collective-permute-start(bf16[256,768]{1,0:T(8,128)(2,1)S(1)} %collective-permute-done.8.refs_4_), channel_id=1, source_target_pairs={{0,1},{1,0},{2,3},{3,2},{4,5},{5,4},{6,7},{7,6}} | collective-permute-start | bytes 1179656 | tf_op jit(solution)/shard_map/ppermute | solution.py:226
  44.5 3.7 %collective-permute-start.3 = (f32[40,128]{1,0:T(8,128)S(1)}, f32[40,128]{1,0:T(8,128)S(1)}, u32[]{:S(2)}, u32[]{:S(2)}) collective-permute-start(f32[40,128]{1,0:T(8,128)S(1)} %collective-permute-done.refs_3_), channel_id=1, source_target_pairs={{0,1},{1,0},{2,3},{3,2},{4,5},{5,4},{6,7},{7,6}} | collective-permute-start | bytes 61448 | tf_op jit(solution)/shard_map/ppermute | solution.py:221
  51.9 2.4 %collective-permute-start.10 = (bf16[512,768]{1,0:T(8,128)(2,1)S(1)}, bf16[512,768]{1,0:T(8,128)(2,1)S(1)}, u32[]{:S(2)}, u32[]{:S(2)}) collective-permute-start(bf16[512,768]{1,0:T(8,128)(2,1)S(1)} %collective-permute-done.7.refs_4_), channel_id=1, source_target_pairs={{0,1},{1,0},{2,3},{3,2},{4,5},{5,4},{6,7},{7,6}} | collective-permute-start | bytes 2359304 | tf_op jit(solution)/shard_map/ppermute | solution.py:226
  52.4 19.1 %collective-permute-start.6 = (bf16[512,768]{1,0:T(8,128)(2,1)S(1)}, bf16[512,768]{1,0:T(8,128)(2,1)S(1)}, u32[]{:S(2)}, u32[]{:S(2)}) collective-permute-start(bf16[512,768]{1,0:T(8,128)(2,1)S(1)} %get-tuple-element.103), channel_id=1, source_target_pairs={{0,2},{1,3},{2,0},{3,1},{4,6},{5,7},{6,4},{7,5}} | collective-permute-start | bytes 2359304 | tf_op jit(solution)/shard_map/ppermute | solution.py:214
  71.4 2.8 %collective-permute-start.11 = (bf16[512,768]{1,0:T(8,128)(2,1)S(1)}, bf16[512,768]{1,0:T(8,128)(2,1)S(1)}, u32[]{:S(2)}, u32[]{:S(2)}) collective-permute-start(bf16[512,768]{1,0:T(8,128)(2,1)S(1)} %collective-permute-done.6.refs_4_), channel_id=1, source_target_pairs={{0,1},{1,0},{2,3},{3,2},{4,5},{5,4},{6,7},{7,6}} | collective-permute-start | bytes 2359304 | tf_op jit(solution)/shard_map/ppermute | solution.py:226
  72.3 19.1 %collective-permute-start.5 = (bf16[512,768]{1,0:T(8,128)(2,1)S(1)}, bf16[512,768]{1,0:T(8,128)(2,1)S(1)}, u32[]{:S(2)}, u32[]{:S(2)}) collective-permute-start(bf16[512,768]{1,0:T(8,128)(2,1)S(1)} %get-tuple-element.104), channel_id=1, source_target_pairs={{0,2},{1,3},{2,0},{3,1},{4,6},{5,7},{6,4},{7,5}} | collective-permute-start | bytes 2359304 | tf_op jit(solution)/shard_map/ppermute | solution.py:214
  91.4 2.8 %collective-permute-start.12 = (bf16[512,768]{1,0:T(8,128)(2,1)S(1)}, bf16[512,768]{1,0:T(8,128)(2,1)S(1)}, u32[]{:S(2)}, u32[]{:S(2)}) collective-permute-start(bf16[512,768]{1,0:T(8,128)(2,1)S(1)} %collective-permute-done.5.refs_4_), channel_id=1, source_target_pairs={{0,1},{1,0},{2,3},{3,2},{4,5},{5,4},{6,7},{7,6}} | collective-permute-start | bytes 2359304 | tf_op jit(solution)/shard_map/ppermute | solution.py:226
  92.3 10.7 %collective-permute-start.4 = (bf16[256,768]{1,0:T(8,128)(2,1)S(1)}, bf16[256,768]{1,0:T(8,128)(2,1)S(1)}, u32[]{:S(2)}, u32[]{:S(2)}) collective-permute-start(bf16[256,768]{1,0:T(8,128)(2,1)S(1)} %slice.16), channel_id=1, source_target_pairs={{0,2},{1,3},{2,0},{3,1},{4,6},{5,7},{6,4},{7,5}} | collective-permute-start | bytes 1179656 | tf_op jit(solution)/shard_map/ppermute | solution.py:214
  103.0 2.2 %collective-permute-start.13 = (bf16[256,768]{1,0:T(8,128)(2,1)S(1)}, bf16[256,768]{1,0:T(8,128)(2,1)S(1)}, u32[]{:S(2)}, u32[]{:S(2)}) collective-permute-start(bf16[256,768]{1,0:T(8,128)(2,1)S(1)} %collective-permute-done.4.refs_4_), channel_id=1, source_target_pairs={{0,1},{1,0},{2,3},{3,2},{4,5},{5,4},{6,7},{7,6}} | collective-permute-start | bytes 1179656 | tf_op jit(solution)/shard_map/ppermute | solution.py:226
  109.1 5.8 %collective-permute-start.14 = (f32[8,128]{1,0:T(8,128)S(1)}, f32[8,128]{1,0:T(8,128)S(1)}, u32[]{:S(2)}, u32[]{:S(2)}) collective-permute-start(f32[8,128]{1,0:T(8,128)S(1)} %get-tuple-element.101), channel_id=1, source_target_pairs={{0,2},{1,3},{2,0},{3,1},{4,6},{5,7},{6,4},{7,5}} | collective-permute-start | bytes 12296 | tf_op jit(solution)/shard_map/ppermute | solution.py:233
  109.2 5.8 %collective-permute-start.15 = (f32[8,128]{1,0:T(8,128)S(1)}, f32[8,128]{1,0:T(8,128)S(1)}, u32[]{:S(2)}, u32[]{:S(2)}) collective-permute-start(f32[8,128]{1,0:T(8,128)S(1)} %get-tuple-element.101), channel_id=1, source_target_pairs={{0,1},{1,0},{2,3},{3,2},{4,5},{5,4},{6,7},{7,6}} | collective-permute-start | bytes 12296 | tf_op jit(solution)/shard_map/ppermute | solution.py:233
  109.8 5.1 %collective-permute-start.16 = (f32[8,128]{1,0:T(8,128)S(1)}, f32[8,128]{1,0:T(8,128)S(1)}, u32[]{:S(2)}, u32[]{:S(2)}) collective-permute-start(f32[8,128]{1,0:T(8,128)S(1)} %get-tuple-element.101), channel_id=1, source_target_pairs={{0,3},{1,2},{2,1},{3,0},{4,7},{5,6},{6,5},{7,4}} | collective-permute-start | bytes 12296 | tf_op jit(solution)/shard_map/ppermute | solution.py:233

commit v3 on v2

v3 whole, which is shorter than its diff:
```python
import functools

import jax
import jax.numpy as jnp
from jax import lax
from jax.experimental import pallas as pl
from jax.experimental.pallas import tpu as pltpu
from jax.sharding import PartitionSpec as P


CHUNK = 128
SUB_ROWS = 512
LOG2E = 1.4426950408889634
F32 = jnp.float32
VMEM_SPEC = pl.BlockSpec(memory_space=pltpu.VMEM)
HBM_SPEC = pl.BlockSpec(memory_space=pl.ANY)
FINISH_TILE = 256


def prep_kernel(kappa, xv, q_ref, count_ref, rowv, info):
    rows = xv.shape[0]
    chunks = rows // CHUNK
    eye = lax.broadcasted_iota(jnp.int32, (CHUNK, CHUNK), 0) == lax.broadcasted_iota(jnp.int32, (CHUNK, CHUNK), 1)
    lane = lax.broadcasted_iota(jnp.int32, (1, CHUNK), 1)
    count = count_ref[0]
    info[2 * chunks:, :] = jnp.full((8, CHUNK), count, jnp.int32).astype(F32)

    def one(c, _):
        sl = pl.ds(pl.multiple_of(c * CHUNK, CHUNK), CHUNK)
        block = xv[sl, :].astype(F32)
        col_s = -kappa * jnp.sum(block * block, axis=1, keepdims=True)
        rowv[0, sl, :] = jnp.broadcast_to(col_s, (CHUNK, CHUNK))
        info[pl.ds(c, 1), :] = jnp.sum(jnp.where(eye, col_s, 0.0), axis=0, keepdims=True)
        live = jnp.where(lane + c * CHUNK < count, q_ref[pl.ds(c, 1), :], 0.0)
        info[pl.ds(chunks + c, 1), :] = live
        rowv[1, sl, :] = jnp.broadcast_to(jnp.sum(jnp.where(eye, live, 0.0), axis=1, keepdims=True), (CHUNK, CHUNK))
        return 0

    lax.fori_loop(0, chunks, one, 0)


def prep(x, charges, counts):
    rows, width = x.shape
    chunks = rows // CHUNK
    return pl.pallas_call(
        functools.partial(prep_kernel, LOG2E * 0.5 / width),
        out_shape=[pltpu.VMEM((2, rows, CHUNK), F32),
                   jax.ShapeDtypeStruct((2 * chunks + 8, CHUNK), F32)],
        in_specs=[VMEM_SPEC, VMEM_SPEC, pl.BlockSpec(memory_space=pltpu.SMEM)], out_specs=[VMEM_SPEC] * 2,
        compiler_params=pltpu.CompilerParams(vmem_limit_bytes=VMEM_LIMIT),
        name='prep')(x, charges.reshape(chunks, CHUNK), counts)


def count_of(info_ref):
    return jnp.max(info_ref[info_ref.shape[0] - 8:, :]).astype(jnp.int32)


def weights(kappa, gram, row_a, row_c, col_a, col_c):
    expo = jnp.minimum(gram * (2.0 * kappa) + row_a + col_a, 0.0)
    return jnp.exp2(expo) * (row_c * col_c)


def step_kernel(cfg, *refs):
    start, num, tile_chunks, first, diag, kappa = cfg
    refs = list(refs)
    xv, rowv, my_info = refs[:3]
    refs = refs[3:]
    cols, src_info = xv, my_info
    if not diag:
        src_info, cols = refs[:2]
        refs = refs[2:]
    if not first:
        refs = refs[2:]
    tv, sv = refs[:2]
    rows, width = xv.shape
    block_chunks = rows // CHUNK
    col_tile = tile_chunks * CHUNK
    live = jnp.clip((count_of(src_info) + CHUNK - 1) // CHUNK - start, 0, num)
    tiles = (live + tile_chunks - 1) // tile_chunks

    def weigh(ct, c0, r0):
        rsl = pl.ds(r0, SUB_ROWS)
        s_sum = sv[rsl, :]
        row_a = rowv[0, rsl, :]
        row_c = rowv[1, rsl, :]
        parts = []
        for q in range(tile_chunks // 2):
            gram = lax.dot_general(xv[rsl, :], cols[pl.ds(c0 + q * 256, 256), :], (((1,), (1,)), ((), ())),
                                   preferred_element_type=F32)
            for h in range(2):
                k = 2 * q + h
                cid = start + ct * tile_chunks + k
                col_a = src_info[pl.ds(cid, 1), :]
                col_c = src_info[pl.ds(block_chunks + cid, 1), :]
                w = weights(kappa, gram[:, h * 128:(h + 1) * 128], row_a, row_c, col_a, col_c)
                if diag:
                    delta = lax.broadcasted_iota(jnp.int32, w.shape, 0) - lax.broadcasted_iota(jnp.int32, w.shape, 1)
                    w = jnp.where(delta == c0 + k * CHUNK - r0, 0.0, w)
                s_sum = s_sum + w
                parts.append(w.astype(jnp.bfloat16))
        sv[rsl, :] = s_sum
        return jnp.concatenate(parts, axis=1)

    def pull(w, c0, r0):
        tv[pl.ds(r0, SUB_ROWS), :] += jnp.dot(w, cols[pl.ds(c0, col_tile), :], preferred_element_type=F32)

    def tile(ct, _):
        c0 = pl.multiple_of(ct * col_tile, col_tile)
        w = None
        for r0 in range(0, rows, SUB_ROWS):
            w_next = weigh(ct, c0, r0)
            if w is not None:
                pull(w, c0, r0 - SUB_ROWS)
            w = w_next
        pull(w, c0, rows - SUB_ROWS)
        return 0

    if first:
        def clear(i, _):
            sl = pl.ds(pl.multiple_of(i * 64, 64), 64)
            tv[sl, :] = jnp.zeros((64, width), F32)
            sv[sl, :] = jnp.zeros((64, 128), F32)
            return 0

        lax.fori_loop(0, rows // 64, clear, 0)
    lax.fori_loop(0, tiles, tile, 0)


def last_kernel(cfg, *refs):
    start, num, total, kappa = cfg
    xv, rowv, src_info, cols, _, sv, wv = refs[:7]
    block_chunks = xv.shape[0] // CHUNK

    def row_tile(rt, acc):
        rsl = pl.ds(pl.multiple_of(rt * SUB_ROWS, SUB_ROWS), SUB_ROWS)
        sums = sv[rsl, :]
        gram = lax.dot_general(xv[rsl, :], cols[...], (((1,), (1,)), ((), ())), preferred_element_type=F32)
        for k in range(num):
            w = weights(kappa, gram[:, k * CHUNK:(k + 1) * CHUNK], rowv[0, rsl, :], rowv[1, rsl, :],
                        src_info[start + k:start + k + 1, :], src_info[block_chunks + start + k:block_chunks + start + k + 1, :])
            sums = sums + w
            wv[rsl, k * CHUNK:(k + 1) * CHUNK] = w.astype(jnp.bfloat16)
        sv[rsl, :] = sums
        if total:
            for g in range(SUB_ROWS // 8):
                acc = acc + sums[g * 8:(g + 1) * 8]
        return acc

    part = lax.fori_loop(0, xv.shape[0] // SUB_ROWS, row_tile, jnp.zeros((8, 128), F32))
    if total:
        refs[7][...] = part


def last_step(x, rowf, src_info, cols, start, s_sum, total):
    rows, width = x.shape
    num = cols.shape[0] // CHUNK
    ins = [x, rowf, src_info, cols, s_sum]
    part_shape = [jax.ShapeDtypeStruct((8, 128), F32)] if total else []
    return pl.pallas_call(
        functools.partial(last_kernel, (start, num, total, LOG2E * 0.5 / width)),
        out_shape=[pltpu.VMEM((rows, 128), F32), pltpu.VMEM((rows, num * CHUNK), jnp.bfloat16)] + part_shape,
        in_specs=[VMEM_SPEC] * len(ins), out_specs=[VMEM_SPEC] * (2 + len(part_shape)),
        input_output_aliases={len(ins) - 1: 0},
        compiler_params=pltpu.CompilerParams(vmem_limit_bytes=VMEM_LIMIT),
        cost_estimate=pl.CostEstimate(flops=2 * rows * num * CHUNK * width, bytes_accessed=rows * width, transcendentals=0))(*ins)


def finish_kernel(inv_len2, xv, tv, sv, wa, wb, cols_a, cols_b, forces, buf, out_sems):
    num = xv.shape[0] // FINISH_TILE

    def out(i):
        return pltpu.make_async_copy(
            buf.at[lax.rem(i, 4)], forces.at[pl.ds(pl.multiple_of(i * FINISH_TILE, FINISH_TILE), FINISH_TILE)], out_sems.at[lax.rem(i, 4)])

    def one(i, _):
        @pl.when(i >= 4)
        def _():
            out(i - 4).wait()

        sl = pl.ds(pl.multiple_of(i * FINISH_TILE, FINISH_TILE), FINISH_TILE)
        total = jnp.sum(sv[sl, :], axis=1, keepdims=True)
        pulled = (tv[sl, :] + jnp.dot(wa[sl, :], cols_a[...], preferred_element_type=F32)
                  + jnp.dot(wb[sl, :], cols_b[...], preferred_element_type=F32))
        buf[lax.rem(i, 4)] = (total * xv[sl, :].astype(F32) - pulled) * inv_len2
        out(i).start()
        return 0

    lax.fori_loop(0, num, one, 0)
    for i in range(num - 4, num):
        out(i).wait()


def finish(*ins):
    x = ins[0]
    rows, width = x.shape
    return pl.pallas_call(
        functools.partial(finish_kernel, 1.0 / width),
        out_shape=jax.ShapeDtypeStruct((rows, width), F32),
        in_specs=[VMEM_SPEC] * len(ins), out_specs=HBM_SPEC,
        scratch_shapes=[pltpu.VMEM((4, FINISH_TILE, width), F32), pltpu.SemaphoreType.DMA((4,))],
        compiler_params=pltpu.CompilerParams(vmem_limit_bytes=VMEM_LIMIT),
        cost_estimate=pl.CostEstimate(flops=rows * width * 1000, bytes_accessed=rows * width * 4, transcendentals=0),
        name='finish')(*ins)


VMEM_LIMIT = 24 * 1024 * 1024


def step(x, rowf, my_info, src_info, cols, start, num, tile_chunks, carry):
    rows, width = x.shape
    first, diag = carry is None, cols is None
    cfg = (start, num, tile_chunks, first, diag, LOG2E * 0.5 / width)
    ins = [x, rowf, my_info] + ([] if diag else [src_info, cols]) + ([] if first else list(carry))
    in_specs = [VMEM_SPEC] * len(ins)
    flops = int(4 * rows * num * CHUNK * width * 0.6)
    common = dict(
        in_specs=in_specs,
        compiler_params=pltpu.CompilerParams(vmem_limit_bytes=VMEM_LIMIT),
        cost_estimate=pl.CostEstimate(flops=flops, bytes_accessed=rows * width, transcendentals=0),
        name='step_%d_%d' % (start, num))
    kernel = functools.partial(step_kernel, cfg)
    return pl.pallas_call(
        kernel,
        out_shape=[pltpu.VMEM((rows, width), F32), pltpu.VMEM((rows, 128), F32)],
        out_specs=[VMEM_SPEC] * 2,
        input_output_aliases={} if first else {len(ins) - 2: 0, len(ins) - 1: 1}, **common)(*ins)


PIECES = (256, 512, 512, 512, 256)


def after(value, *others):
    return lax.optimization_barrier((value,) + others)[0]


def solution(mesh):
    num_blocks = mesh.shape['row']
    cross_perm = [(src, src ^ 2) for src in range(num_blocks)]
    pair_perm = [(src, src ^ 1) for src in range(num_blocks)]
    diag_perm = [(src, src ^ 3) for src in range(num_blocks)]

    def per_device(positions, charges, counts):
        rows, _ = positions.shape
        chunks = rows // CHUNK
        x = pltpu.with_memory_space_constraint(positions, pltpu.VMEM)
        head = positions[:PIECES[0]]
        arrived = [lax.ppermute(head, 'row', cross_perm)]
        positions = after(positions, head)
        rowf, info = prep(x, charges, counts)
        info_cross = lax.ppermute(info, 'row', cross_perm)
        info_pair = lax.ppermute(info, 'row', pair_perm)
        off = PIECES[0]
        for size in PIECES[1:]:
            arrived.append(lax.ppermute(positions[off:off + size], 'row', cross_perm))
            off += size
        partner = lax.ppermute(positions, 'row', pair_perm)
        carry = step(x, rowf, info, None, None, 0, chunks, 4, None)
        partner, *carry = lax.optimization_barrier((partner, *carry))
        carry = step(x, rowf, info, info_pair, partner, 0, chunks, 4, carry)
        info_cross, *carry = lax.optimization_barrier((info_cross, *carry))
        info_diag = lax.ppermute(info_cross, 'row', pair_perm)
        off = 0
        for k, piece in enumerate(arrived):
            num = PIECES[k] // CHUNK
            piece, *carry = lax.optimization_barrier((piece, *carry))
            relay = lax.ppermute(piece, 'row', pair_perm)
            if k < len(PIECES) - 1:
                carry = step(x, rowf, info, info_cross, piece, off, num, min(4, num), carry)
                carry = step(x, rowf, info, info_diag, relay, off, num, min(4, num), carry)
            else:
                t_sum, s_sum = carry
                s_sum, w_piece = last_step(x, rowf, info_cross, piece, off, s_sum, False)
                s_sum, w_relay, part = last_step(x, rowf, info_diag, relay, off, s_sum, True)
            off += num
        total = part
        for perm in (cross_perm, pair_perm, diag_perm):
            total = total + lax.ppermute(part, 'row', perm)
        forces = finish(x, t_sum, s_sum, w_piece, w_relay, piece, relay)
        return forces, (0.5 * jnp.sum(total)).reshape(1)

    row_spec = P(('sys', 'row'), None)
    vec_spec = P(('sys', 'row'))
    return jax.shard_map(per_device, mesh=mesh, in_specs=(row_spec, vec_spec, vec_spec), out_specs=(row_spec, P('sys')), check_vma=False)
```

time: 118 us -> 109 us (0.924)
  Pallas kernels: 64.2 us -> 55.7 us
    pallas_call x12 -> x10, Pallas kernels: 57.9 us -> 45.7 us  [step(): pl.pallas_call(kernel, out_shape=[pltpu.VMEM((rows, width), F32), pltpu.V...]
    pallas_call x0 -> x2, Pallas kernels: none -> 3.66 us  [last_step(): pl.pallas_call(functools.partial(last_kernel, (start, num, total, LOG2E *...]
    ppermute x4, waiting for transfers between devices: 29.8 us -> 31.2 us  [per_device(): arrived.append(lax.ppermute(positions[off:off + size], 'row', cross_perm))]
  transfers between devices with their start and end apart: 17 -> 17, of which waited for: 7 -> 6; matrix products, arithmetic and copies ran while one was open for 0% -> 0% of each run, Pallas kernels for 51% -> 49%
where the time goes in v3:
time: 109 us
  Pallas kernels  55.7 us (51%)
  waiting for transfers between devices  36.3 us (33%)
  starting transfers between devices  9.5 us (9%)
  local copies, waits for them, and re-layouts  3.78 us (3%)
  between operations  3.3 us (3%)
    pallas_call x10, Pallas kernels, step(): pl.pallas_call(kernel, out_shape=[pltpu.VMEM((rows, width), F32), pltpu.V...  45.7 us
    ppermute x4, waiting for transfers between devices, per_device(): arrived.append(lax.ppermute(positions[off:off + size], 'row', cross_perm))  31.2 us
    ppermute x5, waiting for transfers between devices, per_device(): relay = lax.ppermute(piece, 'row', pair_perm)  5.06 us
    pallas_call x1, Pallas kernels, finish(): pl.pallas_call(functools.partial(finish_kernel, 1.0 / width), out_shape=j...  4.13 us
    ppermute x5, starting transfers between devices, per_device(): relay = lax.ppermute(piece, 'row', pair_perm)  4.11 us
    pallas_call x2, Pallas kernels, last_step(): pl.pallas_call(functools.partial(last_kernel, (start, num, total, LOG2E *...  3.66 us
    unnamed x4, local copies, waits for them, and re-layouts  2.58 us
  transfers between devices with their start and end apart: 17, of which 6 were waited for; matrix products, arithmetic and copies ran while one was open for 0% of the time, Pallas kernels for 49%

profile of v3, /device:TPU:5, one launch (start us, length us, event | category | flops | bytes accessed | tf_op | source)
XLA Modules:
  0.0 109.1 jit_solution(13044924794385165935)
XLA Ops:
  0.6 1.0 slice.15
  1.7 0.7 collective-permute-start.3
  3.0 1.9 %copy-done = bf16[2048,768]{1,0:T(8,128)(2,1)S(1)} copy-done((bf16[2048,768]{1,0:T(8,128)(2,1)S(1)}, bf16[2048,768]{1,0:T(8,128)(2,1)}, u32[]{:S(2)}) %copy-start) | copy-done | bytes 3145752
  4.9 0.7 copy-done.1
  5.6 2.1 %prep.1 = (f32[2,2048,128]{2,1,0:T(8,128)S(1)}, f32[40,128]{1,0:T(8,128)S(1)}) custom-call(bf16[2048,768]{1,0:T(8,128)(2,1)S(1)} %copy-done, f32[16,128]{1,0:T(8,128)S(1)} %bitcast.2, s32[1]{0:T(128)S(6)} %copy.45.count_ref), custom_call_target="tpu_custom_call" | custom-call | tf_op jit(solution)/shard_map/prep/pallas_call | solution.py:45
  7.7 0.0 collective-permute-start.2
  7.8 1.2 %collective-permute-start.1 = (f32[40,128]{1,0:T(8,128)S(1)}, f32[40,128]{1,0:T(8,128)S(1)}, u32[]{:S(2)}, u32[]{:S(2)}) collective-permute-start(f32[40,128]{1,0:T(8,128)S(1)} %get-tuple-element.53.refs_2_), channel_id=1, source_target_pairs={{0,2},{1,3},{2,0},{3,1},{4,6},{5,7},{6,4},{7,5}} | collective-permute-start | bytes 61448 | tf_op jit(solution)/shard_map/ppermute | solution.py:250
  9.0 0.3 collective-permute-start.8
  9.3 0.2 fusion
  9.4 1.2 %collective-permute-start.7 = (bf16[512,768]{1,0:T(8,128)(2,1)S(1)}, bf16[512,768]{1,0:T(8,128)(2,1)S(1)}, u32[]{:S(2)}, u32[]{:S(2)}) collective-permute-start(bf16[512,768]{1,0:T(8,128)(2,1)S(1)} %get-tuple-element.100), channel_id=1, source_target_pairs={{0,2},{1,3},{2,0},{3,1},{4,6},{5,7},{6,4},{7,5}} | collective-permute-start | bytes 2359304 | tf_op jit(solution)/shard_map/ppermute | solution.py:254
  10.7 17.2 %step_0_16.2 = (f32[2048,768]{1,0:T(8,128)S(1)}, f32[2048,128]{1,0:T(8,128)S(1)}) custom-call(bf16[2048,768]{1,0:T(8,128)(2,1)S(1)} %copy-done, f32[2,2048,128]{2,1,0:T(8,128)S(1)} %get-tuple-element.52.refs_1_, f32[40,128]{1,0:T(8,128)S(1)} %get-tuple-element.53.refs_2_), custom_call_target="tpu_custom_call" | custom-call | flops 7730940928 | bytes 1572864 | tf_op jit(solution)/shard_map/step_0_16/pallas_call | solution.py:222
  27.8 0.0 collective-permute-done.2.refs_3_
  27.9 11.5 %step_0_16.3 = (f32[2048,768]{1,0:T(8,128)S(1)}, f32[2048,128]{1,0:T(8,128)S(1)}) custom-call(bf16[2048,768]{1,0:T(8,128)(2,1)S(1)} %copy-done, f32[2,2048,128]{2,1,0:T(8,128)S(1)} %get-tuple-element.52.refs_1_, f32[40,128]{1,0:T(8,128)S(1)} %get-tuple-element.53.refs_2_, ...), custom_call_target="tpu_custom_call", output_to_operand_aliasing={{0}: (5, {}), {1}: (6, {})} | custom-call | flops 7730940928 | bytes 1572864 | tf_op jit(solution)/shard_map/step_0_16/pallas_call | solution.py:222
  39.3 0.0 collective-permute-done.1.refs_3_.refs_2_
  39.3 1.0 collective-permute-start.9
  40.3 0.0 collective-permute-start.4
  40.4 2.3 %step_0_2.2 = (f32[2048,768]{1,0:T(8,128)S(1)}, f32[2048,128]{1,0:T(8,128)S(1)}) custom-call(bf16[2048,768]{1,0:T(8,128)(2,1)S(1)} %copy-done, f32[2,2048,128]{2,1,0:T(8,128)S(1)} %get-tuple-element.52.refs_1_, f32[40,128]{1,0:T(8,128)S(1)} %get-tuple-element.53.refs_2_, ...), custom_call_target="tpu_custom_call", output_to_operand_aliasing={{0}: (5, {}), {1}: (6, {})} | custom-call | flops 966367616 | bytes 1572864 | tf_op jit(solution)/shard_map/step_0_2/pallas_call | solution.py:222
  42.7 0.0 collective-permute-done.4.refs_3_.refs_2_
  42.7 0.0 collective-permute-done.9.refs_4_
  42.7 2.3 %step_0_2.3 = (f32[2048,768]{1,0:T(8,128)S(1)}, f32[2048,128]{1,0:T(8,128)S(1)}) custom-call(bf16[2048,768]{1,0:T(8,128)(2,1)S(1)} %copy-done, f32[2,2048,128]{2,1,0:T(8,128)S(1)} %get-tuple-element.52.refs_1_, f32[40,128]{1,0:T(8,128)S(1)} %get-tuple-element.53.refs_2_, ...), custom_call_target="tpu_custom_call", output_to_operand_aliasing={{0}: (5, {}), {1}: (6, {})} | custom-call | flops 966367616 | bytes 1572864 | tf_op jit(solution)/shard_map/step_0_2/pallas_call | solution.py:222
  45.0 0.0 collective-permute-done.7.refs_4_
  45.0 0.5 collective-permute-start.10
  45.5 0.0 collective-permute-start.6
  45.5 0.3 step_2_4.2
  45.9 1.6 %collective-permute-done.10.refs_4_ = bf16[512,768]{1,0:T(8,128)(2,1)S(1)} collective-permute-done((bf16[512,768]{1,0:T(8,128)(2,1)S(1)}, bf16[512,768]{1,0:T(8,128)(2,1)S(1)}, u32[]{:S(2)}, u32[]{:S(2)}) %collective-permute-start.10) | collective-permute-done | bytes 786464 | tf_op jit(solution)/shard_map/ppermute | solution.py:266
  47.4 3.9 %step_2_4.3 = (f32[2048,768]{1,0:T(8,128)S(1)}, f32[2048,128]{1,0:T(8,128)S(1)}) custom-call(bf16[2048,768]{1,0:T(8,128)(2,1)S(1)} %copy-done, f32[2,2048,128]{2,1,0:T(8,128)S(1)} %get-tuple-element.52.refs_1_, f32[40,128]{1,0:T(8,128)S(1)} %get-tuple-element.53.refs_2_, ...), custom_call_target="tpu_custom_call", output_to_operand_aliasing={{0}: (5, {}), {1}: (6, {})} | custom-call | flops 1932735232 | bytes 1572864 | tf_op jit(solution)/shard_map/step_2_4/pallas_call | solution.py:222
  51.3 13.3 %collective-permute-done.6.refs_4_ = bf16[512,768]{1,0:T(8,128)(2,1)S(1)} collective-permute-done((bf16[512,768]{1,0:T(8,128)(2,1)S(1)}, bf16[512,768]{1,0:T(8,128)(2,1)S(1)}, u32[]{:S(2)}, u32[]{:S(2)}) %collective-permute-start.6) | collective-permute-done | bytes 786464 | tf_op jit(solution)/shard_map/ppermute | solution.py:254
  64.6 0.9 collective-permute-start.11
  65.5 0.1 step_6_4.2
  65.6 1.8 %collective-permute-done.11.refs_4_ = bf16[512,768]{1,0:T(8,128)(2,1)S(1)} collective-permute-done((bf16[512,768]{1,0:T(8,128)(2,1)S(1)}, bf16[512,768]{1,0:T(8,128)(2,1)S(1)}, u32[]{:S(2)}, u32[]{:S(2)}) %collective-permute-start.11) | collective-permute-done | bytes 786464 | tf_op jit(solution)/shard_map/ppermute | solution.py:266
  67.4 4.1 %step_6_4.3 = (f32[2048,768]{1,0:T(8,128)S(1)}, f32[2048,128]{1,0:T(8,128)S(1)}) custom-call(bf16[2048,768]{1,0:T(8,128)(2,1)S(1)} %copy-done, f32[2,2048,128]{2,1,0:T(8,128)S(1)} %get-tuple-element.52.refs_1_, f32[40,128]{1,0:T(8,128)S(1)} %get-tuple-element.53.refs_2_, ...), custom_call_target="tpu_custom_call", output_to_operand_aliasing={{0}: (5, {}), {1}: (6, {})} | custom-call | flops 1932735232 | bytes 1572864 | tf_op jit(solution)/shard_map/step_6_4/pallas_call | solution.py:222
  71.5 13.1 %collective-permute-done.5.refs_4_ = bf16[512,768]{1,0:T(8,128)(2,1)S(1)} collective-permute-done((bf16[512,768]{1,0:T(8,128)(2,1)S(1)}, bf16[512,768]{1,0:T(8,128)(2,1)S(1)}, u32[]{:S(2)}, u32[]{:S(2)}) %collective-permute-start.5) | collective-permute-done | bytes 786464 | tf_op jit(solution)/shard_map/ppermute | solution.py:254
  84.6 0.9 collective-permute-start.12
  85.5 0.0 collective-permute-start
  85.5 0.1 step_10_4.2
  85.7 1.7 %collective-permute-done.12.refs_4_ = bf16[512,768]{1,0:T(8,128)(2,1)S(1)} collective-permute-done((bf16[512,768]{1,0:T(8,128)(2,1)S(1)}, bf16[512,768]{1,0:T(8,128)(2,1)S(1)}, u32[]{:S(2)}, u32[]{:S(2)}) %collective-permute-start.12) | collective-permute-done | bytes 786464 | tf_op jit(solution)/shard_map/ppermute | solution.py:266
  87.4 3.9 %step_10_4.3 = (f32[2048,768]{1,0:T(8,128)S(1)}, f32[2048,128]{1,0:T(8,128)S(1)}) custom-call(bf16[2048,768]{1,0:T(8,128)(2,1)S(1)} %copy-done, f32[2,2048,128]{2,1,0:T(8,128)S(1)} %get-tuple-element.52.refs_1_, f32[40,128]{1,0:T(8,128)S(1)} %get-tuple-element.53.refs_2_, ...), custom_call_target="tpu_custom_call", output_to_operand_aliasing={{0}: (5, {}), {1}: (6, {})} | custom-call | flops 1932735232 | bytes 1572864 | tf_op jit(solution)/shard_map/step_10_4/pallas_call | solution.py:222
  91.3 4.9 %collective-permute-done.refs_3_.cols_a = bf16[256,768]{1,0:T(8,128)(2,1)S(1)} collective-permute-done((bf16[256,768]{1,0:T(8,128)(2,1)S(1)}, bf16[256,768]{1,0:T(8,128)(2,1)S(1)}, u32[]{:S(2)}, u32[]{:S(2)}) %collective-permute-start) | collective-permute-done | bytes 393248 | tf_op jit(solution)/shard_map/ppermute | solution.py:254
  96.2 0.9 collective-permute-start.13
  97.0 1.8 %shard_map.50 = (f32[2048,128]{1,0:T(8,128)S(1)}, bf16[2048,256]{1,0:T(8,128)(2,1)S(1)}) custom-call(bf16[2048,768]{1,0:T(8,128)(2,1)S(1)} %copy-done, f32[2,2048,128]{2,1,0:T(8,128)S(1)} %get-tuple-element.52.refs_1_, f32[40,128]{1,0:T(8,128)S(1)} %collective-permute-done.1.refs_3_.refs_2_, ...), custom_call_target="tpu_custom_call", output_to_operand_aliasing={{0}: (4, {})} | custom-call | flops 805306368 | bytes 1572864 | tf_op jit(solution)/shard_map/pallas_call | solution.py:159
  98.8 1.9 %shard_map.51 = (f32[2048,128]{1,0:T(8,128)S(1)}, bf16[2048,256]{1,0:T(8,128)(2,1)S(1)}, f32[8,128]{1,0:T(8,128)S(1)}) custom-call(bf16[2048,768]{1,0:T(8,128)(2,1)S(1)} %copy-done, f32[2,2048,128]{2,1,0:T(8,128)S(1)} %get-tuple-element.52.refs_1_, f32[40,128]{1,0:T(8,128)S(1)} %collective-permute-done.4.refs_3_.refs_2_, ...), custom_call_target="tpu_custom_call", output_to_operand_aliasing={{0}: (4, {})} | custom-call | flops 805306368 | bytes 1572864 | tf_op jit(solution)/shard_map/pallas_call | solution.py:159
  100.7 0.0 collective-permute-start.14
  100.7 0.3 collective-permute-start.15
  101.0 1.6 %collective-permute-start.16 = (f32[8,128]{1,0:T(8,128)S(1)}, f32[8,128]{1,0:T(8,128)S(1)}, u32[]{:S(2)}, u32[]{:S(2)}) collective-permute-start(f32[8,128]{1,0:T(8,128)S(1)} %get-tuple-element.99), channel_id=1, source_target_pairs={{0,3},{1,2},{2,1},{3,0},{4,7},{5,6},{6,5},{7,4}} | collective-permute-start | bytes 12296 | tf_op jit(solution)/shard_map/ppermute | solution.py:277
  102.6 4.1 %finish.1 = f32[2048,768]{1,0:T(8,128)} custom-call(bf16[2048,768]{1,0:T(8,128)(2,1)S(1)} %copy-done, f32[2048,768]{1,0:T(8,128)S(1)} %get-tuple-element.92.tv, f32[2048,128]{1,0:T(8,128)S(1)} %get-tuple-element.96.sv, bf16[2048,256]{1,0:T(8,128)(2,1)S(1)} %get-tuple-element.97.wa, bf16[2048,256]{1,0:T(8,128)(2,1)S(1)} %get-tuple-element.98.wb, ...), custom_call_target="tpu_custom_call" | custom-call | flops 1572864000 | bytes 6291456 | tf_op jit(solution)/shard_map/finish/pallas_call | solution.py:196
  106.7 0.0 collective-permute-done.14
  106.8 0.0 collective-permute-done.16
  106.8 0.6 add_reduce_fusion
  (8 shorter events, 0.0 us)
Async XLA Ops:
  1.7 26.2 %collective-permute-start.3 = (bf16[2048,768]{1,0:T(8,128)(2,1)}, bf16[2048,768]{1,0:T(8,128)(2,1)S(1)}, u32[]{:S(2)}, u32[]{:S(2)}) collective-permute-start(bf16[2048,768]{1,0:T(8,128)(2,1)} %xv.3), channel_id=1, source_target_pairs={{0,1},{1,0},{2,3},{3,2},{4,5},{5,4},{6,7},{7,6}} | collective-permute-start | bytes 9437192 | tf_op jit(solution)/shard_map/ppermute | solution.py:256
  3.0 1.9 %copy-start = (bf16[2048,768]{1,0:T(8,128)(2,1)S(1)}, bf16[2048,768]{1,0:T(8,128)(2,1)}, u32[]{:S(2)}) copy-start(bf16[2048,768]{1,0:T(8,128)(2,1)} %xv.3) | copy-start | bytes 9437188
  4.9 0.7 copy-start.1
  7.7 20.1 %collective-permute-start.2 = (f32[40,128]{1,0:T(8,128)S(1)}, f32[40,128]{1,0:T(8,128)S(1)}, u32[]{:S(2)}, u32[]{:S(2)}) collective-permute-start(f32[40,128]{1,0:T(8,128)S(1)} %get-tuple-element.53.refs_2_), channel_id=1, source_target_pairs={{0,1},{1,0},{2,3},{3,2},{4,5},{5,4},{6,7},{7,6}} | collective-permute-start | bytes 61448 | tf_op jit(solution)/shard_map/ppermute | solution.py:251
  7.8 31.5 %collective-permute-start.1 = (f32[40,128]{1,0:T(8,128)S(1)}, f32[40,128]{1,0:T(8,128)S(1)}, u32[]{:S(2)}, u32[]{:S(2)}) collective-permute-start(f32[40,128]{1,0:T(8,128)S(1)} %get-tuple-element.53.refs_2_), channel_id=1, source_target_pairs={{0,2},{1,3},{2,0},{3,1},{4,6},{5,7},{6,4},{7,5}} | collective-permute-start | bytes 61448 | tf_op jit(solution)/shard_map/ppermute | solution.py:250
  9.0 30.3 %collective-permute-start.8 = (bf16[256,768]{1,0:T(8,128)(2,1)S(1)}, bf16[256,768]{1,0:T(8,128)(2,1)S(1)}, u32[]{:S(2)}, u32[]{:S(2)}) collective-permute-start(bf16[256,768]{1,0:T(8,128)(2,1)S(1)} %slice.15), channel_id=1, source_target_pairs={{0,2},{1,3},{2,0},{3,1},{4,6},{5,7},{6,4},{7,5}} | collective-permute-start | bytes 1179656 | tf_op jit(solution)/shard_map/ppermute | solution.py:247
  9.4 35.6 %collective-permute-start.7 = (bf16[512,768]{1,0:T(8,128)(2,1)S(1)}, bf16[512,768]{1,0:T(8,128)(2,1)S(1)}, u32[]{:S(2)}, u32[]{:S(2)}) collective-permute-start(bf16[512,768]{1,0:T(8,128)(2,1)S(1)} %get-tuple-element.100), channel_id=1, source_target_pairs={{0,2},{1,3},{2,0},{3,1},{4,6},{5,7},{6,4},{7,5}} | collective-permute-start | bytes 2359304 | tf_op jit(solution)/shard_map/ppermute | solution.py:254
  39.3 3.4 %collective-permute-start.9 = (bf16[256,768]{1,0:T(8,128)(2,1)S(1)}, bf16[256,768]{1,0:T(8,128)(2,1)S(1)}, u32[]{:S(2)}, u32[]{:S(2)}) collective-permute-start(bf16[256,768]{1,0:T(8,128)(2,1)S(1)} %collective-permute-done.8.refs_4_), channel_id=1, source_target_pairs={{0,1},{1,0},{2,3},{3,2},{4,5},{5,4},{6,7},{7,6}} | collective-permute-start | bytes 1179656 | tf_op jit(solution)/shard_map/ppermute | solution.py:266
  40.3 2.4 %collective-permute-start.4 = (f32[40,128]{1,0:T(8,128)S(1)}, f32[40,128]{1,0:T(8,128)S(1)}, u32[]{:S(2)}, u32[]{:S(2)}) collective-permute-start(f32[40,128]{1,0:T(8,128)S(1)} %collective-permute-done.1.refs_3_.refs_2_), channel_id=1, source_target_pairs={{0,1},{1,0},{2,3},{3,2},{4,5},{5,4},{6,7},{7,6}} | collective-permute-start | bytes 61448 | tf_op jit(solution)/shard_map/ppermute | solution.py:261
  45.0 2.4 %collective-permute-start.10 = (bf16[512,768]{1,0:T(8,128)(2,1)S(1)}, bf16[512,768]{1,0:T(8,128)(2,1)S(1)}, u32[]{:S(2)}, u32[]{:S(2)}) collective-permute-start(bf16[512,768]{1,0:T(8,128)(2,1)S(1)} %collective-permute-done.7.refs_4_), channel_id=1, source_target_pairs={{0,1},{1,0},{2,3},{3,2},{4,5},{5,4},{6,7},{7,6}} | collective-permute-start | bytes 2359304 | tf_op jit(solution)/shard_map/ppermute | solution.py:266
  45.5 19.1 %collective-permute-start.6 = (bf16[512,768]{1,0:T(8,128)(2,1)S(1)}, bf16[512,768]{1,0:T(8,128)(2,1)S(1)}, u32[]{:S(2)}, u32[]{:S(2)}) collective-permute-start(bf16[512,768]{1,0:T(8,128)(2,1)S(1)} %get-tuple-element.101), channel_id=1, source_target_pairs={{0,2},{1,3},{2,0},{3,1},{4,6},{5,7},{6,4},{7,5}} | collective-permute-start | bytes 2359304 | tf_op jit(solution)/shard_map/ppermute | solution.py:254
  64.6 2.8 %collective-permute-start.11 = (bf16[512,768]{1,0:T(8,128)(2,1)S(1)}, bf16[512,768]{1,0:T(8,128)(2,1)S(1)}, u32[]{:S(2)}, u32[]{:S(2)}) collective-permute-start(bf16[512,768]{1,0:T(8,128)(2,1)S(1)} %collective-permute-done.6.refs_4_), channel_id=1, source_target_pairs={{0,1},{1,0},{2,3},{3,2},{4,5},{5,4},{6,7},{7,6}} | collective-permute-start | bytes 2359304 | tf_op jit(solution)/shard_map/ppermute | solution.py:266
  65.5 19.1 %collective-permute-start.5 = (bf16[512,768]{1,0:T(8,128)(2,1)S(1)}, bf16[512,768]{1,0:T(8,128)(2,1)S(1)}, u32[]{:S(2)}, u32[]{:S(2)}) collective-permute-start(bf16[512,768]{1,0:T(8,128)(2,1)S(1)} %get-tuple-element.102), channel_id=1, source_target_pairs={{0,2},{1,3},{2,0},{3,1},{4,6},{5,7},{6,4},{7,5}} | collective-permute-start | bytes 2359304 | tf_op jit(solution)/shard_map/ppermute | solution.py:254
  84.6 2.8 %collective-permute-start.12 = (bf16[512,768]{1,0:T(8,128)(2,1)S(1)}, bf16[512,768]{1,0:T(8,128)(2,1)S(1)}, u32[]{:S(2)}, u32[]{:S(2)}) collective-permute-start(bf16[512,768]{1,0:T(8,128)(2,1)S(1)} %collective-permute-done.5.refs_4_), channel_id=1, source_target_pairs={{0,1},{1,0},{2,3},{3,2},{4,5},{5,4},{6,7},{7,6}} | collective-permute-start | bytes 2359304 | tf_op jit(solution)/shard_map/ppermute | solution.py:266
  85.5 10.7 %collective-permute-start = (bf16[256,768]{1,0:T(8,128)(2,1)S(1)}, bf16[256,768]{1,0:T(8,128)(2,1)S(1)}, u32[]{:S(2)}, u32[]{:S(2)}) collective-permute-start(bf16[256,768]{1,0:T(8,128)(2,1)S(1)} %slice.16), channel_id=1, source_target_pairs={{0,2},{1,3},{2,0},{3,1},{4,6},{5,7},{6,4},{7,5}} | collective-permute-start | bytes 1179656 | tf_op jit(solution)/shard_map/ppermute | solution.py:254
  96.2 2.7 %collective-permute-start.13 = (bf16[256,768]{1,0:T(8,128)(2,1)S(1)}, bf16[256,768]{1,0:T(8,128)(2,1)S(1)}, u32[]{:S(2)}, u32[]{:S(2)}) collective-permute-start(bf16[256,768]{1,0:T(8,128)(2,1)S(1)} %collective-permute-done.refs_3_.cols_a), channel_id=1, source_target_pairs={{0,1},{1,0},{2,3},{3,2},{4,5},{5,4},{6,7},{7,6}} | collective-permute-start | bytes 1179656 | tf_op jit(solution)/shard_map/ppermute | solution.py:266
  100.7 6.0 %collective-permute-start.14 = (f32[8,128]{1,0:T(8,128)S(1)}, f32[8,128]{1,0:T(8,128)S(1)}, u32[]{:S(2)}, u32[]{:S(2)}) collective-permute-start(f32[8,128]{1,0:T(8,128)S(1)} %get-tuple-element.99), channel_id=1, source_target_pairs={{0,2},{1,3},{2,0},{3,1},{4,6},{5,7},{6,4},{7,5}} | collective-permute-start | bytes 12296 | tf_op jit(solution)/shard_map/ppermute | solution.py:277
  100.7 6.0 %collective-permute-start.15 = (f32[8,128]{1,0:T(8,128)S(1)}, f32[8,128]{1,0:T(8,128)S(1)}, u32[]{:S(2)}, u32[]{:S(2)}) collective-permute-start(f32[8,128]{1,0:T(8,128)S(1)} %get-tuple-element.99), channel_id=1, source_target_pairs={{0,1},{1,0},{2,3},{3,2},{4,5},{5,4},{6,7},{7,6}} | collective-permute-start | bytes 12296 | tf_op jit(solution)/shard_map/ppermute | solution.py:277
  101.0 5.7 %collective-permute-start.16 = (f32[8,128]{1,0:T(8,128)S(1)}, f32[8,128]{1,0:T(8,128)S(1)}, u32[]{:S(2)}, u32[]{:S(2)}) collective-permute-start(f32[8,128]{1,0:T(8,128)S(1)} %get-tuple-element.99), channel_id=1, source_target_pairs={{0,3},{1,2},{2,1},{3,0},{4,7},{5,6},{6,5},{7,4}} | collective-permute-start | bytes 12296 | tf_op jit(solution)/shard_map/ppermute | solution.py:277

commit v4 on v3

--- a/solution.py
+++ b/solution.py
@@ -17,17 +17,39 @@
 FINISH_TILE = 256
 
 
-def prep_kernel(kappa, xv, q_ref, count_ref, rowv, info):
-    rows = xv.shape[0]
+def count_of(info_ref):
+    return jnp.max(info_ref[info_ref.shape[0] - 8:, :]).astype(jnp.int32)
+
+
+def live_tiles(info_ref):
+    return (count_of(info_ref) + FINISH_TILE - 1) // FINISH_TILE
+
+
+def prep_kernel(kappa, raw, q_ref, count_ref, xv, rowv, info, forces, zeros, sem):
+    rows = raw.shape[0]
     chunks = rows // CHUNK
     eye = lax.broadcasted_iota(jnp.int32, (CHUNK, CHUNK), 0) == lax.broadcasted_iota(jnp.int32, (CHUNK, CHUNK), 1)
     lane = lax.broadcasted_iota(jnp.int32, (1, CHUNK), 1)
     count = count_ref[0]
+    tiles = rows // FINISH_TILE
+    live = (count + FINISH_TILE - 1) // FINISH_TILE
+    zeros[...] = jnp.zeros_like(zeros)
+
+    def blank(i):
+        return pltpu.make_async_copy(zeros, forces.at[pl.ds(pl.multiple_of(i * FINISH_TILE, FINISH_TILE), FINISH_TILE)], sem)
+
+    def start(i, _):
+        blank(i).start()
+        return 0
+
+    lax.fori_loop(live, tiles, start, 0)
     info[2 * chunks:, :] = jnp.full((8, CHUNK), count, jnp.int32).astype(F32)
 
     def one(c, _):
         sl = pl.ds(pl.multiple_of(c * CHUNK, CHUNK), CHUNK)
-        block = xv[sl, :].astype(F32)
+        row_ids = lax.broadcasted_iota(jnp.int32, (CHUNK, 1), 0) + c * CHUNK
+        block = jnp.where(row_ids < count, raw[sl, :].astype(F32), 0.0)
+        xv[sl, :] = block.astype(xv.dtype)
         col_s = -kappa * jnp.sum(block * block, axis=1, keepdims=True)
         rowv[0, sl, :] = jnp.broadcast_to(col_s, (CHUNK, CHUNK))
         info[pl.ds(c, 1), :] = jnp.sum(jnp.where(eye, col_s, 0.0), axis=0, keepdims=True)
@@ -38,21 +60,24 @@
 
     lax.fori_loop(0, chunks, one, 0)
 
+    def wait(i, _):
+        blank(i).wait()
+        return 0
+
+    lax.fori_loop(live, tiles, wait, 0)
+
 
 def prep(x, charges, counts):
     rows, width = x.shape
     chunks = rows // CHUNK
     return pl.pallas_call(
         functools.partial(prep_kernel, LOG2E * 0.5 / width),
-        out_shape=[pltpu.VMEM((2, rows, CHUNK), F32),
-                   jax.ShapeDtypeStruct((2 * chunks + 8, CHUNK), F32)],
-        in_specs=[VMEM_SPEC, VMEM_SPEC, pl.BlockSpec(memory_space=pltpu.SMEM)], out_specs=[VMEM_SPEC] * 2,
+        out_shape=[jax.ShapeDtypeStruct(x.shape, x.dtype), pltpu.VMEM((2, rows, CHUNK), F32),
+                   jax.ShapeDtypeStruct((2 * chunks + 8, CHUNK), F32), jax.ShapeDtypeStruct((rows, width), F32)],
+        in_specs=[VMEM_SPEC, VMEM_SPEC, pl.BlockSpec(memory_space=pltpu.SMEM)], out_specs=[VMEM_SPEC] * 3 + [HBM_SPEC],
+        scratch_shapes=[pltpu.VMEM((FINISH_TILE, width), F32), pltpu.SemaphoreType.DMA],
         compiler_params=pltpu.CompilerParams(vmem_limit_bytes=VMEM_LIMIT),
         name='prep')(x, charges.reshape(chunks, CHUNK), counts)
-
-
-def count_of(info_ref):
-    return jnp.max(info_ref[info_ref.shape[0] - 8:, :]).astype(jnp.int32)
 
 
 def weights(kappa, gram, row_a, row_c, col_a, col_c):
@@ -126,47 +151,85 @@
     lax.fori_loop(0, tiles, tile, 0)
 
 
+def pair_kernel(cfg, xv, rowv, info_a, info_b, cols_a, cols_b, t_in, s_in, tv, sv, xc):
+    start, kappa = cfg
+    block_chunks = xv.shape[0] // CHUNK
+    xc[:CHUNK, :] = cols_a[...]
+    xc[CHUNK:, :] = cols_b[...]
+
+    @pl.when(jnp.maximum(count_of(info_a), count_of(info_b)) > start * CHUNK)
+    def _():
+        w_old = None
+        for r0 in range(0, xv.shape[0] + SUB_ROWS, SUB_ROWS):
+            w_new = None
+            if r0 < xv.shape[0]:
+                rsl = pl.ds(r0, SUB_ROWS)
+                gram = lax.dot_general(xv[rsl, :], xc[...], (((1,), (1,)), ((), ())), preferred_element_type=F32)
+                w = [weights(kappa, gram[:, k * CHUNK:(k + 1) * CHUNK], rowv[0, rsl, :], rowv[1, rsl, :],
+                             info[start:start + 1, :], info[block_chunks + start:block_chunks + start + 1, :])
+                     for k, info in enumerate((info_a, info_b))]
+                sv[rsl, :] += w[0] + w[1]
+                w_new = jnp.concatenate([part.astype(jnp.bfloat16) for part in w], axis=1)
+            if w_old is not None:
+                tv[pl.ds(r0 - SUB_ROWS, SUB_ROWS), :] += jnp.dot(w_old, xc[...], preferred_element_type=F32)
+            w_old = w_new
+
+
+def pair_step(x, rowf, infos, cols, start, carry):
+    rows, width = x.shape
+    ins = [x, rowf, *infos, *cols, *carry]
+    return pl.pallas_call(
+        functools.partial(pair_kernel, (start, LOG2E * 0.5 / width)),
+        out_shape=[pltpu.VMEM((rows, width), F32), pltpu.VMEM((rows, 128), F32)],
+        in_specs=[VMEM_SPEC] * len(ins), out_specs=[VMEM_SPEC] * 2,
+        scratch_shapes=[pltpu.VMEM((2 * CHUNK, width), x.dtype)],
+        input_output_aliases={len(ins) - 2: 0, len(ins) - 1: 1},
+        compiler_params=pltpu.CompilerParams(vmem_limit_bytes=VMEM_LIMIT),
+        cost_estimate=pl.CostEstimate(flops=8 * rows * CHUNK * width, bytes_accessed=rows * width, transcendentals=0))(*ins)
+
+
 def last_kernel(cfg, *refs):
-    start, num, total, kappa = cfg
-    xv, rowv, src_info, cols, _, sv, wv = refs[:7]
+    start, half, kappa = cfg
+    xv, rowv, src_info, cols = refs[:4]
+    sv, wv = refs[6:8] if half else refs[5:7]
     block_chunks = xv.shape[0] // CHUNK
 
     def row_tile(rt, acc):
         rsl = pl.ds(pl.multiple_of(rt * SUB_ROWS, SUB_ROWS), SUB_ROWS)
-        sums = sv[rsl, :]
         gram = lax.dot_general(xv[rsl, :], cols[...], (((1,), (1,)), ((), ())), preferred_element_type=F32)
-        for k in range(num):
-            w = weights(kappa, gram[:, k * CHUNK:(k + 1) * CHUNK], rowv[0, rsl, :], rowv[1, rsl, :],
-                        src_info[start + k:start + k + 1, :], src_info[block_chunks + start + k:block_chunks + start + k + 1, :])
-            sums = sums + w
-            wv[rsl, k * CHUNK:(k + 1) * CHUNK] = w.astype(jnp.bfloat16)
+        w = weights(kappa, gram, rowv[0, rsl, :], rowv[1, rsl, :],
+                    src_info[start:start + 1, :], src_info[block_chunks + start:block_chunks + start + 1, :])
+        sums = sv[rsl, :] + w
+        wv[rsl, half * CHUNK:(half + 1) * CHUNK] = w.astype(jnp.bfloat16)
         sv[rsl, :] = sums
-        if total:
+        if half:
             for g in range(SUB_ROWS // 8):
                 acc = acc + sums[g * 8:(g + 1) * 8]
         return acc
 
     part = lax.fori_loop(0, xv.shape[0] // SUB_ROWS, row_tile, jnp.zeros((8, 128), F32))
-    if total:
-        refs[7][...] = part
-
-
-def last_step(x, rowf, src_info, cols, start, s_sum, total):
-    rows, width = x.shape
-    num = cols.shape[0] // CHUNK
-    ins = [x, rowf, src_info, cols, s_sum]
-    part_shape = [jax.ShapeDtypeStruct((8, 128), F32)] if total else []
-    return pl.pallas_call(
-        functools.partial(last_kernel, (start, num, total, LOG2E * 0.5 / width)),
-        out_shape=[pltpu.VMEM((rows, 128), F32), pltpu.VMEM((rows, num * CHUNK), jnp.bfloat16)] + part_shape,
+    if half:
+        refs[8][...] = part
+
+
+def last_step(x, rowf, src_info, cols, start, carry, half):
+    rows, width = x.shape
+    ins = [x, rowf, src_info, cols, *carry]
+    part_shape = [jax.ShapeDtypeStruct((8, 128), F32)] if half else []
+    return pl.pallas_call(
+        functools.partial(last_kernel, (start, half, LOG2E * 0.5 / width)),
+        out_shape=[pltpu.VMEM((rows, 128), F32), pltpu.VMEM((rows, 2 * CHUNK), jnp.bfloat16)] + part_shape,
         in_specs=[VMEM_SPEC] * len(ins), out_specs=[VMEM_SPEC] * (2 + len(part_shape)),
-        input_output_aliases={len(ins) - 1: 0},
-        compiler_params=pltpu.CompilerParams(vmem_limit_bytes=VMEM_LIMIT),
-        cost_estimate=pl.CostEstimate(flops=2 * rows * num * CHUNK * width, bytes_accessed=rows * width, transcendentals=0))(*ins)
-
-
-def finish_kernel(inv_len2, xv, tv, sv, wa, wb, cols_a, cols_b, forces, buf, out_sems):
-    num = xv.shape[0] // FINISH_TILE
+        input_output_aliases={4 + k: k for k in range(len(carry))},
+        compiler_params=pltpu.CompilerParams(vmem_limit_bytes=VMEM_LIMIT),
+        cost_estimate=pl.CostEstimate(flops=2 * rows * CHUNK * width, bytes_accessed=rows * width, transcendentals=0))(*ins)
+
+
+def finish_kernel(inv_len2, xv, tv, sv, wv, cols_a, cols_b, my_info, blank, forces, xc, buf, out_sems):
+    del blank
+    xc[:CHUNK, :] = cols_a[...]
+    xc[CHUNK:, :] = cols_b[...]
+    num = live_tiles(my_info)
 
     def out(i):
         return pltpu.make_async_copy(
@@ -179,15 +242,18 @@
 
         sl = pl.ds(pl.multiple_of(i * FINISH_TILE, FINISH_TILE), FINISH_TILE)
         total = jnp.sum(sv[sl, :], axis=1, keepdims=True)
-        pulled = (tv[sl, :] + jnp.dot(wa[sl, :], cols_a[...], preferred_element_type=F32)
-                  + jnp.dot(wb[sl, :], cols_b[...], preferred_element_type=F32))
+        pulled = tv[sl, :] + jnp.dot(wv[sl, :], xc[...], preferred_element_type=F32)
         buf[lax.rem(i, 4)] = (total * xv[sl, :].astype(F32) - pulled) * inv_len2
         out(i).start()
         return 0
 
     lax.fori_loop(0, num, one, 0)
-    for i in range(num - 4, num):
+
+    def drain(i, _):
         out(i).wait()
+        return 0
+
+    lax.fori_loop(jnp.maximum(num - 4, 0), num, drain, 0)
 
 
 def finish(*ins):
@@ -196,8 +262,10 @@
     return pl.pallas_call(
         functools.partial(finish_kernel, 1.0 / width),
         out_shape=jax.ShapeDtypeStruct((rows, width), F32),
-        in_specs=[VMEM_SPEC] * len(ins), out_specs=HBM_SPEC,
-        scratch_shapes=[pltpu.VMEM((4, FINISH_TILE, width), F32), pltpu.SemaphoreType.DMA((4,))],
+        in_specs=[VMEM_SPEC] * (len(ins) - 1) + [HBM_SPEC], out_specs=HBM_SPEC,
+        scratch_shapes=[pltpu.VMEM((2 * CHUNK, width), x.dtype), pltpu.VMEM((4, FINISH_TILE, width), F32),
+                        pltpu.SemaphoreType.DMA((4,))],
+        input_output_aliases={len(ins) - 1: 0},
         compiler_params=pltpu.CompilerParams(vmem_limit_bytes=VMEM_LIMIT),
         cost_estimate=pl.CostEstimate(flops=rows * width * 1000, bytes_accessed=rows * width * 4, transcendentals=0),
         name='finish')(*ins)
@@ -226,11 +294,7 @@
         input_output_aliases={} if first else {len(ins) - 2: 0, len(ins) - 1: 1}, **common)(*ins)
 
 
-PIECES = (256, 512, 512, 512, 256)
-
-
-def after(value, *others):
-    return lax.optimization_barrier((value,) + others)[0]
+PIECES = (512, 512, 512, 256, 128, 128)
 
 
 def solution(mesh):
@@ -242,18 +306,17 @@
     def per_device(positions, charges, counts):
         rows, _ = positions.shape
         chunks = rows // CHUNK
-        x = pltpu.with_memory_space_constraint(positions, pltpu.VMEM)
-        head = positions[:PIECES[0]]
+        raw = pltpu.with_memory_space_constraint(positions, pltpu.VMEM)
+        head = jnp.where(jnp.arange(PIECES[0])[:, None] < counts[0], positions[:PIECES[0]], 0)
         arrived = [lax.ppermute(head, 'row', cross_perm)]
-        positions = after(positions, head)
-        rowf, info = prep(x, charges, counts)
+        x, rowf, info, blank = prep(raw, charges, counts)
         info_cross = lax.ppermute(info, 'row', cross_perm)
         info_pair = lax.ppermute(info, 'row', pair_perm)
         off = PIECES[0]
         for size in PIECES[1:]:
-            arrived.append(lax.ppermute(positions[off:off + size], 'row', cross_perm))
+            arrived.append(lax.ppermute(x[off:off + size], 'row', cross_perm))
             off += size
-        partner = lax.ppermute(positions, 'row', pair_perm)
+        partner = lax.ppermute(x, 'row', pair_perm)
         carry = step(x, rowf, info, None, None, 0, chunks, 4, None)
         partner, *carry = lax.optimization_barrier((partner, *carry))
         carry = step(x, rowf, info, info_pair, partner, 0, chunks, 4, carry)
@@ -264,18 +327,20 @@
             num = PIECES[k] // CHUNK
             piece, *carry = lax.optimization_barrier((piece, *carry))
             relay = lax.ppermute(piece, 'row', pair_perm)
-            if k < len(PIECES) - 1:
+            if num > 1:
                 carry = step(x, rowf, info, info_cross, piece, off, num, min(4, num), carry)
                 carry = step(x, rowf, info, info_diag, relay, off, num, min(4, num), carry)
+            elif k < len(PIECES) - 1:
+                carry = pair_step(x, rowf, (info_cross, info_diag), (piece, relay), off, carry)
             else:
                 t_sum, s_sum = carry
-                s_sum, w_piece = last_step(x, rowf, info_cross, piece, off, s_sum, False)
-                s_sum, w_relay, part = last_step(x, rowf, info_diag, relay, off, s_sum, True)
+                carry = last_step(x, rowf, info_cross, piece, off, (s_sum,), 0)
+                s_sum, w_last, part = last_step(x, rowf, info_diag, relay, off, carry, 1)
             off += num
         total = part
         for perm in (cross_perm, pair_perm, diag_perm):
             total = total + lax.ppermute(part, 'row', perm)
-        forces = finish(x, t_sum, s_sum, w_piece, w_relay, piece, relay)
+        forces = finish(x, t_sum, s_sum, w_last, piece, relay, info, blank)
         return forces, (0.5 * jnp.sum(total)).reshape(1)
 
     row_spec = P(('sys', 'row'), None)

time: 109 us -> 116 us (1.064)
  waiting for transfers between devices: 36.3 us -> 40.4 us
  Pallas kernels: 55.7 us -> 59.7 us
    ppermute x5 -> x6, waiting for transfers between devices: 31.2 us -> 34.9 us  [the longest x5 34.9 us: per_device(): arrived.append(lax.ppermute(x[off:off + size], 'row', cross_perm))]
    pallas_call x10, Pallas kernels: 45.7 us -> 48.3 us  [step(): pl.pallas_call(kernel, out_shape=[pltpu.VMEM((rows, width), F32), pltpu.V...]
    pallas_call x2 -> x3, Pallas kernels: 3.66 us -> 5.36 us  [the longest x2 3.03 us: last_step(): pl.pallas_call(functools.partial(last_kernel, (start, half, LOG2E * 0.5 /...]
    ppermute x5 -> x6, starting transfers between devices: 4.11 us -> 4.9 us  [per_device(): relay = lax.ppermute(piece, 'row', pair_perm)]
    ppermute x5 -> x6, waiting for transfers between devices: 5.06 us -> 5.46 us  [per_device(): relay = lax.ppermute(piece, 'row', pair_perm)]
  transfers between devices with their start and end apart: 17 -> 19, of which waited for: 6 -> 9; matrix products, arithmetic and copies ran while one was open for 0% -> 0% of each run, Pallas kernels for 49% -> 48%
where the time goes in v4:
time: 116 us
  Pallas kernels  59.7 us (51%)
  waiting for transfers between devices  40.4 us (35%)
  starting transfers between devices  9.14 us (8%)
  between operations  3.32 us (3%)
  local copies, waits for them, and re-layouts  2.73 us (2%)
    pallas_call x10, Pallas kernels, step(): pl.pallas_call(kernel, out_shape=[pltpu.VMEM((rows, width), F32), pltpu.V...  48.3 us
    ppermute x5, waiting for transfers between devices, per_device(): arrived.append(lax.ppermute(x[off:off + size], 'row', cross_perm))  34.9 us
    ppermute x6, waiting for transfers between devices, per_device(): relay = lax.ppermute(piece, 'row', pair_perm)  5.46 us
    ppermute x6, starting transfers between devices, per_device(): relay = lax.ppermute(piece, 'row', pair_perm)  4.9 us
    pallas_call x1, Pallas kernels, finish(): pl.pallas_call(functools.partial(finish_kernel, 1.0 / width), out_shape=j...  3.42 us
    pallas_call x2, Pallas kernels, last_step(): pl.pallas_call(functools.partial(last_kernel, (start, half, LOG2E * 0.5 /...  3.03 us
    pallas_call x1, Pallas kernels, prep(): pl.pallas_call(functools.partial(prep_kernel, LOG2E * 0.5 / width), out_s...  2.6 us
    unnamed x4, local copies, waits for them, and re-layouts  2.58 us
  transfers between devices with their start and end apart: 19, of which 9 were waited for; matrix products, arithmetic and copies ran while one was open for 0% of the time, Pallas kernels for 48%

profile of v4, /device:TPU:5, one launch (start us, length us, event | category | flops | bytes accessed | tf_op | source)
XLA Modules:
  0.0 116.0 jit_solution(12157070870414529404)
XLA Ops:
  1.3 1.9 %copy-done = bf16[2048,768]{1,0:T(8,128)(2,1)S(1)} copy-done((bf16[2048,768]{1,0:T(8,128)(2,1)S(1)}, bf16[2048,768]{1,0:T(8,128)(2,1)}, u32[]{:S(2)}) %copy-start) | copy-done | bytes 3145752
  3.2 0.7 copy-done.1
  3.9 2.6 %prep.1 = (bf16[2048,768]{1,0:T(8,128)(2,1)S(1)}, f32[2,2048,128]{2,1,0:T(8,128)S(1)}, f32[40,128]{1,0:T(8,128)S(1)}, f32[2048,768]{1,0:T(8,128)}) custom-call(bf16[2048,768]{1,0:T(8,128)(2,1)S(1)} %copy-done, f32[16,128]{1,0:T(8,128)S(1)} %bitcast.4, s32[1]{0:T(128)} %copy.53.count_ref), custom_call_target="tpu_custom_call" | custom-call | tf_op jit(solution)/shard_map/prep/pallas_call | solution.py:73
  6.5 0.7 collective-permute-start.3
  7.2 0.0 collective-permute-start.2
  7.2 1.2 %collective-permute-start.1 = (f32[40,128]{1,0:T(8,128)S(1)}, f32[40,128]{1,0:T(8,128)S(1)}, u32[]{:S(2)}, u32[]{:S(2)}) collective-permute-start(f32[40,128]{1,0:T(8,128)S(1)} %get-tuple-element.59.refs_2_.my_info), channel_id=1, source_target_pairs={{0,2},{1,3},{2,0},{3,1},{4,6},{5,7},{6,4},{7,5}} | collective-permute-start | bytes 61448 | tf_op jit(solution)/shard_map/ppermute | solution.py:313
  8.4 0.1 slice_select_fusion
  8.6 0.3 collective-permute-start.9
  8.9 17.9 %step_0_16.2 = (f32[2048,768]{1,0:T(8,128)S(1)}, f32[2048,128]{1,0:T(8,128)S(1)}) custom-call(bf16[2048,768]{1,0:T(8,128)(2,1)S(1)} %get-tuple-element.57.refs_0_.xv, f32[2,2048,128]{2,1,0:T(8,128)S(1)} %get-tuple-element.58.refs_1_.rowv, f32[40,128]{1,0:T(8,128)S(1)} %get-tuple-element.59.refs_2_.my_info), custom_call_target="tpu_custom_call" | custom-call | flops 7730940928 | bytes 1572864 | tf_op jit(solution)/shard_map/step_0_16/pallas_call | solution.py:290
  26.8 11.6 %step_0_16.3 = (f32[2048,768]{1,0:T(8,128)S(1)}, f32[2048,128]{1,0:T(8,128)S(1)}) custom-call(bf16[2048,768]{1,0:T(8,128)(2,1)S(1)} %get-tuple-element.57.refs_0_.xv, f32[2,2048,128]{2,1,0:T(8,128)S(1)} %get-tuple-element.58.refs_1_.rowv, f32[40,128]{1,0:T(8,128)S(1)} %get-tuple-element.59.refs_2_.my_info, ...), custom_call_target="tpu_custom_call", output_to_operand_aliasing={{0}: (5, {}), {1}: (6, {})} | custom-call | flops 7730940928 | bytes 1572864 | tf_op jit(solution)/shard_map/step_0_16/pallas_call | solution.py:290
  38.4 0.6 collective-permute-start.10
  39.0 0.1 fusion
  39.1 0.0 collective-permute-start.8
  39.1 0.0 collective-permute-start.4
  39.1 3.9 %step_0_4.2 = (f32[2048,768]{1,0:T(8,128)S(1)}, f32[2048,128]{1,0:T(8,128)S(1)}) custom-call(bf16[2048,768]{1,0:T(8,128)(2,1)S(1)} %get-tuple-element.57.refs_0_.xv, f32[2,2048,128]{2,1,0:T(8,128)S(1)} %get-tuple-element.58.refs_1_.rowv, f32[40,128]{1,0:T(8,128)S(1)} %get-tuple-element.59.refs_2_.my_info, ...), custom_call_target="tpu_custom_call", output_to_operand_aliasing={{0}: (5, {}), {1}: (6, {})} | custom-call | flops 1932735232 | bytes 1572864 | tf_op jit(solution)/shard_map/step_0_4/pallas_call | solution.py:290
  43.1 4.1 %step_0_4.3 = (f32[2048,768]{1,0:T(8,128)S(1)}, f32[2048,128]{1,0:T(8,128)S(1)}) custom-call(bf16[2048,768]{1,0:T(8,128)(2,1)S(1)} %get-tuple-element.57.refs_0_.xv, f32[2,2048,128]{2,1,0:T(8,128)S(1)} %get-tuple-element.58.refs_1_.rowv, f32[40,128]{1,0:T(8,128)S(1)} %get-tuple-element.59.refs_2_.my_info, ...), custom_call_target="tpu_custom_call", output_to_operand_aliasing={{0}: (5, {}), {1}: (6, {})} | custom-call | flops 1932735232 | bytes 1572864 | tf_op jit(solution)/shard_map/step_0_4/pallas_call | solution.py:290
  47.2 10.9 %collective-permute-done.8.refs_4_ = bf16[512,768]{1,0:T(8,128)(2,1)S(1)} collective-permute-done((bf16[512,768]{1,0:T(8,128)(2,1)S(1)}, bf16[512,768]{1,0:T(8,128)(2,1)S(1)}, u32[]{:S(2)}, u32[]{:S(2)}) %collective-permute-start.8) | collective-permute-done | bytes 786464 | tf_op jit(solution)/shard_map/ppermute | solution.py:317
  58.2 0.9 collective-permute-start.11
  59.0 0.0 collective-permute-start.7
  59.0 0.1 step_4_4.2
  59.2 1.8 %collective-permute-done.11.refs_4_ = bf16[512,768]{1,0:T(8,128)(2,1)S(1)} collective-permute-done((bf16[512,768]{1,0:T(8,128)(2,1)S(1)}, bf16[512,768]{1,0:T(8,128)(2,1)S(1)}, u32[]{:S(2)}, u32[]{:S(2)}) %collective-permute-start.11) | collective-permute-done | bytes 786464 | tf_op jit(solution)/shard_map/ppermute | solution.py:329
  61.0 3.9 %step_4_4.3 = (f32[2048,768]{1,0:T(8,128)S(1)}, f32[2048,128]{1,0:T(8,128)S(1)}) custom-call(bf16[2048,768]{1,0:T(8,128)(2,1)S(1)} %get-tuple-element.57.refs_0_.xv, f32[2,2048,128]{2,1,0:T(8,128)S(1)} %get-tuple-element.58.refs_1_.rowv, f32[40,128]{1,0:T(8,128)S(1)} %get-tuple-element.59.refs_2_.my_info, ...), custom_call_target="tpu_custom_call", output_to_operand_aliasing={{0}: (5, {}), {1}: (6, {})} | custom-call | flops 1932735232 | bytes 1572864 | tf_op jit(solution)/shard_map/step_4_4/pallas_call | solution.py:290
  64.9 13.2 %collective-permute-done.7.refs_4_ = bf16[512,768]{1,0:T(8,128)(2,1)S(1)} collective-permute-done((bf16[512,768]{1,0:T(8,128)(2,1)S(1)}, bf16[512,768]{1,0:T(8,128)(2,1)S(1)}, u32[]{:S(2)}, u32[]{:S(2)}) %collective-permute-start.7) | collective-permute-done | bytes 786464 | tf_op jit(solution)/shard_map/ppermute | solution.py:317
  78.1 0.9 collective-permute-start.12
  79.0 0.0 collective-permute-start.6
  79.1 0.4 step_8_4.2
  79.4 1.5 %collective-permute-done.12.refs_4_ = bf16[512,768]{1,0:T(8,128)(2,1)S(1)} collective-permute-done((bf16[512,768]{1,0:T(8,128)(2,1)S(1)}, bf16[512,768]{1,0:T(8,128)(2,1)S(1)}, u32[]{:S(2)}, u32[]{:S(2)}) %collective-permute-start.12) | collective-permute-done | bytes 786464 | tf_op jit(solution)/shard_map/ppermute | solution.py:329
  80.9 3.9 %step_8_4.3 = (f32[2048,768]{1,0:T(8,128)S(1)}, f32[2048,128]{1,0:T(8,128)S(1)}) custom-call(bf16[2048,768]{1,0:T(8,128)(2,1)S(1)} %get-tuple-element.57.refs_0_.xv, f32[2,2048,128]{2,1,0:T(8,128)S(1)} %get-tuple-element.58.refs_1_.rowv, f32[40,128]{1,0:T(8,128)S(1)} %get-tuple-element.59.refs_2_.my_info, ...), custom_call_target="tpu_custom_call", output_to_operand_aliasing={{0}: (5, {}), {1}: (6, {})} | custom-call | flops 1932735232 | bytes 1572864 | tf_op jit(solution)/shard_map/step_8_4/pallas_call | solution.py:290
  84.9 4.9 %collective-permute-done.6.refs_4_ = bf16[256,768]{1,0:T(8,128)(2,1)S(1)} collective-permute-done((bf16[256,768]{1,0:T(8,128)(2,1)S(1)}, bf16[256,768]{1,0:T(8,128)(2,1)S(1)}, u32[]{:S(2)}, u32[]{:S(2)}) %collective-permute-start.6) | collective-permute-done | bytes 393248 | tf_op jit(solution)/shard_map/ppermute | solution.py:317
  89.7 0.9 collective-permute-start.13
  90.6 0.0 collective-permute-start.5
  90.6 0.1 step_12_2.2
  90.8 1.1 collective-permute-done.13.refs_4_
  91.9 2.3 %step_12_2.3 = (f32[2048,768]{1,0:T(8,128)S(1)}, f32[2048,128]{1,0:T(8,128)S(1)}) custom-call(bf16[2048,768]{1,0:T(8,128)(2,1)S(1)} %get-tuple-element.57.refs_0_.xv, f32[2,2048,128]{2,1,0:T(8,128)S(1)} %get-tuple-element.58.refs_1_.rowv, f32[40,128]{1,0:T(8,128)S(1)} %get-tuple-element.59.refs_2_.my_info, ...), custom_call_target="tpu_custom_call", output_to_operand_aliasing={{0}: (5, {}), {1}: (6, {})} | custom-call | flops 966367616 | bytes 1572864 | tf_op jit(solution)/shard_map/step_12_2/pallas_call | solution.py:290
  94.3 2.8 %collective-permute-done.5.cols_a = bf16[128,768]{1,0:T(8,128)(2,1)S(1)} collective-permute-done((bf16[128,768]{1,0:T(8,128)(2,1)S(1)}, bf16[128,768]{1,0:T(8,128)(2,1)S(1)}, u32[]{:S(2)}, u32[]{:S(2)}) %collective-permute-start.5) | collective-permute-done | bytes 196640 | tf_op jit(solution)/shard_map/ppermute | solution.py:317
  97.1 0.9 collective-permute-start.14
  97.9 0.0 collective-permute-start
  98.0 1.1 collective-permute-done.14.cols_b
  99.0 2.3 %shard_map.50 = (f32[2048,768]{1,0:T(8,128)S(1)}, f32[2048,128]{1,0:T(8,128)S(1)}) custom-call(bf16[2048,768]{1,0:T(8,128)(2,1)S(1)} %get-tuple-element.57.refs_0_.xv, f32[2,2048,128]{2,1,0:T(8,128)S(1)} %get-tuple-element.58.refs_1_.rowv, f32[40,128]{1,0:T(8,128)S(1)} %collective-permute-done.1.refs_3_.info_a.refs_2_, ...), custom_call_target="tpu_custom_call", output_to_operand_aliasing={{0}: (6, {}), {1}: (7, {})} | custom-call | flops 1610612736 | bytes 1572864 | tf_op jit(solution)/shard_map/pallas_call | solution.py:181
  101.4 3.0 %collective-permute-done.refs_3_.cols_a = bf16[128,768]{1,0:T(8,128)(2,1)S(1)} collective-permute-done((bf16[128,768]{1,0:T(8,128)(2,1)S(1)}, bf16[128,768]{1,0:T(8,128)(2,1)S(1)}, u32[]{:S(2)}, u32[]{:S(2)}) %collective-permute-start) | collective-permute-done | bytes 196640 | tf_op jit(solution)/shard_map/ppermute | solution.py:317
  104.4 0.9 collective-permute-start.15
  105.3 1.5 %shard_map.51 = (f32[2048,128]{1,0:T(8,128)S(1)}, bf16[2048,256]{1,0:T(8,128)(2,1)S(1)}) custom-call(bf16[2048,768]{1,0:T(8,128)(2,1)S(1)} %get-tuple-element.57.refs_0_.xv, f32[2,2048,128]{2,1,0:T(8,128)S(1)} %get-tuple-element.58.refs_1_.rowv, f32[40,128]{1,0:T(8,128)S(1)} %collective-permute-done.1.refs_3_.info_a.refs_2_, ...), custom_call_target="tpu_custom_call", output_to_operand_aliasing={{0}: (4, {})} | custom-call | flops 402653184 | bytes 1572864 | tf_op jit(solution)/shard_map/pallas_call | solution.py:219
  106.8 1.5 %shard_map.52 = (f32[2048,128]{1,0:T(8,128)S(1)}, bf16[2048,256]{1,0:T(8,128)(2,1)S(1)}, f32[8,128]{1,0:T(8,128)S(1)}) custom-call(bf16[2048,768]{1,0:T(8,128)(2,1)S(1)} %get-tuple-element.57.refs_0_.xv, f32[2,2048,128]{2,1,0:T(8,128)S(1)} %get-tuple-element.58.refs_1_.rowv, ...), custom_call_target="tpu_custom_call", output_to_operand_aliasing={{0}: (4, {}), {1}: (5, {})} | custom-call | flops 402653184 | bytes 1572864 | tf_op jit(solution)/shard_map/pallas_call | solution.py:219
  108.3 0.0 collective-permute-start.16
  108.4 0.3 collective-permute-start.17
  108.6 1.6 %collective-permute-start.18 = (f32[8,128]{1,0:T(8,128)S(1)}, f32[8,128]{1,0:T(8,128)S(1)}, u32[]{:S(2)}, u32[]{:S(2)}) collective-permute-start(f32[8,128]{1,0:T(8,128)S(1)} %get-tuple-element.111), channel_id=1, source_target_pairs={{0,3},{1,2},{2,1},{3,0},{4,7},{5,6},{6,5},{7,4}} | collective-permute-start | bytes 12296 | tf_op jit(solution)/shard_map/ppermute | solution.py:342
  110.2 3.4 %finish.1 = f32[2048,768]{1,0:T(8,128)} custom-call(bf16[2048,768]{1,0:T(8,128)(2,1)S(1)} %get-tuple-element.57.refs_0_.xv, f32[2048,768]{1,0:T(8,128)S(1)} %get-tuple-element.103.tv, f32[2048,128]{1,0:T(8,128)S(1)} %get-tuple-element.108.sv, bf16[2048,256]{1,0:T(8,128)(2,1)S(1)} %get-tuple-element.109.wv, ...), custom_call_target="tpu_custom_call", output_to_operand_aliasing={{}: (7, {})} | custom-call | flops 1572864000 | bytes 6291456 | tf_op jit(solution)/shard_map/finish/pallas_call | solution.py:262
  113.7 0.6 add_reduce_fusion
  (15 shorter events, 0.1 us)
Async XLA Ops:
  1.3 1.9 %copy-start = (bf16[2048,768]{1,0:T(8,128)(2,1)S(1)}, bf16[2048,768]{1,0:T(8,128)(2,1)}, u32[]{:S(2)}) copy-start(bf16[2048,768]{1,0:T(8,128)(2,1)} %raw.1) | copy-start | bytes 9437188
  3.2 0.7 copy-start.1
  6.5 20.3 %collective-permute-start.3 = (bf16[2048,768]{1,0:T(8,128)(2,1)S(1)}, bf16[2048,768]{1,0:T(8,128)(2,1)S(1)}, u32[]{:S(2)}, u32[]{:S(2)}) collective-permute-start(bf16[2048,768]{1,0:T(8,128)(2,1)S(1)} %get-tuple-element.57.refs_0_.xv), channel_id=1, source_target_pairs={{0,1},{1,0},{2,3},{3,2},{4,5},{5,4},{6,7},{7,6}} | collective-permute-start | bytes 9437192 | tf_op jit(solution)/shard_map/ppermute | solution.py:319
  7.2 19.6 %collective-permute-start.2 = (f32[40,128]{1,0:T(8,128)S(1)}, f32[40,128]{1,0:T(8,128)S(1)}, u32[]{:S(2)}, u32[]{:S(2)}) collective-permute-start(f32[40,128]{1,0:T(8,128)S(1)} %get-tuple-element.59.refs_2_.my_info), channel_id=1, source_target_pairs={{0,1},{1,0},{2,3},{3,2},{4,5},{5,4},{6,7},{7,6}} | collective-permute-start | bytes 61448 | tf_op jit(solution)/shard_map/ppermute | solution.py:314
  7.2 31.1 %collective-permute-start.1 = (f32[40,128]{1,0:T(8,128)S(1)}, f32[40,128]{1,0:T(8,128)S(1)}, u32[]{:S(2)}, u32[]{:S(2)}) collective-permute-start(f32[40,128]{1,0:T(8,128)S(1)} %get-tuple-element.59.refs_2_.my_info), channel_id=1, source_target_pairs={{0,2},{1,3},{2,0},{3,1},{4,6},{5,7},{6,4},{7,5}} | collective-permute-start | bytes 61448 | tf_op jit(solution)/shard_map/ppermute | solution.py:313
  8.6 29.8 %collective-permute-start.9 = (bf16[512,768]{1,0:T(8,128)(2,1)S(1)}, bf16[512,768]{1,0:T(8,128)(2,1)S(1)}, u32[]{:S(2)}, u32[]{:S(2)}) collective-permute-start(bf16[512,768]{1,0:T(8,128)(2,1)S(1)} %slice_select_fusion), channel_id=1, source_target_pairs={{0,2},{1,3},{2,0},{3,1},{4,6},{5,7},{6,4},{7,5}} | collective-permute-start | bytes 2359304 | tf_op jit(solution)/shard_map/ppermute | solution.py:311
  38.4 4.7 %collective-permute-start.10 = (bf16[512,768]{1,0:T(8,128)(2,1)S(1)}, bf16[512,768]{1,0:T(8,128)(2,1)S(1)}, u32[]{:S(2)}, u32[]{:S(2)}) collective-permute-start(bf16[512,768]{1,0:T(8,128)(2,1)S(1)} %collective-permute-done.9.refs_4_), channel_id=1, source_target_pairs={{0,1},{1,0},{2,3},{3,2},{4,5},{5,4},{6,7},{7,6}} | collective-permute-start | bytes 2359304 | tf_op jit(solution)/shard_map/ppermute | solution.py:329
  39.1 19.1 %collective-permute-start.8 = (bf16[512,768]{1,0:T(8,128)(2,1)S(1)}, bf16[512,768]{1,0:T(8,128)(2,1)S(1)}, u32[]{:S(2)}, u32[]{:S(2)}) collective-permute-start(bf16[512,768]{1,0:T(8,128)(2,1)S(1)} %get-tuple-element.112), channel_id=1, source_target_pairs={{0,2},{1,3},{2,0},{3,1},{4,6},{5,7},{6,4},{7,5}} | collective-permute-start | bytes 2359304 | tf_op jit(solution)/shard_map/ppermute | solution.py:317
  39.1 4.0 %collective-permute-start.4 = (f32[40,128]{1,0:T(8,128)S(1)}, f32[40,128]{1,0:T(8,128)S(1)}, u32[]{:S(2)}, u32[]{:S(2)}) collective-permute-start(f32[40,128]{1,0:T(8,128)S(1)} %collective-permute-done.1.refs_3_.info_a.refs_2_), channel_id=1, source_target_pairs={{0,1},{1,0},{2,3},{3,2},{4,5},{5,4},{6,7},{7,6}} | collective-permute-start | bytes 61448 | tf_op jit(solution)/shard_map/ppermute | solution.py:324
  58.2 2.8 %collective-permute-start.11 = (bf16[512,768]{1,0:T(8,128)(2,1)S(1)}, bf16[512,768]{1,0:T(8,128)(2,1)S(1)}, u32[]{:S(2)}, u32[]{:S(2)}) collective-permute-start(bf16[512,768]{1,0:T(8,128)(2,1)S(1)} %collective-permute-done.8.refs_4_), channel_id=1, source_target_pairs={{0,1},{1,0},{2,3},{3,2},{4,5},{5,4},{6,7},{7,6}} | collective-permute-start | bytes 2359304 | tf_op jit(solution)/shard_map/ppermute | solution.py:329
  59.0 19.1 %collective-permute-start.7 = (bf16[512,768]{1,0:T(8,128)(2,1)S(1)}, bf16[512,768]{1,0:T(8,128)(2,1)S(1)}, u32[]{:S(2)}, u32[]{:S(2)}) collective-permute-start(bf16[512,768]{1,0:T(8,128)(2,1)S(1)} %get-tuple-element.113), channel_id=1, source_target_pairs={{0,2},{1,3},{2,0},{3,1},{4,6},{5,7},{6,4},{7,5}} | collective-permute-start | bytes 2359304 | tf_op jit(solution)/shard_map/ppermute | solution.py:317
  78.1 2.8 %collective-permute-start.12 = (bf16[512,768]{1,0:T(8,128)(2,1)S(1)}, bf16[512,768]{1,0:T(8,128)(2,1)S(1)}, u32[]{:S(2)}, u32[]{:S(2)}) collective-permute-start(bf16[512,768]{1,0:T(8,128)(2,1)S(1)} %collective-permute-done.7.refs_4_), channel_id=1, source_target_pairs={{0,1},{1,0},{2,3},{3,2},{4,5},{5,4},{6,7},{7,6}} | collective-permute-start | bytes 2359304 | tf_op jit(solution)/shard_map/ppermute | solution.py:329
  79.0 10.7 %collective-permute-start.6 = (bf16[256,768]{1,0:T(8,128)(2,1)S(1)}, bf16[256,768]{1,0:T(8,128)(2,1)S(1)}, u32[]{:S(2)}, u32[]{:S(2)}) collective-permute-start(bf16[256,768]{1,0:T(8,128)(2,1)S(1)} %slice.20), channel_id=1, source_target_pairs={{0,2},{1,3},{2,0},{3,1},{4,6},{5,7},{6,4},{7,5}} | collective-permute-start | bytes 1179656 | tf_op jit(solution)/shard_map/ppermute | solution.py:317
  89.7 2.2 %collective-permute-start.13 = (bf16[256,768]{1,0:T(8,128)(2,1)S(1)}, bf16[256,768]{1,0:T(8,128)(2,1)S(1)}, u32[]{:S(2)}, u32[]{:S(2)}) collective-permute-start(bf16[256,768]{1,0:T(8,128)(2,1)S(1)} %collective-permute-done.6.refs_4_), channel_id=1, source_target_pairs={{0,1},{1,0},{2,3},{3,2},{4,5},{5,4},{6,7},{7,6}} | collective-permute-start | bytes 1179656 | tf_op jit(solution)/shard_map/ppermute | solution.py:329
  90.6 6.5 %collective-permute-start.5 = (bf16[128,768]{1,0:T(8,128)(2,1)S(1)}, bf16[128,768]{1,0:T(8,128)(2,1)S(1)}, u32[]{:S(2)}, u32[]{:S(2)}) collective-permute-start(bf16[128,768]{1,0:T(8,128)(2,1)S(1)} %get-tuple-element.114), channel_id=1, source_target_pairs={{0,2},{1,3},{2,0},{3,1},{4,6},{5,7},{6,4},{7,5}} | collective-permute-start | bytes 589832 | tf_op jit(solution)/shard_map/ppermute | solution.py:317
  97.1 1.9 %collective-permute-start.14 = (bf16[128,768]{1,0:T(8,128)(2,1)S(1)}, bf16[128,768]{1,0:T(8,128)(2,1)S(1)}, u32[]{:S(2)}, u32[]{:S(2)}) collective-permute-start(bf16[128,768]{1,0:T(8,128)(2,1)S(1)} %collective-permute-done.5.cols_a), channel_id=1, source_target_pairs={{0,1},{1,0},{2,3},{3,2},{4,5},{5,4},{6,7},{7,6}} | collective-permute-start | bytes 589832 | tf_op jit(solution)/shard_map/ppermute | solution.py:329
  97.9 6.5 %collective-permute-start = (bf16[128,768]{1,0:T(8,128)(2,1)S(1)}, bf16[128,768]{1,0:T(8,128)(2,1)S(1)}, u32[]{:S(2)}, u32[]{:S(2)}) collective-permute-start(bf16[128,768]{1,0:T(8,128)(2,1)S(1)} %get-tuple-element.115), channel_id=1, source_target_pairs={{0,2},{1,3},{2,0},{3,1},{4,6},{5,7},{6,4},{7,5}} | collective-permute-start | bytes 589832 | tf_op jit(solution)/shard_map/ppermute | solution.py:317
  104.4 2.4 %collective-permute-start.15 = (bf16[128,768]{1,0:T(8,128)(2,1)S(1)}, bf16[128,768]{1,0:T(8,128)(2,1)S(1)}, u32[]{:S(2)}, u32[]{:S(2)}) collective-permute-start(bf16[128,768]{1,0:T(8,128)(2,1)S(1)} %collective-permute-done.refs_3_.cols_a), channel_id=1, source_target_pairs={{0,1},{1,0},{2,3},{3,2},{4,5},{5,4},{6,7},{7,6}} | collective-permute-start | bytes 589832 | tf_op jit(solution)/shard_map/ppermute | solution.py:329
  108.3 5.3 %collective-permute-start.16 = (f32[8,128]{1,0:T(8,128)S(1)}, f32[8,128]{1,0:T(8,128)S(1)}, u32[]{:S(2)}, u32[]{:S(2)}) collective-permute-start(f32[8,128]{1,0:T(8,128)S(1)} %get-tuple-element.111), channel_id=1, source_target_pairs={{0,2},{1,3},{2,0},{3,1},{4,6},{5,7},{6,4},{7,5}} | collective-permute-start | bytes 12296 | tf_op jit(solution)/shard_map/ppermute | solution.py:342
  108.4 5.3 %collective-permute-start.17 = (f32[8,128]{1,0:T(8,128)S(1)}, f32[8,128]{1,0:T(8,128)S(1)}, u32[]{:S(2)}, u32[]{:S(2)}) collective-permute-start(f32[8,128]{1,0:T(8,128)S(1)} %get-tuple-element.111), channel_id=1, source_target_pairs={{0,1},{1,0},{2,3},{3,2},{4,5},{5,4},{6,7},{7,6}} | collective-permute-start | bytes 12296 | tf_op jit(solution)/shard_map/ppermute | solution.py:342
  108.6 5.0 %collective-permute-start.18 = (f32[8,128]{1,0:T(8,128)S(1)}, f32[8,128]{1,0:T(8,128)S(1)}, u32[]{:S(2)}, u32[]{:S(2)}) collective-permute-start(f32[8,128]{1,0:T(8,128)S(1)} %get-tuple-element.111), channel_id=1, source_target_pairs={{0,3},{1,2},{2,1},{3,0},{4,7},{5,6},{6,5},{7,4}} | collective-permute-start | bytes 12296 | tf_op jit(solution)/shard_map/ppermute | solution.py:342

commit v5 on v3

v5 whole, which is shorter than its diff:
```python
import functools

import jax
import jax.numpy as jnp
from jax import lax
from jax.experimental import pallas as pl
from jax.experimental.pallas import tpu as pltpu
from jax.sharding import PartitionSpec as P


CHUNK = 128
SUB_ROWS = 512
LOG2E = 1.4426950408889634
F32 = jnp.float32
VMEM_SPEC = pl.BlockSpec(memory_space=pltpu.VMEM)
HBM_SPEC = pl.BlockSpec(memory_space=pl.ANY)
FINISH_TILE = 256


def count_of(info_ref):
    return jnp.max(info_ref[info_ref.shape[0] - 8:, :]).astype(jnp.int32)


def live_tiles(info_ref):
    return (count_of(info_ref) + FINISH_TILE - 1) // FINISH_TILE


def prep_kernel(kappa, raw_hbm, q_hbm, count_ref, xv, rowv, info, forces, zeros, q_ref, sem, in_sems):
    rows = raw_hbm.shape[0]
    chunks = rows // CHUNK
    eye = lax.broadcasted_iota(jnp.int32, (CHUNK, CHUNK), 0) == lax.broadcasted_iota(jnp.int32, (CHUNK, CHUNK), 1)
    lane = lax.broadcasted_iota(jnp.int32, (1, CHUNK), 1)
    count = count_ref[0]
    group = rows // 4
    charge_copy = pltpu.make_async_copy(q_hbm, q_ref, in_sems.at[4])
    charge_copy.start()

    def fetch(g):
        return pltpu.make_async_copy(raw_hbm.at[pl.ds(g * group, group)], xv.at[pl.ds(g * group, group)], in_sems.at[g])

    for g in range(4):
        fetch(g).start()
    tiles = rows // FINISH_TILE
    live = (count + FINISH_TILE - 1) // FINISH_TILE
    zeros[...] = jnp.zeros_like(zeros)

    def blank(i):
        return pltpu.make_async_copy(zeros, forces.at[pl.ds(pl.multiple_of(i * FINISH_TILE, FINISH_TILE), FINISH_TILE)], sem)

    def start(i, _):
        blank(i).start()
        return 0

    lax.fori_loop(live, tiles, start, 0)
    info[2 * chunks:, :] = jnp.full((8, CHUNK), count, jnp.int32).astype(F32)

    def one(c, _):
        sl = pl.ds(pl.multiple_of(c * CHUNK, CHUNK), CHUNK)
        row_ids = lax.broadcasted_iota(jnp.int32, (CHUNK, 1), 0) + c * CHUNK
        block = jnp.where(row_ids < count, xv[sl, :].astype(F32), 0.0)
        xv[sl, :] = block.astype(xv.dtype)
        col_s = -kappa * jnp.sum(block * block, axis=1, keepdims=True)
        rowv[0, sl, :] = jnp.broadcast_to(col_s, (CHUNK, CHUNK))
        info[pl.ds(c, 1), :] = jnp.sum(jnp.where(eye, col_s, 0.0), axis=0, keepdims=True)
        live = jnp.where(lane + c * CHUNK < count, q_ref[pl.ds(c, 1), :], 0.0)
        info[pl.ds(chunks + c, 1), :] = live
        rowv[1, sl, :] = jnp.broadcast_to(jnp.sum(jnp.where(eye, live, 0.0), axis=1, keepdims=True), (CHUNK, CHUNK))
        return 0

    charge_copy.wait()
    for g in range(4):
        fetch(g).wait()
        lax.fori_loop(g * chunks // 4, (g + 1) * chunks // 4, one, 0)

    def wait(i, _):
        blank(i).wait()
        return 0

    lax.fori_loop(live, tiles, wait, 0)


def prep(x, charges, counts):
    rows, width = x.shape
    chunks = rows // CHUNK
    return pl.pallas_call(
        functools.partial(prep_kernel, LOG2E * 0.5 / width),
        out_shape=[jax.ShapeDtypeStruct(x.shape, x.dtype), pltpu.VMEM((2, rows, CHUNK), F32),
                   jax.ShapeDtypeStruct((2 * chunks + 8, CHUNK), F32), jax.ShapeDtypeStruct((rows, width), F32)],
        in_specs=[pl.BlockSpec(memory_space=pltpu.HBM)] * 2 + [pl.BlockSpec(memory_space=pltpu.SMEM)], out_specs=[VMEM_SPEC] * 3 + [HBM_SPEC],
        scratch_shapes=[pltpu.VMEM((FINISH_TILE, width), F32), pltpu.VMEM((chunks, CHUNK), F32), pltpu.SemaphoreType.DMA,
                        pltpu.SemaphoreType.DMA((5,))],
        compiler_params=pltpu.CompilerParams(vmem_limit_bytes=VMEM_LIMIT),
        name='prep')(x, charges.reshape(chunks, CHUNK), counts)


def weights(kappa, gram, row_a, row_c, col_a, col_c):
    expo = jnp.minimum(gram * (2.0 * kappa) + row_a + col_a, 0.0)
    return jnp.exp2(expo) * (row_c * col_c)


def step_kernel(cfg, *refs):
    start, num, tile_chunks, first, diag, kappa = cfg
    refs = list(refs)
    xv, rowv, my_info = refs[:3]
    refs = refs[3:]
    cols, src_info = xv, my_info
    if not diag:
        src_info, cols = refs[:2]
        refs = refs[2:]
    if not first:
        refs = refs[2:]
    tv, sv = refs[:2]
    rows, _ = xv.shape
    block_chunks = rows // CHUNK
    col_tile = tile_chunks * CHUNK
    live = jnp.clip((count_of(src_info) + CHUNK - 1) // CHUNK - start, 0, num)
    tiles = (live + tile_chunks - 1) // tile_chunks

    def old(ref, ct, rsl):
        return jnp.where(ct == 0, 0.0, ref[rsl, :]) if first else ref[rsl, :]

    def weigh(ct, c0, r0):
        rsl = pl.ds(r0, SUB_ROWS)
        s_sum = old(sv, ct, rsl)
        row_a = rowv[0, rsl, :]
        row_c = rowv[1, rsl, :]
        parts = []
        for q in range(tile_chunks // 2):
            gram = lax.dot_general(xv[rsl, :], cols[pl.ds(c0 + q * 256, 256), :], (((1,), (1,)), ((), ())),
                                   preferred_element_type=F32)
            for h in range(2):
                k = 2 * q + h
                cid = start + ct * tile_chunks + k
                col_a = src_info[pl.ds(cid, 1), :]
                col_c = src_info[pl.ds(block_chunks + cid, 1), :]
                w = weights(kappa, gram[:, h * 128:(h + 1) * 128], row_a, row_c, col_a, col_c)
                if diag:
                    delta = lax.broadcasted_iota(jnp.int32, w.shape, 0) - lax.broadcasted_iota(jnp.int32, w.shape, 1)
                    w = jnp.where(delta == c0 + k * CHUNK - r0, 0.0, w)
                s_sum = s_sum + w
                parts.append(w.astype(jnp.bfloat16))
        sv[rsl, :] = s_sum
        return jnp.concatenate(parts, axis=1)

    def pull(w, ct, c0, r0):
        rsl = pl.ds(r0, SUB_ROWS)
        tv[rsl, :] = old(tv, ct, rsl) + jnp.dot(w, cols[pl.ds(c0, col_tile), :], preferred_element_type=F32)

    def tile(ct, _):
        c0 = pl.multiple_of(ct * col_tile, col_tile)
        w = None
        for r0 in range(0, rows, SUB_ROWS):
            w_next = weigh(ct, c0, r0)
            if w is not None:
                pull(w, ct, c0, r0 - SUB_ROWS)
            w = w_next
        pull(w, ct, c0, rows - SUB_ROWS)
        return 0

    lax.fori_loop(0, tiles, tile, 0)


def last_kernel(cfg, xv, rowv, src_info, cols, s_in, sv, wv, part):
    start, num, kappa = cfg
    block_chunks = xv.shape[0] // CHUNK

    def row_tile(rt, acc):
        rsl = pl.ds(pl.multiple_of(rt * SUB_ROWS, SUB_ROWS), SUB_ROWS)
        gram = lax.dot_general(xv[rsl, :], cols[...], (((1,), (1,)), ((), ())), preferred_element_type=F32)
        sums = sv[rsl, :]
        for k in range(num):
            w = weights(kappa, gram[:, k * CHUNK:(k + 1) * CHUNK], rowv[0, rsl, :], rowv[1, rsl, :],
                        src_info[start + k:start + k + 1, :], src_info[block_chunks + start + k:block_chunks + start + k + 1, :])
            sums = sums + w
            wv[rsl, k * CHUNK:(k + 1) * CHUNK] = w.astype(jnp.bfloat16)
        sv[rsl, :] = sums
        for g in range(SUB_ROWS // 8):
            acc = acc + sums[g * 8:(g + 1) * 8]
        return acc

    part[...] = lax.fori_loop(0, xv.shape[0] // SUB_ROWS, row_tile, jnp.zeros((8, 128), F32))


def last_step(x, rowf, src_info, cols, start, s_sum):
    rows, width = x.shape
    num = cols.shape[0] // CHUNK
    ins = [x, rowf, src_info, cols, s_sum]
    return pl.pallas_call(
        functools.partial(last_kernel, (start, num, LOG2E * 0.5 / width)),
        out_shape=[pltpu.VMEM((rows, 128), F32), pltpu.VMEM((rows, num * CHUNK), jnp.bfloat16), jax.ShapeDtypeStruct((8, 128), F32)],
        in_specs=[VMEM_SPEC] * len(ins), out_specs=[VMEM_SPEC] * 3,
        input_output_aliases={4: 0},
        compiler_params=pltpu.CompilerParams(vmem_limit_bytes=VMEM_LIMIT),
        cost_estimate=pl.CostEstimate(flops=2 * rows * num * CHUNK * width, bytes_accessed=rows * width, transcendentals=0),
        name='last')(*ins)


def finish_kernel(inv_len2, xv, tv, sv, wv, cols, my_info, blank, forces, buf, out_sems):
    del blank
    num = live_tiles(my_info)

    def out(i):
        return pltpu.make_async_copy(
            buf.at[lax.rem(i, 4)], forces.at[pl.ds(pl.multiple_of(i * FINISH_TILE, FINISH_TILE), FINISH_TILE)], out_sems.at[lax.rem(i, 4)])

    def one(i, _):
        @pl.when(i >= 4)
        def _():
            out(i - 4).wait()

        sl = pl.ds(pl.multiple_of(i * FINISH_TILE, FINISH_TILE), FINISH_TILE)
        total = jnp.sum(sv[sl, :], axis=1, keepdims=True)
        pulled = tv[sl, :] + jnp.dot(wv[sl, :], cols[...], preferred_element_type=F32)
        buf[lax.rem(i, 4)] = (total * xv[sl, :].astype(F32) - pulled) * inv_len2
        out(i).start()
        return 0

    lax.fori_loop(0, num, one, 0)

    def drain(i, _):
        out(i).wait()
        return 0

    lax.fori_loop(jnp.maximum(num - 4, 0), num, drain, 0)


def finish(*ins):
    x = ins[0]
    rows, width = x.shape
    return pl.pallas_call(
        functools.partial(finish_kernel, 1.0 / width),
        out_shape=jax.ShapeDtypeStruct((rows, width), F32),
        in_specs=[VMEM_SPEC] * (len(ins) - 1) + [HBM_SPEC], out_specs=HBM_SPEC,
        scratch_shapes=[pltpu.VMEM((4, FINISH_TILE, width), F32), pltpu.SemaphoreType.DMA((4,))],
        input_output_aliases={len(ins) - 1: 0},
        compiler_params=pltpu.CompilerParams(vmem_limit_bytes=VMEM_LIMIT),
        cost_estimate=pl.CostEstimate(flops=rows * width * 1000, bytes_accessed=rows * width * 4, transcendentals=0),
        name='finish')(*ins)


VMEM_LIMIT = 24 * 1024 * 1024


def step(x, rowf, my_info, src_info, cols, start, num, tile_chunks, carry):
    rows, width = x.shape
    first, diag = carry is None, cols is None
    cfg = (start, num, tile_chunks, first, diag, LOG2E * 0.5 / width)
    ins = [x, rowf, my_info] + ([] if diag else [src_info, cols]) + ([] if first else list(carry))
    in_specs = [VMEM_SPEC] * len(ins)
    flops = int(4 * rows * num * CHUNK * width * 0.6)
    common = dict(
        in_specs=in_specs,
        compiler_params=pltpu.CompilerParams(vmem_limit_bytes=VMEM_LIMIT),
        cost_estimate=pl.CostEstimate(flops=flops, bytes_accessed=rows * width, transcendentals=0),
        name='step_%d_%d' % (start, num))
    kernel = functools.partial(step_kernel, cfg)
    return pl.pallas_call(
        kernel,
        out_shape=[pltpu.VMEM((rows, width), F32), pltpu.VMEM((rows, 128), F32)],
        out_specs=[VMEM_SPEC] * 2,
        input_output_aliases={} if first else {len(ins) - 2: 0, len(ins) - 1: 1}, **common)(*ins)


PIECES = (512, 512, 512, 256, 256)


def solution(mesh):
    num_blocks = mesh.shape['row']
    cross_perm = [(src, src ^ 2) for src in range(num_blocks)]
    pair_perm = [(src, src ^ 1) for src in range(num_blocks)]
    diag_perm = [(src, src ^ 3) for src in range(num_blocks)]

    def per_device(positions, charges, counts):
        rows, _ = positions.shape
        chunks = rows // CHUNK
        head = jnp.where(jnp.arange(PIECES[0])[:, None] < counts[0], positions[:PIECES[0]], 0)
        arrived = [lax.ppermute(head, 'row', cross_perm)]
        x, rowf, info, blank = prep(positions, charges, counts)
        info_cross = lax.ppermute(info, 'row', cross_perm)
        info_pair = lax.ppermute(info, 'row', pair_perm)
        off = PIECES[0]
        for size in PIECES[1:]:
            arrived.append(lax.ppermute(x[off:off + size], 'row', cross_perm))
            off += size
        partner = lax.ppermute(x, 'row', pair_perm)
        carry = step(x, rowf, info, None, None, 0, chunks, 4, None)
        partner, *carry = lax.optimization_barrier((partner, *carry))
        carry = step(x, rowf, info, info_pair, partner, 0, chunks, 4, carry)
        info_cross, *carry = lax.optimization_barrier((info_cross, *carry))
        info_diag = lax.ppermute(info_cross, 'row', pair_perm)
        off = 0
        for k, piece in enumerate(arrived):
            num = PIECES[k] // CHUNK
            piece, *carry = lax.optimization_barrier((piece, *carry))
            relay = lax.ppermute(piece, 'row', pair_perm)
            carry = step(x, rowf, info, info_cross, piece, off, num, min(4, num), carry)
            if k < len(PIECES) - 1:
                carry = step(x, rowf, info, info_diag, relay, off, num, min(4, num), carry)
            else:
                t_sum, s_sum = carry
                s_sum, w_last, part = last_step(x, rowf, info_diag, relay, off, s_sum)
            off += num
        total = part
        for perm in (cross_perm, pair_perm, diag_perm):
            total = total + lax.ppermute(part, 'row', perm)
        forces = finish(x, t_sum, s_sum, w_last, relay, info, blank)
        return forces, (0.5 * jnp.sum(total)).reshape(1)

    row_spec = P(('sys', 'row'), None)
    vec_spec = P(('sys', 'row'))
    return jax.shard_map(per_device, mesh=mesh, in_specs=(row_spec, vec_spec, vec_spec), out_specs=(row_spec, P('sys')), check_vma=False)
```

time: 109 us -> 114 us (1.046)
  waiting for transfers between devices: 36.3 us -> 41.7 us
    ppermute x5, waiting for transfers between devices: 31.2 us -> 36 us  [the longest x4 36 us: per_device(): arrived.append(lax.ppermute(x[off:off + size], 'row', cross_perm))]
    pallas_call x10 -> x11, Pallas kernels: 45.7 us -> 47.9 us  [step(): pl.pallas_call(kernel, out_shape=[pltpu.VMEM((rows, width), F32), pltpu.V...]
    pallas_call x2 -> x1, Pallas kernels: 3.66 us -> 1.84 us  [last_step(): pl.pallas_call(functools.partial(last_kernel, (start, num, LOG2E * 0.5 /...]
    ppermute x5, starting transfers between devices: 1.96 us -> 0.79 us  [the longest x1 0.72 us: per_device(): partner = lax.ppermute(x, 'row', pair_perm)]
  transfers between devices with their start and end apart: 17 -> 17, of which waited for: 6 -> 8; matrix products, arithmetic and copies ran while one was open for 0% -> 0% of each run, Pallas kernels for 49% -> 45%
where the time goes in v5:
time: 114 us; the launch traced here: 113 us
  Pallas kernels  56 us (49%)
  waiting for transfers between devices  41.7 us (37%)
  starting transfers between devices  9.05 us (8%)
  between operations  3.29 us (3%)
  local copies, waits for them, and re-layouts  2.73 us (2%)
    pallas_call x11, Pallas kernels, step(): pl.pallas_call(kernel, out_shape=[pltpu.VMEM((rows, width), F32), pltpu.V...  47.9 us
    ppermute x4, waiting for transfers between devices, per_device(): arrived.append(lax.ppermute(x[off:off + size], 'row', cross_perm))  36 us
    ppermute x5, waiting for transfers between devices, per_device(): relay = lax.ppermute(piece, 'row', pair_perm)  5.63 us
    ppermute x5, starting transfers between devices, per_device(): relay = lax.ppermute(piece, 'row', pair_perm)  4.01 us
    pallas_call x1, Pallas kernels, finish(): pl.pallas_call(functools.partial(finish_kernel, 1.0 / width), out_shape=j...  3.4 us
    pallas_call x1, Pallas kernels, prep(): pl.pallas_call(functools.partial(prep_kernel, LOG2E * 0.5 / width), out_s...  2.87 us
    ppermute x3, starting transfers between devices, per_device(): total = total + lax.ppermute(part, 'row', perm)  2.69 us
    unnamed x4, local copies, waits for them, and re-layouts  2.58 us
  transfers between devices with their start and end apart: 17, of which 8 were waited for; matrix products, arithmetic and copies ran while one was open for 0% of the time, Pallas kernels for 45%

profile of v5, /device:TPU:5, one launch (start us, length us, event | category | flops | bytes accessed | tf_op | source)
XLA Modules:
  0.0 113.5 jit_solution(10913393580064831107)
XLA Ops:
  1.3 1.9 %copy-done = bf16[2048,768]{1,0:T(8,128)(2,1)S(1)} copy-done((bf16[2048,768]{1,0:T(8,128)(2,1)S(1)}, bf16[2048,768]{1,0:T(8,128)(2,1)}, u32[]{:S(2)}) %copy-start) | copy-done | bytes 3145752
  3.2 0.7 copy-done.1
  3.9 2.9 %prep.1 = (bf16[2048,768]{1,0:T(8,128)(2,1)S(1)}, f32[2,2048,128]{2,1,0:T(8,128)S(1)}, f32[40,128]{1,0:T(8,128)S(1)}, f32[2048,768]{1,0:T(8,128)}) custom-call(bf16[2048,768]{1,0:T(8,128)(2,1)S(1)} %copy-done, f32[16,128]{1,0:T(8,128)S(1)} %bitcast.4, s32[1]{0:T(128)} %copy.49.count_ref), custom_call_target="tpu_custom_call" | custom-call | tf_op jit(solution)/shard_map/prep/pallas_call | solution.py:85
  6.7 0.7 collective-permute-start.2
  7.5 0.0 collective-permute-start.1
  7.5 1.2 %collective-permute-start = (f32[40,128]{1,0:T(8,128)S(1)}, f32[40,128]{1,0:T(8,128)S(1)}, u32[]{:S(2)}, u32[]{:S(2)}) collective-permute-start(f32[40,128]{1,0:T(8,128)S(1)} %get-tuple-element.54.refs_2_.my_info), channel_id=1, source_target_pairs={{0,2},{1,3},{2,0},{3,1},{4,6},{5,7},{6,4},{7,5}} | collective-permute-start | bytes 61448 | tf_op jit(solution)/shard_map/ppermute | solution.py:279
  8.7 0.1 slice_select_fusion
  8.8 0.3 collective-permute-start.8
  9.1 17.3 %step_0_16.2 = (f32[2048,768]{1,0:T(8,128)S(1)}, f32[2048,128]{1,0:T(8,128)S(1)}) custom-call(bf16[2048,768]{1,0:T(8,128)(2,1)S(1)} %get-tuple-element.52.refs_0_.xv, f32[2,2048,128]{2,1,0:T(8,128)S(1)} %get-tuple-element.53.refs_1_.rowv, f32[40,128]{1,0:T(8,128)S(1)} %get-tuple-element.54.refs_2_.my_info), custom_call_target="tpu_custom_call" | custom-call | flops 7730940928 | bytes 1572864 | tf_op jit(solution)/shard_map/step_0_16/pallas_call | solution.py:257
  26.4 0.0 collective-permute-done.2.refs_4_
  26.4 0.0 collective-permute-done.1.refs_3_
  26.4 11.6 %step_0_16.3 = (f32[2048,768]{1,0:T(8,128)S(1)}, f32[2048,128]{1,0:T(8,128)S(1)}) custom-call(bf16[2048,768]{1,0:T(8,128)(2,1)S(1)} %get-tuple-element.52.refs_0_.xv, f32[2,2048,128]{2,1,0:T(8,128)S(1)} %get-tuple-element.53.refs_1_.rowv, f32[40,128]{1,0:T(8,128)S(1)} %get-tuple-element.54.refs_2_.my_info, ...), custom_call_target="tpu_custom_call", output_to_operand_aliasing={{0}: (5, {}), {1}: (6, {})} | custom-call | flops 7730940928 | bytes 1572864 | tf_op jit(solution)/shard_map/step_0_16/pallas_call | solution.py:257
  38.0 0.0 collective-permute-done.8.refs_4_
  38.0 0.5 collective-permute-start.9
  38.6 0.1 fusion
  38.7 0.0 collective-permute-start.7
  38.7 0.0 collective-permute-start.4
  38.8 3.9 %step_0_4.2 = (f32[2048,768]{1,0:T(8,128)S(1)}, f32[2048,128]{1,0:T(8,128)S(1)}) custom-call(bf16[2048,768]{1,0:T(8,128)(2,1)S(1)} %get-tuple-element.52.refs_0_.xv, f32[2,2048,128]{2,1,0:T(8,128)S(1)} %get-tuple-element.53.refs_1_.rowv, f32[40,128]{1,0:T(8,128)S(1)} %get-tuple-element.54.refs_2_.my_info, ...), custom_call_target="tpu_custom_call", output_to_operand_aliasing={{0}: (5, {}), {1}: (6, {})} | custom-call | flops 1932735232 | bytes 1572864 | tf_op jit(solution)/shard_map/step_0_4/pallas_call | solution.py:257
  42.7 4.1 %step_0_4.3 = (f32[2048,768]{1,0:T(8,128)S(1)}, f32[2048,128]{1,0:T(8,128)S(1)}) custom-call(bf16[2048,768]{1,0:T(8,128)(2,1)S(1)} %get-tuple-element.52.refs_0_.xv, f32[2,2048,128]{2,1,0:T(8,128)S(1)} %get-tuple-element.53.refs_1_.rowv, f32[40,128]{1,0:T(8,128)S(1)} %get-tuple-element.54.refs_2_.my_info, ...), custom_call_target="tpu_custom_call", output_to_operand_aliasing={{0}: (5, {}), {1}: (6, {})} | custom-call | flops 1932735232 | bytes 1572864 | tf_op jit(solution)/shard_map/step_0_4/pallas_call | solution.py:257
  46.9 10.9 %collective-permute-done.7.refs_4_ = bf16[512,768]{1,0:T(8,128)(2,1)S(1)} collective-permute-done((bf16[512,768]{1,0:T(8,128)(2,1)S(1)}, bf16[512,768]{1,0:T(8,128)(2,1)S(1)}, u32[]{:S(2)}, u32[]{:S(2)}) %collective-permute-start.7) | collective-permute-done | bytes 786464 | tf_op jit(solution)/shard_map/ppermute | solution.py:283
  57.8 0.9 collective-permute-start.10
  58.7 0.0 collective-permute-start.6
  58.7 0.1 step_4_4.2
  58.8 1.8 %collective-permute-done.10.refs_4_ = bf16[512,768]{1,0:T(8,128)(2,1)S(1)} collective-permute-done((bf16[512,768]{1,0:T(8,128)(2,1)S(1)}, bf16[512,768]{1,0:T(8,128)(2,1)S(1)}, u32[]{:S(2)}, u32[]{:S(2)}) %collective-permute-start.10) | collective-permute-done | bytes 786464 | tf_op jit(solution)/shard_map/ppermute | solution.py:295
  60.6 3.9 %step_4_4.3 = (f32[2048,768]{1,0:T(8,128)S(1)}, f32[2048,128]{1,0:T(8,128)S(1)}) custom-call(bf16[2048,768]{1,0:T(8,128)(2,1)S(1)} %get-tuple-element.52.refs_0_.xv, f32[2,2048,128]{2,1,0:T(8,128)S(1)} %get-tuple-element.53.refs_1_.rowv, f32[40,128]{1,0:T(8,128)S(1)} %get-tuple-element.54.refs_2_.my_info, ...), custom_call_target="tpu_custom_call", output_to_operand_aliasing={{0}: (5, {}), {1}: (6, {})} | custom-call | flops 1932735232 | bytes 1572864 | tf_op jit(solution)/shard_map/step_4_4/pallas_call | solution.py:257
  64.5 13.2 %collective-permute-done.6.refs_4_ = bf16[512,768]{1,0:T(8,128)(2,1)S(1)} collective-permute-done((bf16[512,768]{1,0:T(8,128)(2,1)S(1)}, bf16[512,768]{1,0:T(8,128)(2,1)S(1)}, u32[]{:S(2)}, u32[]{:S(2)}) %collective-permute-start.6) | collective-permute-done | bytes 786464 | tf_op jit(solution)/shard_map/ppermute | solution.py:283
  77.8 0.9 collective-permute-start.11
  78.6 0.1 fusion.1
  78.7 0.0 collective-permute-start.5
  78.7 0.4 step_8_4.2
  79.1 1.5 %collective-permute-done.11.refs_4_ = bf16[512,768]{1,0:T(8,128)(2,1)S(1)} collective-permute-done((bf16[512,768]{1,0:T(8,128)(2,1)S(1)}, bf16[512,768]{1,0:T(8,128)(2,1)S(1)}, u32[]{:S(2)}, u32[]{:S(2)}) %collective-permute-start.11) | collective-permute-done | bytes 786464 | tf_op jit(solution)/shard_map/ppermute | solution.py:295
  80.5 3.9 %step_8_4.3 = (f32[2048,768]{1,0:T(8,128)S(1)}, f32[2048,128]{1,0:T(8,128)S(1)}) custom-call(bf16[2048,768]{1,0:T(8,128)(2,1)S(1)} %get-tuple-element.52.refs_0_.xv, f32[2,2048,128]{2,1,0:T(8,128)S(1)} %get-tuple-element.53.refs_1_.rowv, f32[40,128]{1,0:T(8,128)S(1)} %get-tuple-element.54.refs_2_.my_info, ...), custom_call_target="tpu_custom_call", output_to_operand_aliasing={{0}: (5, {}), {1}: (6, {})} | custom-call | flops 1932735232 | bytes 1572864 | tf_op jit(solution)/shard_map/step_8_4/pallas_call | solution.py:257
  84.5 4.9 %collective-permute-done.5.refs_4_ = bf16[256,768]{1,0:T(8,128)(2,1)S(1)} collective-permute-done((bf16[256,768]{1,0:T(8,128)(2,1)S(1)}, bf16[256,768]{1,0:T(8,128)(2,1)S(1)}, u32[]{:S(2)}, u32[]{:S(2)}) %collective-permute-start.5) | collective-permute-done | bytes 393248 | tf_op jit(solution)/shard_map/ppermute | solution.py:283
  89.4 0.9 collective-permute-start.12
  90.2 0.0 collective-permute-start.3
  90.2 0.1 step_12_2.2
  90.4 1.2 %collective-permute-done.12.refs_4_ = bf16[256,768]{1,0:T(8,128)(2,1)S(1)} collective-permute-done((bf16[256,768]{1,0:T(8,128)(2,1)S(1)}, bf16[256,768]{1,0:T(8,128)(2,1)S(1)}, u32[]{:S(2)}, u32[]{:S(2)}) %collective-permute-start.12) | collective-permute-done | bytes 393248 | tf_op jit(solution)/shard_map/ppermute | solution.py:295
  91.6 2.3 %step_12_2.3 = (f32[2048,768]{1,0:T(8,128)S(1)}, f32[2048,128]{1,0:T(8,128)S(1)}) custom-call(bf16[2048,768]{1,0:T(8,128)(2,1)S(1)} %get-tuple-element.52.refs_0_.xv, f32[2,2048,128]{2,1,0:T(8,128)S(1)} %get-tuple-element.53.refs_1_.rowv, f32[40,128]{1,0:T(8,128)S(1)} %get-tuple-element.54.refs_2_.my_info, ...), custom_call_target="tpu_custom_call", output_to_operand_aliasing={{0}: (5, {}), {1}: (6, {})} | custom-call | flops 966367616 | bytes 1572864 | tf_op jit(solution)/shard_map/step_12_2/pallas_call | solution.py:257
  93.9 7.0 %collective-permute-done.3.refs_4_ = bf16[256,768]{1,0:T(8,128)(2,1)S(1)} collective-permute-done((bf16[256,768]{1,0:T(8,128)(2,1)S(1)}, bf16[256,768]{1,0:T(8,128)(2,1)S(1)}, u32[]{:S(2)}, u32[]{:S(2)}) %collective-permute-start.3) | collective-permute-done | bytes 393248 | tf_op jit(solution)/shard_map/ppermute | solution.py:283
  100.9 0.9 collective-permute-start.13
  101.8 0.1 step_14_2.1
  101.9 1.2 %collective-permute-done.13.cols = bf16[256,768]{1,0:T(8,128)(2,1)S(1)} collective-permute-done((bf16[256,768]{1,0:T(8,128)(2,1)S(1)}, bf16[256,768]{1,0:T(8,128)(2,1)S(1)}, u32[]{:S(2)}, u32[]{:S(2)}) %collective-permute-start.13) | collective-permute-done | bytes 393248 | tf_op jit(solution)/shard_map/ppermute | solution.py:295
  103.1 1.8 %last.1 = (f32[2048,128]{1,0:T(8,128)S(1)}, bf16[2048,256]{1,0:T(8,128)(2,1)S(1)}, f32[8,128]{1,0:T(8,128)S(1)}) custom-call(bf16[2048,768]{1,0:T(8,128)(2,1)S(1)} %get-tuple-element.52.refs_0_.xv, f32[2,2048,128]{2,1,0:T(8,128)S(1)} %get-tuple-element.53.refs_1_.rowv, ...), custom_call_target="tpu_custom_call", output_to_operand_aliasing={{0}: (4, {})} | custom-call | flops 805306368 | bytes 1572864 | tf_op jit(solution)/shard_map/last/pallas_call | solution.py:188
  105.0 1.0 collective-permute-start.14
  106.0 0.0 collective-permute-start.15
  106.1 1.6 %collective-permute-start.16 = (f32[8,128]{1,0:T(8,128)S(1)}, f32[8,128]{1,0:T(8,128)S(1)}, u32[]{:S(2)}, u32[]{:S(2)}) collective-permute-start(f32[8,128]{1,0:T(8,128)S(1)} %get-tuple-element.101), channel_id=1, source_target_pairs={{0,3},{1,2},{2,1},{3,0},{4,7},{5,6},{6,5},{7,4}} | collective-permute-start | bytes 12296 | tf_op jit(solution)/shard_map/ppermute | solution.py:305
  107.7 3.4 %finish.1 = f32[2048,768]{1,0:T(8,128)} custom-call(bf16[2048,768]{1,0:T(8,128)(2,1)S(1)} %get-tuple-element.52.refs_0_.xv, f32[2048,768]{1,0:T(8,128)S(1)} %get-tuple-element.96.tv, f32[2048,128]{1,0:T(8,128)S(1)} %get-tuple-element.98.sv, bf16[2048,256]{1,0:T(8,128)(2,1)S(1)} %get-tuple-element.99.wv, ...), custom_call_target="tpu_custom_call", output_to_operand_aliasing={{}: (6, {})} | custom-call | flops 1572864000 | bytes 6291456 | tf_op jit(solution)/shard_map/finish/pallas_call | solution.py:230
  111.1 0.6 add_reduce_fusion
  (9 shorter events, 0.0 us)
Async XLA Ops:
  1.3 1.9 %copy-start = (bf16[2048,768]{1,0:T(8,128)(2,1)S(1)}, bf16[2048,768]{1,0:T(8,128)(2,1)}, u32[]{:S(2)}) copy-start(bf16[2048,768]{1,0:T(8,128)(2,1)} %raw_hbm.1) | copy-start | bytes 9437188
  3.2 0.7 copy-start.1
  6.7 19.7 %collective-permute-start.2 = (bf16[2048,768]{1,0:T(8,128)(2,1)S(1)}, bf16[2048,768]{1,0:T(8,128)(2,1)S(1)}, u32[]{:S(2)}, u32[]{:S(2)}) collective-permute-start(bf16[2048,768]{1,0:T(8,128)(2,1)S(1)} %get-tuple-element.52.refs_0_.xv), channel_id=1, source_target_pairs={{0,1},{1,0},{2,3},{3,2},{4,5},{5,4},{6,7},{7,6}} | collective-permute-start | bytes 9437192 | tf_op jit(solution)/shard_map/ppermute | solution.py:285
  7.5 19.0 %collective-permute-start.1 = (f32[40,128]{1,0:T(8,128)S(1)}, f32[40,128]{1,0:T(8,128)S(1)}, u32[]{:S(2)}, u32[]{:S(2)}) collective-permute-start(f32[40,128]{1,0:T(8,128)S(1)} %get-tuple-element.54.refs_2_.my_info), channel_id=1, source_target_pairs={{0,1},{1,0},{2,3},{3,2},{4,5},{5,4},{6,7},{7,6}} | collective-permute-start | bytes 61448 | tf_op jit(solution)/shard_map/ppermute | solution.py:280
  7.5 30.5 %collective-permute-start = (f32[40,128]{1,0:T(8,128)S(1)}, f32[40,128]{1,0:T(8,128)S(1)}, u32[]{:S(2)}, u32[]{:S(2)}) collective-permute-start(f32[40,128]{1,0:T(8,128)S(1)} %get-tuple-element.54.refs_2_.my_info), channel_id=1, source_target_pairs={{0,2},{1,3},{2,0},{3,1},{4,6},{5,7},{6,4},{7,5}} | collective-permute-start | bytes 61448 | tf_op jit(solution)/shard_map/ppermute | solution.py:279
  8.8 29.2 %collective-permute-start.8 = (bf16[512,768]{1,0:T(8,128)(2,1)S(1)}, bf16[512,768]{1,0:T(8,128)(2,1)S(1)}, u32[]{:S(2)}, u32[]{:S(2)}) collective-permute-start(bf16[512,768]{1,0:T(8,128)(2,1)S(1)} %slice_select_fusion), channel_id=1, source_target_pairs={{0,2},{1,3},{2,0},{3,1},{4,6},{5,7},{6,4},{7,5}} | collective-permute-start | bytes 2359304 | tf_op jit(solution)/shard_map/ppermute | solution.py:277
  38.0 4.7 %collective-permute-start.9 = (bf16[512,768]{1,0:T(8,128)(2,1)S(1)}, bf16[512,768]{1,0:T(8,128)(2,1)S(1)}, u32[]{:S(2)}, u32[]{:S(2)}) collective-permute-start(bf16[512,768]{1,0:T(8,128)(2,1)S(1)} %collective-permute-done.8.refs_4_), channel_id=1, source_target_pairs={{0,1},{1,0},{2,3},{3,2},{4,5},{5,4},{6,7},{7,6}} | collective-permute-start | bytes 2359304 | tf_op jit(solution)/shard_map/ppermute | solution.py:295
  38.7 19.1 %collective-permute-start.7 = (bf16[512,768]{1,0:T(8,128)(2,1)S(1)}, bf16[512,768]{1,0:T(8,128)(2,1)S(1)}, u32[]{:S(2)}, u32[]{:S(2)}) collective-permute-start(bf16[512,768]{1,0:T(8,128)(2,1)S(1)} %get-tuple-element.102), channel_id=1, source_target_pairs={{0,2},{1,3},{2,0},{3,1},{4,6},{5,7},{6,4},{7,5}} | collective-permute-start | bytes 2359304 | tf_op jit(solution)/shard_map/ppermute | solution.py:283
  38.7 4.0 %collective-permute-start.4 = (f32[40,128]{1,0:T(8,128)S(1)}, f32[40,128]{1,0:T(8,128)S(1)}, u32[]{:S(2)}, u32[]{:S(2)}) collective-permute-start(f32[40,128]{1,0:T(8,128)S(1)} %collective-permute-done.refs_3_), channel_id=1, source_target_pairs={{0,1},{1,0},{2,3},{3,2},{4,5},{5,4},{6,7},{7,6}} | collective-permute-start | bytes 61448 | tf_op jit(solution)/shard_map/ppermute | solution.py:290
  57.8 2.8 %collective-permute-start.10 = (bf16[512,768]{1,0:T(8,128)(2,1)S(1)}, bf16[512,768]{1,0:T(8,128)(2,1)S(1)}, u32[]{:S(2)}, u32[]{:S(2)}) collective-permute-start(bf16[512,768]{1,0:T(8,128)(2,1)S(1)} %collective-permute-done.7.refs_4_), channel_id=1, source_target_pairs={{0,1},{1,0},{2,3},{3,2},{4,5},{5,4},{6,7},{7,6}} | collective-permute-start | bytes 2359304 | tf_op jit(solution)/shard_map/ppermute | solution.py:295
  58.7 19.1 %collective-permute-start.6 = (bf16[512,768]{1,0:T(8,128)(2,1)S(1)}, bf16[512,768]{1,0:T(8,128)(2,1)S(1)}, u32[]{:S(2)}, u32[]{:S(2)}) collective-permute-start(bf16[512,768]{1,0:T(8,128)(2,1)S(1)} %get-tuple-element.103), channel_id=1, source_target_pairs={{0,2},{1,3},{2,0},{3,1},{4,6},{5,7},{6,4},{7,5}} | collective-permute-start | bytes 2359304 | tf_op jit(solution)/shard_map/ppermute | solution.py:283
  77.8 2.8 %collective-permute-start.11 = (bf16[512,768]{1,0:T(8,128)(2,1)S(1)}, bf16[512,768]{1,0:T(8,128)(2,1)S(1)}, u32[]{:S(2)}, u32[]{:S(2)}) collective-permute-start(bf16[512,768]{1,0:T(8,128)(2,1)S(1)} %collective-permute-done.6.refs_4_), channel_id=1, source_target_pairs={{0,1},{1,0},{2,3},{3,2},{4,5},{5,4},{6,7},{7,6}} | collective-permute-start | bytes 2359304 | tf_op jit(solution)/shard_map/ppermute | solution.py:295
  78.7 10.7 %collective-permute-start.5 = (bf16[256,768]{1,0:T(8,128)(2,1)S(1)}, bf16[256,768]{1,0:T(8,128)(2,1)S(1)}, u32[]{:S(2)}, u32[]{:S(2)}) collective-permute-start(bf16[256,768]{1,0:T(8,128)(2,1)S(1)} %get-tuple-element.104), channel_id=1, source_target_pairs={{0,2},{1,3},{2,0},{3,1},{4,6},{5,7},{6,4},{7,5}} | collective-permute-start | bytes 1179656 | tf_op jit(solution)/shard_map/ppermute | solution.py:283
  89.4 2.2 %collective-permute-start.12 = (bf16[256,768]{1,0:T(8,128)(2,1)S(1)}, bf16[256,768]{1,0:T(8,128)(2,1)S(1)}, u32[]{:S(2)}, u32[]{:S(2)}) collective-permute-start(bf16[256,768]{1,0:T(8,128)(2,1)S(1)} %collective-permute-done.5.refs_4_), channel_id=1, source_target_pairs={{0,1},{1,0},{2,3},{3,2},{4,5},{5,4},{6,7},{7,6}} | collective-permute-start | bytes 1179656 | tf_op jit(solution)/shard_map/ppermute | solution.py:295
  90.2 10.7 %collective-permute-start.3 = (bf16[256,768]{1,0:T(8,128)(2,1)S(1)}, bf16[256,768]{1,0:T(8,128)(2,1)S(1)}, u32[]{:S(2)}, u32[]{:S(2)}) collective-permute-start(bf16[256,768]{1,0:T(8,128)(2,1)S(1)} %get-tuple-element.105), channel_id=1, source_target_pairs={{0,2},{1,3},{2,0},{3,1},{4,6},{5,7},{6,4},{7,5}} | collective-permute-start | bytes 1179656 | tf_op jit(solution)/shard_map/ppermute | solution.py:283
  100.9 2.2 %collective-permute-start.13 = (bf16[256,768]{1,0:T(8,128)(2,1)S(1)}, bf16[256,768]{1,0:T(8,128)(2,1)S(1)}, u32[]{:S(2)}, u32[]{:S(2)}) collective-permute-start(bf16[256,768]{1,0:T(8,128)(2,1)S(1)} %collective-permute-done.3.refs_4_), channel_id=1, source_target_pairs={{0,1},{1,0},{2,3},{3,2},{4,5},{5,4},{6,7},{7,6}} | collective-permute-start | bytes 1179656 | tf_op jit(solution)/shard_map/ppermute | solution.py:295
  105.0 6.1 %collective-permute-start.14 = (f32[8,128]{1,0:T(8,128)S(1)}, f32[8,128]{1,0:T(8,128)S(1)}, u32[]{:S(2)}, u32[]{:S(2)}) collective-permute-start(f32[8,128]{1,0:T(8,128)S(1)} %get-tuple-element.101), channel_id=1, source_target_pairs={{0,2},{1,3},{2,0},{3,1},{4,6},{5,7},{6,4},{7,5}} | collective-permute-start | bytes 12296 | tf_op jit(solution)/shard_map/ppermute | solution.py:305
  106.0 5.1 %collective-permute-start.15 = (f32[8,128]{1,0:T(8,128)S(1)}, f32[8,128]{1,0:T(8,128)S(1)}, u32[]{:S(2)}, u32[]{:S(2)}) collective-permute-start(f32[8,128]{1,0:T(8,128)S(1)} %get-tuple-element.101), channel_id=1, source_target_pairs={{0,1},{1,0},{2,3},{3,2},{4,5},{5,4},{6,7},{7,6}} | collective-permute-start | bytes 12296 | tf_op jit(solution)/shard_map/ppermute | solution.py:305
  106.1 5.0 %collective-permute-start.16 = (f32[8,128]{1,0:T(8,128)S(1)}, f32[8,128]{1,0:T(8,128)S(1)}, u32[]{:S(2)}, u32[]{:S(2)}) collective-permute-start(f32[8,128]{1,0:T(8,128)S(1)} %get-tuple-element.101), channel_id=1, source_target_pairs={{0,3},{1,2},{2,1},{3,0},{4,7},{5,6},{6,5},{7,4}} | collective-permute-start | bytes 12296 | tf_op jit(solution)/shard_map/ppermute | solution.py:305

commit v6 on v5

--- a/solution.py
+++ b/solution.py
@@ -160,44 +160,49 @@
     lax.fori_loop(0, tiles, tile, 0)
 
 
-def last_kernel(cfg, xv, rowv, src_info, cols, s_in, sv, wv, part):
-    start, num, kappa = cfg
+def last_kernel(cfg, *refs):
+    start, num, half, kappa = cfg
+    xv, rowv, src_info, cols = refs[:4]
+    sv, wv = refs[6:8] if half else refs[5:7]
     block_chunks = xv.shape[0] // CHUNK
-
-    def row_tile(rt, acc):
-        rsl = pl.ds(pl.multiple_of(rt * SUB_ROWS, SUB_ROWS), SUB_ROWS)
+    acc = jnp.zeros((8, 128), F32)
+    for r0 in range(0, xv.shape[0], SUB_ROWS):
+        rsl = pl.ds(r0, SUB_ROWS)
         gram = lax.dot_general(xv[rsl, :], cols[...], (((1,), (1,)), ((), ())), preferred_element_type=F32)
         sums = sv[rsl, :]
         for k in range(num):
             w = weights(kappa, gram[:, k * CHUNK:(k + 1) * CHUNK], rowv[0, rsl, :], rowv[1, rsl, :],
                         src_info[start + k:start + k + 1, :], src_info[block_chunks + start + k:block_chunks + start + k + 1, :])
             sums = sums + w
-            wv[rsl, k * CHUNK:(k + 1) * CHUNK] = w.astype(jnp.bfloat16)
+            wv[rsl, (half * num + k) * CHUNK:(half * num + k + 1) * CHUNK] = w.astype(jnp.bfloat16)
         sv[rsl, :] = sums
-        for g in range(SUB_ROWS // 8):
-            acc = acc + sums[g * 8:(g + 1) * 8]
-        return acc
-
-    part[...] = lax.fori_loop(0, xv.shape[0] // SUB_ROWS, row_tile, jnp.zeros((8, 128), F32))
-
-
-def last_step(x, rowf, src_info, cols, start, s_sum):
+        if half:
+            for g in range(SUB_ROWS // 8):
+                acc = acc + sums[g * 8:(g + 1) * 8]
+    if half:
+        refs[8][...] = acc
+
+
+def last_step(x, rowf, src_info, cols, start, carry, half):
     rows, width = x.shape
     num = cols.shape[0] // CHUNK
-    ins = [x, rowf, src_info, cols, s_sum]
+    ins = [x, rowf, src_info, cols, *carry]
+    part_shape = [jax.ShapeDtypeStruct((8, 128), F32)] if half else []
     return pl.pallas_call(
-        functools.partial(last_kernel, (start, num, LOG2E * 0.5 / width)),
-        out_shape=[pltpu.VMEM((rows, 128), F32), pltpu.VMEM((rows, num * CHUNK), jnp.bfloat16), jax.ShapeDtypeStruct((8, 128), F32)],
-        in_specs=[VMEM_SPEC] * len(ins), out_specs=[VMEM_SPEC] * 3,
-        input_output_aliases={4: 0},
+        functools.partial(last_kernel, (start, num, half, LOG2E * 0.5 / width)),
+        out_shape=[pltpu.VMEM((rows, 128), F32), pltpu.VMEM((rows, 2 * num * CHUNK), jnp.bfloat16)] + part_shape,
+        in_specs=[VMEM_SPEC] * len(ins), out_specs=[VMEM_SPEC] * (2 + len(part_shape)),
+        input_output_aliases={4 + k: k for k in range(len(carry))},
         compiler_params=pltpu.CompilerParams(vmem_limit_bytes=VMEM_LIMIT),
-        cost_estimate=pl.CostEstimate(flops=2 * rows * num * CHUNK * width, bytes_accessed=rows * width, transcendentals=0),
-        name='last')(*ins)
-
-
-def finish_kernel(inv_len2, xv, tv, sv, wv, cols, my_info, blank, forces, buf, out_sems):
+        cost_estimate=pl.CostEstimate(flops=2 * rows * num * CHUNK * width, bytes_accessed=rows * width, transcendentals=0))(*ins)
+
+
+def finish_kernel(inv_len2, xv, tv, sv, wv, cols_a, cols_b, my_info, blank, forces, cols, buf, out_sems):
     del blank
     num = live_tiles(my_info)
+    half = cols_a.shape[0]
+    cols[:half, :] = cols_a[...]
+    cols[half:, :] = cols_b[...]
 
     def out(i):
         return pltpu.make_async_copy(
@@ -231,7 +236,7 @@
         functools.partial(finish_kernel, 1.0 / width),
         out_shape=jax.ShapeDtypeStruct((rows, width), F32),
         in_specs=[VMEM_SPEC] * (len(ins) - 1) + [HBM_SPEC], out_specs=HBM_SPEC,
-        scratch_shapes=[pltpu.VMEM((4, FINISH_TILE, width), F32), pltpu.SemaphoreType.DMA((4,))],
+        scratch_shapes=[pltpu.VMEM((2 * ins[4].shape[0], width), x.dtype), pltpu.VMEM((4, FINISH_TILE, width), F32), pltpu.SemaphoreType.DMA((4,))],
         input_output_aliases={len(ins) - 1: 0},
         compiler_params=pltpu.CompilerParams(vmem_limit_bytes=VMEM_LIMIT),
         cost_estimate=pl.CostEstimate(flops=rows * width * 1000, bytes_accessed=rows * width * 4, transcendentals=0),
@@ -261,7 +266,7 @@
         input_output_aliases={} if first else {len(ins) - 2: 0, len(ins) - 1: 1}, **common)(*ins)
 
 
-PIECES = (512, 512, 512, 256, 256)
+PIECES = (256, 512, 512, 512, 256)
 
 
 def solution(mesh):
@@ -293,17 +298,18 @@
             num = PIECES[k] // CHUNK
             piece, *carry = lax.optimization_barrier((piece, *carry))
             relay = lax.ppermute(piece, 'row', pair_perm)
-            carry = step(x, rowf, info, info_cross, piece, off, num, min(4, num), carry)
             if k < len(PIECES) - 1:
+                carry = step(x, rowf, info, info_cross, piece, off, num, min(4, num), carry)
                 carry = step(x, rowf, info, info_diag, relay, off, num, min(4, num), carry)
             else:
                 t_sum, s_sum = carry
-                s_sum, w_last, part = last_step(x, rowf, info_diag, relay, off, s_sum)
+                carry = last_step(x, rowf, info_cross, piece, off, (s_sum,), 0)
+                s_sum, w_last, part = last_step(x, rowf, info_diag, relay, off, carry, 1)
             off += num
         total = part
         for perm in (cross_perm, pair_perm, diag_perm):
             total = total + lax.ppermute(part, 'row', perm)
-        forces = finish(x, t_sum, s_sum, w_last, relay, info, blank)
+        forces = finish(x, t_sum, s_sum, w_last, piece, relay, info, blank)
         return forces, (0.5 * jnp.sum(total)).reshape(1)
 
     row_spec = P(('sys', 'row'), None)

time: 114 us -> 108 us (0.947)
  waiting for transfers between devices: 41.7 us -> 36.3 us
    ppermute x4, waiting for transfers between devices: 36 us -> 31.2 us  [per_device(): arrived.append(lax.ppermute(x[off:off + size], 'row', cross_perm))]
    pallas_call x11 -> x10, Pallas kernels: 47.9 us -> 45.6 us  [step(): pl.pallas_call(kernel, out_shape=[pltpu.VMEM((rows, width), F32), pltpu.V...]
    ppermute x4, starting transfers between devices: 0.07 us -> 1.24 us  [per_device(): arrived.append(lax.ppermute(x[off:off + size], 'row', cross_perm))]
    pallas_call x1 -> x2, Pallas kernels: 1.84 us -> 2.74 us  [last_step(): pl.pallas_call(functools.partial(last_kernel, (start, num, half, LOG2E *...]
  transfers between devices with their start and end apart: 17 -> 17, of which waited for: 8 -> 6; matrix products, arithmetic and copies ran while one was open for 0% -> 0% of each run, Pallas kernels for 45% -> 47%
where the time goes in v6:
time: 108 us
  Pallas kernels  55.3 us (51%)
  waiting for transfers between devices  36.3 us (34%)
  starting transfers between devices  9.49 us (9%)
  between operations  3.28 us (3%)
  local copies, waits for them, and re-layouts  2.76 us (3%)
    pallas_call x10, Pallas kernels, step(): pl.pallas_call(kernel, out_shape=[pltpu.VMEM((rows, width), F32), pltpu.V...  45.6 us
    ppermute x4, waiting for transfers between devices, per_device(): arrived.append(lax.ppermute(x[off:off + size], 'row', cross_perm))  31.2 us
    ppermute x5, waiting for transfers between devices, per_device(): relay = lax.ppermute(piece, 'row', pair_perm)  5.07 us
    pallas_call x1, Pallas kernels, finish(): pl.pallas_call(functools.partial(finish_kernel, 1.0 / width), out_shape=j...  4.11 us
    ppermute x5, starting transfers between devices, per_device(): relay = lax.ppermute(piece, 'row', pair_perm)  3.96 us
    pallas_call x1, Pallas kernels, prep(): pl.pallas_call(functools.partial(prep_kernel, LOG2E * 0.5 / width), out_s...  2.87 us
    pallas_call x2, Pallas kernels, last_step(): pl.pallas_call(functools.partial(last_kernel, (start, num, half, LOG2E *...  2.74 us
    unnamed x4, local copies, waits for them, and re-layouts  2.58 us
  transfers between devices with their start and end apart: 17, of which 6 were waited for; matrix products, arithmetic and copies ran while one was open for 0% of the time, Pallas kernels for 47%

profile of v6, /device:TPU:5, one launch (start us, length us, event | category | flops | bytes accessed | tf_op | source)
XLA Modules:
  0.0 107.9 jit_solution(6591577696130224190)
XLA Ops:
  1.3 1.9 %copy-done = bf16[2048,768]{1,0:T(8,128)(2,1)S(1)} copy-done((bf16[2048,768]{1,0:T(8,128)(2,1)S(1)}, bf16[2048,768]{1,0:T(8,128)(2,1)}, u32[]{:S(2)}) %copy-start) | copy-done | bytes 3145752
  3.2 0.7 copy-done.1
  3.9 2.9 %prep.1 = (bf16[2048,768]{1,0:T(8,128)(2,1)S(1)}, f32[2,2048,128]{2,1,0:T(8,128)S(1)}, f32[40,128]{1,0:T(8,128)S(1)}, f32[2048,768]{1,0:T(8,128)}) custom-call(bf16[2048,768]{1,0:T(8,128)(2,1)S(1)} %copy-done, f32[16,128]{1,0:T(8,128)S(1)} %bitcast.4, s32[1]{0:T(128)} %copy.49.count_ref), custom_call_target="tpu_custom_call" | custom-call | tf_op jit(solution)/shard_map/prep/pallas_call | solution.py:85
  6.7 0.7 collective-permute-start.3
  7.5 0.0 collective-permute-start.2
  7.5 1.2 %collective-permute-start.1 = (f32[40,128]{1,0:T(8,128)S(1)}, f32[40,128]{1,0:T(8,128)S(1)}, u32[]{:S(2)}, u32[]{:S(2)}) collective-permute-start(f32[40,128]{1,0:T(8,128)S(1)} %get-tuple-element.54.refs_2_.my_info), channel_id=1, source_target_pairs={{0,2},{1,3},{2,0},{3,1},{4,6},{5,7},{6,4},{7,5}} | collective-permute-start | bytes 61448 | tf_op jit(solution)/shard_map/ppermute | solution.py:284
  8.7 0.1 slice_select_fusion
  8.8 0.3 collective-permute-start.8
  9.1 0.2 fusion
  9.3 1.2 %collective-permute-start.7 = (bf16[512,768]{1,0:T(8,128)(2,1)S(1)}, bf16[512,768]{1,0:T(8,128)(2,1)S(1)}, u32[]{:S(2)}, u32[]{:S(2)}) collective-permute-start(bf16[512,768]{1,0:T(8,128)(2,1)S(1)} %get-tuple-element.102), channel_id=1, source_target_pairs={{0,2},{1,3},{2,0},{3,1},{4,6},{5,7},{6,4},{7,5}} | collective-permute-start | bytes 2359304 | tf_op jit(solution)/shard_map/ppermute | solution.py:288
  10.5 17.1 %step_0_16.2 = (f32[2048,768]{1,0:T(8,128)S(1)}, f32[2048,128]{1,0:T(8,128)S(1)}) custom-call(bf16[2048,768]{1,0:T(8,128)(2,1)S(1)} %get-tuple-element.52.refs_0_.xv, f32[2,2048,128]{2,1,0:T(8,128)S(1)} %get-tuple-element.53.refs_1_, f32[40,128]{1,0:T(8,128)S(1)} %get-tuple-element.54.refs_2_.my_info), custom_call_target="tpu_custom_call" | custom-call | flops 7730940928 | bytes 1572864 | tf_op jit(solution)/shard_map/step_0_16/pallas_call | solution.py:262
  27.5 0.0 collective-permute-done.3.refs_4_
  27.5 0.0 collective-permute-done.2.refs_3_
  27.5 11.4 %step_0_16.3 = (f32[2048,768]{1,0:T(8,128)S(1)}, f32[2048,128]{1,0:T(8,128)S(1)}) custom-call(bf16[2048,768]{1,0:T(8,128)(2,1)S(1)} %get-tuple-element.52.refs_0_.xv, f32[2,2048,128]{2,1,0:T(8,128)S(1)} %get-tuple-element.53.refs_1_, f32[40,128]{1,0:T(8,128)S(1)} %get-tuple-element.54.refs_2_.my_info, ...), custom_call_target="tpu_custom_call", output_to_operand_aliasing={{0}: (5, {}), {1}: (6, {})} | custom-call | flops 7730940928 | bytes 1572864 | tf_op jit(solution)/shard_map/step_0_16/pallas_call | solution.py:262
  39.0 0.0 collective-permute-done.8.refs_4_
  39.0 0.8 collective-permute-start.9
  39.9 0.0 collective-permute-start.4
  39.9 2.3 %step_0_2.2 = (f32[2048,768]{1,0:T(8,128)S(1)}, f32[2048,128]{1,0:T(8,128)S(1)}) custom-call(bf16[2048,768]{1,0:T(8,128)(2,1)S(1)} %get-tuple-element.52.refs_0_.xv, f32[2,2048,128]{2,1,0:T(8,128)S(1)} %get-tuple-element.53.refs_1_, f32[40,128]{1,0:T(8,128)S(1)} %get-tuple-element.54.refs_2_.my_info, ...), custom_call_target="tpu_custom_call", output_to_operand_aliasing={{0}: (5, {}), {1}: (6, {})} | custom-call | flops 966367616 | bytes 1572864 | tf_op jit(solution)/shard_map/step_0_2/pallas_call | solution.py:262
  42.2 0.0 collective-permute-done.4.refs_3_.refs_2_
  42.2 2.3 %step_0_2.3 = (f32[2048,768]{1,0:T(8,128)S(1)}, f32[2048,128]{1,0:T(8,128)S(1)}) custom-call(bf16[2048,768]{1,0:T(8,128)(2,1)S(1)} %get-tuple-element.52.refs_0_.xv, f32[2,2048,128]{2,1,0:T(8,128)S(1)} %get-tuple-element.53.refs_1_, f32[40,128]{1,0:T(8,128)S(1)} %get-tuple-element.54.refs_2_.my_info, ...), custom_call_target="tpu_custom_call", output_to_operand_aliasing={{0}: (5, {}), {1}: (6, {})} | custom-call | flops 966367616 | bytes 1572864 | tf_op jit(solution)/shard_map/step_0_2/pallas_call | solution.py:262
  44.5 0.0 collective-permute-done.7.refs_4_
  44.5 0.5 collective-permute-start.10
  45.0 0.3 step_2_4.2
  45.4 1.6 %collective-permute-done.10.refs_4_ = bf16[512,768]{1,0:T(8,128)(2,1)S(1)} collective-permute-done((bf16[512,768]{1,0:T(8,128)(2,1)S(1)}, bf16[512,768]{1,0:T(8,128)(2,1)S(1)}, u32[]{:S(2)}, u32[]{:S(2)}) %collective-permute-start.10) | collective-permute-done | bytes 786464 | tf_op jit(solution)/shard_map/ppermute | solution.py:300
  46.9 3.9 %step_2_4.3 = (f32[2048,768]{1,0:T(8,128)S(1)}, f32[2048,128]{1,0:T(8,128)S(1)}) custom-call(bf16[2048,768]{1,0:T(8,128)(2,1)S(1)} %get-tuple-element.52.refs_0_.xv, f32[2,2048,128]{2,1,0:T(8,128)S(1)} %get-tuple-element.53.refs_1_, f32[40,128]{1,0:T(8,128)S(1)} %get-tuple-element.54.refs_2_.my_info, ...), custom_call_target="tpu_custom_call", output_to_operand_aliasing={{0}: (5, {}), {1}: (6, {})} | custom-call | flops 1932735232 | bytes 1572864 | tf_op jit(solution)/shard_map/step_2_4/pallas_call | solution.py:262
  50.8 13.3 %collective-permute-done.6.refs_4_ = bf16[512,768]{1,0:T(8,128)(2,1)S(1)} collective-permute-done((bf16[512,768]{1,0:T(8,128)(2,1)S(1)}, bf16[512,768]{1,0:T(8,128)(2,1)S(1)}, u32[]{:S(2)}, u32[]{:S(2)}) %collective-permute-start.6) | collective-permute-done | bytes 786464 | tf_op jit(solution)/shard_map/ppermute | solution.py:288
  64.1 0.9 collective-permute-start.11
  65.0 0.0 collective-permute-start.5
  65.0 0.1 step_6_4.2
  65.1 1.8 %collective-permute-done.11.refs_4_ = bf16[512,768]{1,0:T(8,128)(2,1)S(1)} collective-permute-done((bf16[512,768]{1,0:T(8,128)(2,1)S(1)}, bf16[512,768]{1,0:T(8,128)(2,1)S(1)}, u32[]{:S(2)}, u32[]{:S(2)}) %collective-permute-start.11) | collective-permute-done | bytes 786464 | tf_op jit(solution)/shard_map/ppermute | solution.py:300
  66.9 4.1 %step_6_4.3 = (f32[2048,768]{1,0:T(8,128)S(1)}, f32[2048,128]{1,0:T(8,128)S(1)}) custom-call(bf16[2048,768]{1,0:T(8,128)(2,1)S(1)} %get-tuple-element.52.refs_0_.xv, f32[2,2048,128]{2,1,0:T(8,128)S(1)} %get-tuple-element.53.refs_1_, f32[40,128]{1,0:T(8,128)S(1)} %get-tuple-element.54.refs_2_.my_info, ...), custom_call_target="tpu_custom_call", output_to_operand_aliasing={{0}: (5, {}), {1}: (6, {})} | custom-call | flops 1932735232 | bytes 1572864 | tf_op jit(solution)/shard_map/step_6_4/pallas_call | solution.py:262
  71.0 13.1 %collective-permute-done.5.refs_4_ = bf16[512,768]{1,0:T(8,128)(2,1)S(1)} collective-permute-done((bf16[512,768]{1,0:T(8,128)(2,1)S(1)}, bf16[512,768]{1,0:T(8,128)(2,1)S(1)}, u32[]{:S(2)}, u32[]{:S(2)}) %collective-permute-start.5) | collective-permute-done | bytes 786464 | tf_op jit(solution)/shard_map/ppermute | solution.py:288
  84.1 0.9 collective-permute-start.12
  85.0 0.0 collective-permute-start
  85.0 0.1 step_10_4.2
  85.2 1.7 %collective-permute-done.12.refs_4_ = bf16[512,768]{1,0:T(8,128)(2,1)S(1)} collective-permute-done((bf16[512,768]{1,0:T(8,128)(2,1)S(1)}, bf16[512,768]{1,0:T(8,128)(2,1)S(1)}, u32[]{:S(2)}, u32[]{:S(2)}) %collective-permute-start.12) | collective-permute-done | bytes 786464 | tf_op jit(solution)/shard_map/ppermute | solution.py:300
  86.9 3.9 %step_10_4.3 = (f32[2048,768]{1,0:T(8,128)S(1)}, f32[2048,128]{1,0:T(8,128)S(1)}) custom-call(bf16[2048,768]{1,0:T(8,128)(2,1)S(1)} %get-tuple-element.52.refs_0_.xv, f32[2,2048,128]{2,1,0:T(8,128)S(1)} %get-tuple-element.53.refs_1_, f32[40,128]{1,0:T(8,128)S(1)} %get-tuple-element.54.refs_2_.my_info, ...), custom_call_target="tpu_custom_call", output_to_operand_aliasing={{0}: (5, {}), {1}: (6, {})} | custom-call | flops 1932735232 | bytes 1572864 | tf_op jit(solution)/shard_map/step_10_4/pallas_call | solution.py:262
  90.8 4.9 %collective-permute-done.refs_3_.cols_a = bf16[256,768]{1,0:T(8,128)(2,1)S(1)} collective-permute-done((bf16[256,768]{1,0:T(8,128)(2,1)S(1)}, bf16[256,768]{1,0:T(8,128)(2,1)S(1)}, u32[]{:S(2)}, u32[]{:S(2)}) %collective-permute-start) | collective-permute-done | bytes 393248 | tf_op jit(solution)/shard_map/ppermute | solution.py:288
  95.7 0.9 collective-permute-start.13
  96.5 1.3 %shard_map.50 = (f32[2048,128]{1,0:T(8,128)S(1)}, bf16[2048,512]{1,0:T(8,128)(2,1)S(1)}) custom-call(bf16[2048,768]{1,0:T(8,128)(2,1)S(1)} %get-tuple-element.52.refs_0_.xv, f32[2,2048,128]{2,1,0:T(8,128)S(1)} %get-tuple-element.53.refs_1_, f32[40,128]{1,0:T(8,128)S(1)} %collective-permute-done.1.refs_3_.refs_2_, ...), custom_call_target="tpu_custom_call", output_to_operand_aliasing={{0}: (4, {})} | custom-call | flops 805306368 | bytes 1572864 | tf_op jit(solution)/shard_map/pallas_call | solution.py:191
  97.9 0.0 collective-permute-done.13.refs_3_.cols_b
  97.9 1.4 %shard_map.51 = (f32[2048,128]{1,0:T(8,128)S(1)}, bf16[2048,512]{1,0:T(8,128)(2,1)S(1)}, f32[8,128]{1,0:T(8,128)S(1)}) custom-call(bf16[2048,768]{1,0:T(8,128)(2,1)S(1)} %get-tuple-element.52.refs_0_.xv, f32[2,2048,128]{2,1,0:T(8,128)S(1)} %get-tuple-element.53.refs_1_, ...), custom_call_target="tpu_custom_call", output_to_operand_aliasing={{0}: (4, {}), {1}: (5, {})} | custom-call | flops 805306368 | bytes 1572864 | tf_op jit(solution)/shard_map/pallas_call | solution.py:191
  99.3 0.0 collective-permute-start.14
  99.3 0.6 collective-permute-start.15
  100.0 1.4 %collective-permute-start.16 = (f32[8,128]{1,0:T(8,128)S(1)}, f32[8,128]{1,0:T(8,128)S(1)}, u32[]{:S(2)}, u32[]{:S(2)}) collective-permute-start(f32[8,128]{1,0:T(8,128)S(1)} %get-tuple-element.101), channel_id=1, source_target_pairs={{0,3},{1,2},{2,1},{3,0},{4,7},{5,6},{6,5},{7,4}} | collective-permute-start | bytes 12296 | tf_op jit(solution)/shard_map/ppermute | solution.py:311
  101.3 4.1 %finish.1 = f32[2048,768]{1,0:T(8,128)} custom-call(bf16[2048,768]{1,0:T(8,128)(2,1)S(1)} %get-tuple-element.52.refs_0_.xv, f32[2048,768]{1,0:T(8,128)S(1)} %get-tuple-element.93.tv, f32[2048,128]{1,0:T(8,128)S(1)} %get-tuple-element.98.sv, bf16[2048,512]{1,0:T(8,128)(2,1)S(1)} %get-tuple-element.99.wv, ...), custom_call_target="tpu_custom_call", output_to_operand_aliasing={{}: (7, {})} | custom-call | flops 1572864000 | bytes 6291456 | tf_op jit(solution)/shard_map/finish/pallas_call | solution.py:235
  105.4 0.0 collective-permute-done.14
  105.5 0.6 add_reduce_fusion
  (9 shorter events, 0.0 us)
Async XLA Ops:
  1.3 1.9 %copy-start = (bf16[2048,768]{1,0:T(8,128)(2,1)S(1)}, bf16[2048,768]{1,0:T(8,128)(2,1)}, u32[]{:S(2)}) copy-start(bf16[2048,768]{1,0:T(8,128)(2,1)} %raw_hbm.1) | copy-start | bytes 9437188
  3.2 0.7 copy-start.1
  6.7 20.8 %collective-permute-start.3 = (bf16[2048,768]{1,0:T(8,128)(2,1)S(1)}, bf16[2048,768]{1,0:T(8,128)(2,1)S(1)}, u32[]{:S(2)}, u32[]{:S(2)}) collective-permute-start(bf16[2048,768]{1,0:T(8,128)(2,1)S(1)} %get-tuple-element.52.refs_0_.xv), channel_id=1, source_target_pairs={{0,1},{1,0},{2,3},{3,2},{4,5},{5,4},{6,7},{7,6}} | collective-permute-start | bytes 9437192 | tf_op jit(solution)/shard_map/ppermute | solution.py:290
  7.5 20.1 %collective-permute-start.2 = (f32[40,128]{1,0:T(8,128)S(1)}, f32[40,128]{1,0:T(8,128)S(1)}, u32[]{:S(2)}, u32[]{:S(2)}) collective-permute-start(f32[40,128]{1,0:T(8,128)S(1)} %get-tuple-element.54.refs_2_.my_info), channel_id=1, source_target_pairs={{0,1},{1,0},{2,3},{3,2},{4,5},{5,4},{6,7},{7,6}} | collective-permute-start | bytes 61448 | tf_op jit(solution)/shard_map/ppermute | solution.py:285
  7.5 31.5 %collective-permute-start.1 = (f32[40,128]{1,0:T(8,128)S(1)}, f32[40,128]{1,0:T(8,128)S(1)}, u32[]{:S(2)}, u32[]{:S(2)}) collective-permute-start(f32[40,128]{1,0:T(8,128)S(1)} %get-tuple-element.54.refs_2_.my_info), channel_id=1, source_target_pairs={{0,2},{1,3},{2,0},{3,1},{4,6},{5,7},{6,4},{7,5}} | collective-permute-start | bytes 61448 | tf_op jit(solution)/shard_map/ppermute | solution.py:284
  8.8 30.2 %collective-permute-start.8 = (bf16[256,768]{1,0:T(8,128)(2,1)S(1)}, bf16[256,768]{1,0:T(8,128)(2,1)S(1)}, u32[]{:S(2)}, u32[]{:S(2)}) collective-permute-start(bf16[256,768]{1,0:T(8,128)(2,1)S(1)} %slice_select_fusion), channel_id=1, source_target_pairs={{0,2},{1,3},{2,0},{3,1},{4,6},{5,7},{6,4},{7,5}} | collective-permute-start | bytes 1179656 | tf_op jit(solution)/shard_map/ppermute | solution.py:282
  9.3 35.3 %collective-permute-start.7 = (bf16[512,768]{1,0:T(8,128)(2,1)S(1)}, bf16[512,768]{1,0:T(8,128)(2,1)S(1)}, u32[]{:S(2)}, u32[]{:S(2)}) collective-permute-start(bf16[512,768]{1,0:T(8,128)(2,1)S(1)} %get-tuple-element.102), channel_id=1, source_target_pairs={{0,2},{1,3},{2,0},{3,1},{4,6},{5,7},{6,4},{7,5}} | collective-permute-start | bytes 2359304 | tf_op jit(solution)/shard_map/ppermute | solution.py:288
  39.0 3.2 %collective-permute-start.9 = (bf16[256,768]{1,0:T(8,128)(2,1)S(1)}, bf16[256,768]{1,0:T(8,128)(2,1)S(1)}, u32[]{:S(2)}, u32[]{:S(2)}) collective-permute-start(bf16[256,768]{1,0:T(8,128)(2,1)S(1)} %collective-permute-done.8.refs_4_), channel_id=1, source_target_pairs={{0,1},{1,0},{2,3},{3,2},{4,5},{5,4},{6,7},{7,6}} | collective-permute-start | bytes 1179656 | tf_op jit(solution)/shard_map/ppermute | solution.py:300
  39.9 2.3 %collective-permute-start.4 = (f32[40,128]{1,0:T(8,128)S(1)}, f32[40,128]{1,0:T(8,128)S(1)}, u32[]{:S(2)}, u32[]{:S(2)}) collective-permute-start(f32[40,128]{1,0:T(8,128)S(1)} %collective-permute-done.1.refs_3_.refs_2_), channel_id=1, source_target_pairs={{0,1},{1,0},{2,3},{3,2},{4,5},{5,4},{6,7},{7,6}} | collective-permute-start | bytes 61448 | tf_op jit(solution)/shard_map/ppermute | solution.py:295
  44.5 2.4 %collective-permute-start.10 = (bf16[512,768]{1,0:T(8,128)(2,1)S(1)}, bf16[512,768]{1,0:T(8,128)(2,1)S(1)}, u32[]{:S(2)}, u32[]{:S(2)}) collective-permute-start(bf16[512,768]{1,0:T(8,128)(2,1)S(1)} %collective-permute-done.7.refs_4_), channel_id=1, source_target_pairs={{0,1},{1,0},{2,3},{3,2},{4,5},{5,4},{6,7},{7,6}} | collective-permute-start | bytes 2359304 | tf_op jit(solution)/shard_map/ppermute | solution.py:300
  45.0 19.1 %collective-permute-start.6 = (bf16[512,768]{1,0:T(8,128)(2,1)S(1)}, bf16[512,768]{1,0:T(8,128)(2,1)S(1)}, u32[]{:S(2)}, u32[]{:S(2)}) collective-permute-start(bf16[512,768]{1,0:T(8,128)(2,1)S(1)} %get-tuple-element.103), channel_id=1, source_target_pairs={{0,2},{1,3},{2,0},{3,1},{4,6},{5,7},{6,4},{7,5}} | collective-permute-start | bytes 2359304 | tf_op jit(solution)/shard_map/ppermute | solution.py:288
  64.1 2.8 %collective-permute-start.11 = (bf16[512,768]{1,0:T(8,128)(2,1)S(1)}, bf16[512,768]{1,0:T(8,128)(2,1)S(1)}, u32[]{:S(2)}, u32[]{:S(2)}) collective-permute-start(bf16[512,768]{1,0:T(8,128)(2,1)S(1)} %collective-permute-done.6.refs_4_), channel_id=1, source_target_pairs={{0,1},{1,0},{2,3},{3,2},{4,5},{5,4},{6,7},{7,6}} | collective-permute-start | bytes 2359304 | tf_op jit(solution)/shard_map/ppermute | solution.py:300
  65.0 19.1 %collective-permute-start.5 = (bf16[512,768]{1,0:T(8,128)(2,1)S(1)}, bf16[512,768]{1,0:T(8,128)(2,1)S(1)}, u32[]{:S(2)}, u32[]{:S(2)}) collective-permute-start(bf16[512,768]{1,0:T(8,128)(2,1)S(1)} %get-tuple-element.104), channel_id=1, source_target_pairs={{0,2},{1,3},{2,0},{3,1},{4,6},{5,7},{6,4},{7,5}} | collective-permute-start | bytes 2359304 | tf_op jit(solution)/shard_map/ppermute | solution.py:288
  84.1 2.8 %collective-permute-start.12 = (bf16[512,768]{1,0:T(8,128)(2,1)S(1)}, bf16[512,768]{1,0:T(8,128)(2,1)S(1)}, u32[]{:S(2)}, u32[]{:S(2)}) collective-permute-start(bf16[512,768]{1,0:T(8,128)(2,1)S(1)} %collective-permute-done.5.refs_4_), channel_id=1, source_target_pairs={{0,1},{1,0},{2,3},{3,2},{4,5},{5,4},{6,7},{7,6}} | collective-permute-start | bytes 2359304 | tf_op jit(solution)/shard_map/ppermute | solution.py:300
  85.0 10.7 %collective-permute-start = (bf16[256,768]{1,0:T(8,128)(2,1)S(1)}, bf16[256,768]{1,0:T(8,128)(2,1)S(1)}, u32[]{:S(2)}, u32[]{:S(2)}) collective-permute-start(bf16[256,768]{1,0:T(8,128)(2,1)S(1)} %slice.15), channel_id=1, source_target_pairs={{0,2},{1,3},{2,0},{3,1},{4,6},{5,7},{6,4},{7,5}} | collective-permute-start | bytes 1179656 | tf_op jit(solution)/shard_map/ppermute | solution.py:288
  95.7 2.2 %collective-permute-start.13 = (bf16[256,768]{1,0:T(8,128)(2,1)S(1)}, bf16[256,768]{1,0:T(8,128)(2,1)S(1)}, u32[]{:S(2)}, u32[]{:S(2)}) collective-permute-start(bf16[256,768]{1,0:T(8,128)(2,1)S(1)} %collective-permute-done.refs_3_.cols_a), channel_id=1, source_target_pairs={{0,1},{1,0},{2,3},{3,2},{4,5},{5,4},{6,7},{7,6}} | collective-permute-start | bytes 1179656 | tf_op jit(solution)/shard_map/ppermute | solution.py:300
  99.3 6.1 %collective-permute-start.14 = (f32[8,128]{1,0:T(8,128)S(1)}, f32[8,128]{1,0:T(8,128)S(1)}, u32[]{:S(2)}, u32[]{:S(2)}) collective-permute-start(f32[8,128]{1,0:T(8,128)S(1)} %get-tuple-element.101), channel_id=1, source_target_pairs={{0,2},{1,3},{2,0},{3,1},{4,6},{5,7},{6,4},{7,5}} | collective-permute-start | bytes 12296 | tf_op jit(solution)/shard_map/ppermute | solution.py:311
  99.3 6.1 %collective-permute-start.15 = (f32[8,128]{1,0:T(8,128)S(1)}, f32[8,128]{1,0:T(8,128)S(1)}, u32[]{:S(2)}, u32[]{:S(2)}) collective-permute-start(f32[8,128]{1,0:T(8,128)S(1)} %get-tuple-element.101), channel_id=1, source_target_pairs={{0,1},{1,0},{2,3},{3,2},{4,5},{5,4},{6,7},{7,6}} | collective-permute-start | bytes 12296 | tf_op jit(solution)/shard_map/ppermute | solution.py:311
  100.0 5.5 %collective-permute-start.16 = (f32[8,128]{1,0:T(8,128)S(1)}, f32[8,128]{1,0:T(8,128)S(1)}, u32[]{:S(2)}, u32[]{:S(2)}) collective-permute-start(f32[8,128]{1,0:T(8,128)S(1)} %get-tuple-element.101), channel_id=1, source_target_pairs={{0,3},{1,2},{2,1},{3,0},{4,7},{5,6},{6,5},{7,4}} | collective-permute-start | bytes 12296 | tf_op jit(solution)/shard_map/ppermute | solution.py:311

commit v7 on v5

--- a/solution.py
+++ b/solution.py
@@ -164,8 +164,9 @@
     start, num, kappa = cfg
     block_chunks = xv.shape[0] // CHUNK
 
-    def row_tile(rt, acc):
-        rsl = pl.ds(pl.multiple_of(rt * SUB_ROWS, SUB_ROWS), SUB_ROWS)
+    acc = jnp.zeros((8, 128), F32)
+    for r0 in range(0, xv.shape[0], SUB_ROWS):
+        rsl = pl.ds(r0, SUB_ROWS)
         gram = lax.dot_general(xv[rsl, :], cols[...], (((1,), (1,)), ((), ())), preferred_element_type=F32)
         sums = sv[rsl, :]
         for k in range(num):
@@ -176,9 +177,7 @@
         sv[rsl, :] = sums
         for g in range(SUB_ROWS // 8):
             acc = acc + sums[g * 8:(g + 1) * 8]
-        return acc
-
-    part[...] = lax.fori_loop(0, xv.shape[0] // SUB_ROWS, row_tile, jnp.zeros((8, 128), F32))
+    part[...] = acc
 
 
 def last_step(x, rowf, src_info, cols, start, s_sum):
@@ -261,7 +260,7 @@
         input_output_aliases={} if first else {len(ins) - 2: 0, len(ins) - 1: 1}, **common)(*ins)
 
 
-PIECES = (512, 512, 512, 256, 256)
+PIECES = (256, 512, 512, 512, 256)
 
 
 def solution(mesh):

time: 114 us -> 108 us (0.947)
  waiting for transfers between devices: 41.7 us -> 37.4 us
  Pallas kernels: 56 us -> 54 us
    ppermute x4, waiting for transfers between devices: 36 us -> 31.1 us  [per_device(): arrived.append(lax.ppermute(x[off:off + size], 'row', cross_perm))]
    pallas_call x11, Pallas kernels: 47.9 us -> 46.3 us  [step(): pl.pallas_call(kernel, out_shape=[pltpu.VMEM((rows, width), F32), pltpu.V...]
    ppermute x4, starting transfers between devices: 0.07 us -> 1.24 us  [per_device(): arrived.append(lax.ppermute(x[off:off + size], 'row', cross_perm))]
  transfers between devices with their start and end apart: 17 -> 17, of which waited for: 8 -> 7; matrix products, arithmetic and copies ran while one was open for 0% -> 0% of each run, Pallas kernels for 45% -> 46%
where the time goes in v7:
time: 108 us
  Pallas kernels  54 us (50%)
  waiting for transfers between devices  37.4 us (35%)
  starting transfers between devices  10.1 us (9%)
  between operations  3.28 us (3%)
  local copies, waits for them, and re-layouts  2.76 us (3%)
    pallas_call x11, Pallas kernels, step(): pl.pallas_call(kernel, out_shape=[pltpu.VMEM((rows, width), F32), pltpu.V...  46.3 us
    ppermute x4, waiting for transfers between devices, per_device(): arrived.append(lax.ppermute(x[off:off + size], 'row', cross_perm))  31.1 us
    ppermute x5, waiting for transfers between devices, per_device(): relay = lax.ppermute(piece, 'row', pair_perm)  6.27 us
    ppermute x5, starting transfers between devices, per_device(): relay = lax.ppermute(piece, 'row', pair_perm)  3.93 us
    pallas_call x1, Pallas kernels, finish(): pl.pallas_call(functools.partial(finish_kernel, 1.0 / width), out_shape=j...  3.4 us
    pallas_call x1, Pallas kernels, prep(): pl.pallas_call(functools.partial(prep_kernel, LOG2E * 0.5 / width), out_s...  2.87 us
    ppermute x3, starting transfers between devices, per_device(): total = total + lax.ppermute(part, 'row', perm)  2.68 us
    unnamed x4, local copies, waits for them, and re-layouts  2.58 us
  transfers between devices with their start and end apart: 17, of which 7 were waited for; matrix products, arithmetic and copies ran while one was open for 0% of the time, Pallas kernels for 46%

profile of v7, /device:TPU:5, one launch (start us, length us, event | category | flops | bytes accessed | tf_op | source)
XLA Modules:
  0.0 108.3 jit_solution(11659023450150449519)
XLA Ops:
  1.3 1.9 %copy-done = bf16[2048,768]{1,0:T(8,128)(2,1)S(1)} copy-done((bf16[2048,768]{1,0:T(8,128)(2,1)S(1)}, bf16[2048,768]{1,0:T(8,128)(2,1)}, u32[]{:S(2)}) %copy-start) | copy-done | bytes 3145752
  3.2 0.7 copy-done.1
  3.9 2.9 %prep.1 = (bf16[2048,768]{1,0:T(8,128)(2,1)S(1)}, f32[2,2048,128]{2,1,0:T(8,128)S(1)}, f32[40,128]{1,0:T(8,128)S(1)}, f32[2048,768]{1,0:T(8,128)}) custom-call(bf16[2048,768]{1,0:T(8,128)(2,1)S(1)} %copy-done, f32[16,128]{1,0:T(8,128)S(1)} %bitcast.4, s32[1]{0:T(128)} %copy.49.count_ref), custom_call_target="tpu_custom_call" | custom-call | tf_op jit(solution)/shard_map/prep/pallas_call | solution.py:85
  6.7 0.7 collective-permute-start.2
  7.5 0.0 collective-permute-start.1
  7.5 1.2 %collective-permute-start = (f32[40,128]{1,0:T(8,128)S(1)}, f32[40,128]{1,0:T(8,128)S(1)}, u32[]{:S(2)}, u32[]{:S(2)}) collective-permute-start(f32[40,128]{1,0:T(8,128)S(1)} %get-tuple-element.54.refs_2_.my_info), channel_id=1, source_target_pairs={{0,2},{1,3},{2,0},{3,1},{4,6},{5,7},{6,4},{7,5}} | collective-permute-start | bytes 61448 | tf_op jit(solution)/shard_map/ppermute | solution.py:278
  8.7 0.1 slice_select_fusion
  8.8 0.3 collective-permute-start.8
  9.1 0.2 fusion
  9.3 1.2 %collective-permute-start.7 = (bf16[512,768]{1,0:T(8,128)(2,1)S(1)}, bf16[512,768]{1,0:T(8,128)(2,1)S(1)}, u32[]{:S(2)}, u32[]{:S(2)}) collective-permute-start(bf16[512,768]{1,0:T(8,128)(2,1)S(1)} %get-tuple-element.102), channel_id=1, source_target_pairs={{0,2},{1,3},{2,0},{3,1},{4,6},{5,7},{6,4},{7,5}} | collective-permute-start | bytes 2359304 | tf_op jit(solution)/shard_map/ppermute | solution.py:282
  10.5 17.3 %step_0_16.2 = (f32[2048,768]{1,0:T(8,128)S(1)}, f32[2048,128]{1,0:T(8,128)S(1)}) custom-call(bf16[2048,768]{1,0:T(8,128)(2,1)S(1)} %get-tuple-element.52.refs_0_.xv, f32[2,2048,128]{2,1,0:T(8,128)S(1)} %get-tuple-element.53.refs_1_.rowv, f32[40,128]{1,0:T(8,128)S(1)} %get-tuple-element.54.refs_2_.my_info), custom_call_target="tpu_custom_call" | custom-call | flops 7730940928 | bytes 1572864 | tf_op jit(solution)/shard_map/step_0_16/pallas_call | solution.py:256
  27.7 0.0 collective-permute-done.2.refs_4_
  27.8 11.6 %step_0_16.3 = (f32[2048,768]{1,0:T(8,128)S(1)}, f32[2048,128]{1,0:T(8,128)S(1)}) custom-call(bf16[2048,768]{1,0:T(8,128)(2,1)S(1)} %get-tuple-element.52.refs_0_.xv, f32[2,2048,128]{2,1,0:T(8,128)S(1)} %get-tuple-element.53.refs_1_.rowv, f32[40,128]{1,0:T(8,128)S(1)} %get-tuple-element.54.refs_2_.my_info, ...), custom_call_target="tpu_custom_call", output_to_operand_aliasing={{0}: (5, {}), {1}: (6, {})} | custom-call | flops 7730940928 | bytes 1572864 | tf_op jit(solution)/shard_map/step_0_16/pallas_call | solution.py:256
  39.4 0.0 collective-permute-done.refs_3_
  39.4 0.0 collective-permute-done.8.refs_4_
  39.4 0.8 collective-permute-start.9
  40.2 0.0 collective-permute-start.4
  40.2 2.4 %step_0_2.2 = (f32[2048,768]{1,0:T(8,128)S(1)}, f32[2048,128]{1,0:T(8,128)S(1)}) custom-call(bf16[2048,768]{1,0:T(8,128)(2,1)S(1)} %get-tuple-element.52.refs_0_.xv, f32[2,2048,128]{2,1,0:T(8,128)S(1)} %get-tuple-element.53.refs_1_.rowv, f32[40,128]{1,0:T(8,128)S(1)} %get-tuple-element.54.refs_2_.my_info, ...), custom_call_target="tpu_custom_call", output_to_operand_aliasing={{0}: (5, {}), {1}: (6, {})} | custom-call | flops 966367616 | bytes 1572864 | tf_op jit(solution)/shard_map/step_0_2/pallas_call | solution.py:256
  42.6 0.0 collective-permute-done.4.refs_3_.src_info
  42.6 2.4 %step_0_2.3 = (f32[2048,768]{1,0:T(8,128)S(1)}, f32[2048,128]{1,0:T(8,128)S(1)}) custom-call(bf16[2048,768]{1,0:T(8,128)(2,1)S(1)} %get-tuple-element.52.refs_0_.xv, f32[2,2048,128]{2,1,0:T(8,128)S(1)} %get-tuple-element.53.refs_1_.rowv, f32[40,128]{1,0:T(8,128)S(1)} %get-tuple-element.54.refs_2_.my_info, ...), custom_call_target="tpu_custom_call", output_to_operand_aliasing={{0}: (5, {}), {1}: (6, {})} | custom-call | flops 966367616 | bytes 1572864 | tf_op jit(solution)/shard_map/step_0_2/pallas_call | solution.py:256
  45.0 0.0 collective-permute-done.7.refs_4_
  45.0 0.5 collective-permute-start.10
  45.5 0.3 step_2_4.2
  45.8 1.6 %collective-permute-done.10.refs_4_ = bf16[512,768]{1,0:T(8,128)(2,1)S(1)} collective-permute-done((bf16[512,768]{1,0:T(8,128)(2,1)S(1)}, bf16[512,768]{1,0:T(8,128)(2,1)S(1)}, u32[]{:S(2)}, u32[]{:S(2)}) %collective-permute-start.10) | collective-permute-done | bytes 786464 | tf_op jit(solution)/shard_map/ppermute | solution.py:294
  47.4 3.9 %step_2_4.3 = (f32[2048,768]{1,0:T(8,128)S(1)}, f32[2048,128]{1,0:T(8,128)S(1)}) custom-call(bf16[2048,768]{1,0:T(8,128)(2,1)S(1)} %get-tuple-element.52.refs_0_.xv, f32[2,2048,128]{2,1,0:T(8,128)S(1)} %get-tuple-element.53.refs_1_.rowv, f32[40,128]{1,0:T(8,128)S(1)} %get-tuple-element.54.refs_2_.my_info, ...), custom_call_target="tpu_custom_call", output_to_operand_aliasing={{0}: (5, {}), {1}: (6, {})} | custom-call | flops 1932735232 | bytes 1572864 | tf_op jit(solution)/shard_map/step_2_4/pallas_call | solution.py:256
  51.3 13.2 %collective-permute-done.6.refs_4_ = bf16[512,768]{1,0:T(8,128)(2,1)S(1)} collective-permute-done((bf16[512,768]{1,0:T(8,128)(2,1)S(1)}, bf16[512,768]{1,0:T(8,128)(2,1)S(1)}, u32[]{:S(2)}, u32[]{:S(2)}) %collective-permute-start.6) | collective-permute-done | bytes 786464 | tf_op jit(solution)/shard_map/ppermute | solution.py:282
  64.5 0.9 collective-permute-start.11
  65.4 0.0 collective-permute-start.5
  65.5 0.1 step_6_4.2
  65.6 1.8 %collective-permute-done.11.refs_4_ = bf16[512,768]{1,0:T(8,128)(2,1)S(1)} collective-permute-done((bf16[512,768]{1,0:T(8,128)(2,1)S(1)}, bf16[512,768]{1,0:T(8,128)(2,1)S(1)}, u32[]{:S(2)}, u32[]{:S(2)}) %collective-permute-start.11) | collective-permute-done | bytes 786464 | tf_op jit(solution)/shard_map/ppermute | solution.py:294
  67.4 4.2 %step_6_4.3 = (f32[2048,768]{1,0:T(8,128)S(1)}, f32[2048,128]{1,0:T(8,128)S(1)}) custom-call(bf16[2048,768]{1,0:T(8,128)(2,1)S(1)} %get-tuple-element.52.refs_0_.xv, f32[2,2048,128]{2,1,0:T(8,128)S(1)} %get-tuple-element.53.refs_1_.rowv, f32[40,128]{1,0:T(8,128)S(1)} %get-tuple-element.54.refs_2_.my_info, ...), custom_call_target="tpu_custom_call", output_to_operand_aliasing={{0}: (5, {}), {1}: (6, {})} | custom-call | flops 1932735232 | bytes 1572864 | tf_op jit(solution)/shard_map/step_6_4/pallas_call | solution.py:256
  71.5 13.0 %collective-permute-done.5.refs_4_ = bf16[512,768]{1,0:T(8,128)(2,1)S(1)} collective-permute-done((bf16[512,768]{1,0:T(8,128)(2,1)S(1)}, bf16[512,768]{1,0:T(8,128)(2,1)S(1)}, u32[]{:S(2)}, u32[]{:S(2)}) %collective-permute-start.5) | collective-permute-done | bytes 786464 | tf_op jit(solution)/shard_map/ppermute | solution.py:282
  84.5 0.9 collective-permute-start.12
  85.4 0.0 collective-permute-start.3
  85.5 0.1 step_10_4.2
  85.6 1.7 %collective-permute-done.12.refs_4_ = bf16[512,768]{1,0:T(8,128)(2,1)S(1)} collective-permute-done((bf16[512,768]{1,0:T(8,128)(2,1)S(1)}, bf16[512,768]{1,0:T(8,128)(2,1)S(1)}, u32[]{:S(2)}, u32[]{:S(2)}) %collective-permute-start.12) | collective-permute-done | bytes 786464 | tf_op jit(solution)/shard_map/ppermute | solution.py:294
  87.3 3.9 %step_10_4.3 = (f32[2048,768]{1,0:T(8,128)S(1)}, f32[2048,128]{1,0:T(8,128)S(1)}) custom-call(bf16[2048,768]{1,0:T(8,128)(2,1)S(1)} %get-tuple-element.52.refs_0_.xv, f32[2,2048,128]{2,1,0:T(8,128)S(1)} %get-tuple-element.53.refs_1_.rowv, f32[40,128]{1,0:T(8,128)S(1)} %get-tuple-element.54.refs_2_.my_info, ...), custom_call_target="tpu_custom_call", output_to_operand_aliasing={{0}: (5, {}), {1}: (6, {})} | custom-call | flops 1932735232 | bytes 1572864 | tf_op jit(solution)/shard_map/step_10_4/pallas_call | solution.py:256
  91.3 4.9 %collective-permute-done.3.refs_4_ = bf16[256,768]{1,0:T(8,128)(2,1)S(1)} collective-permute-done((bf16[256,768]{1,0:T(8,128)(2,1)S(1)}, bf16[256,768]{1,0:T(8,128)(2,1)S(1)}, u32[]{:S(2)}, u32[]{:S(2)}) %collective-permute-start.3) | collective-permute-done | bytes 393248 | tf_op jit(solution)/shard_map/ppermute | solution.py:282
  96.1 0.9 collective-permute-start.13
  97.0 0.1 step_14_2.1
  97.1 1.2 %collective-permute-done.13.cols = bf16[256,768]{1,0:T(8,128)(2,1)S(1)} collective-permute-done((bf16[256,768]{1,0:T(8,128)(2,1)S(1)}, bf16[256,768]{1,0:T(8,128)(2,1)S(1)}, u32[]{:S(2)}, u32[]{:S(2)}) %collective-permute-start.13) | collective-permute-done | bytes 393248 | tf_op jit(solution)/shard_map/ppermute | solution.py:294
  98.3 1.4 %last.1 = (f32[2048,128]{1,0:T(8,128)S(1)}, bf16[2048,256]{1,0:T(8,128)(2,1)S(1)}, f32[8,128]{1,0:T(8,128)S(1)}) custom-call(bf16[2048,768]{1,0:T(8,128)(2,1)S(1)} %get-tuple-element.52.refs_0_.xv, f32[2,2048,128]{2,1,0:T(8,128)S(1)} %get-tuple-element.53.refs_1_.rowv, ...), custom_call_target="tpu_custom_call", output_to_operand_aliasing={{0}: (4, {})} | custom-call | flops 805306368 | bytes 1572864 | tf_op jit(solution)/shard_map/last/pallas_call | solution.py:187
  99.8 1.1 collective-permute-start.14
  100.8 0.0 collective-permute-start.15
  100.9 1.6 %collective-permute-start.16 = (f32[8,128]{1,0:T(8,128)S(1)}, f32[8,128]{1,0:T(8,128)S(1)}, u32[]{:S(2)}, u32[]{:S(2)}) collective-permute-start(f32[8,128]{1,0:T(8,128)S(1)} %get-tuple-element.101), channel_id=1, source_target_pairs={{0,3},{1,2},{2,1},{3,0},{4,7},{5,6},{6,5},{7,4}} | collective-permute-start | bytes 12296 | tf_op jit(solution)/shard_map/ppermute | solution.py:304
  102.5 3.4 %finish.1 = f32[2048,768]{1,0:T(8,128)} custom-call(bf16[2048,768]{1,0:T(8,128)(2,1)S(1)} %get-tuple-element.52.refs_0_.xv, f32[2048,768]{1,0:T(8,128)S(1)} %get-tuple-element.96.tv, f32[2048,128]{1,0:T(8,128)S(1)} %get-tuple-element.98.sv, bf16[2048,256]{1,0:T(8,128)(2,1)S(1)} %get-tuple-element.99.wv, ...), custom_call_target="tpu_custom_call", output_to_operand_aliasing={{}: (6, {})} | custom-call | flops 1572864000 | bytes 6291456 | tf_op jit(solution)/shard_map/finish/pallas_call | solution.py:229
  105.9 0.0 collective-permute-done.14
  105.9 0.6 add_reduce_fusion
  (9 shorter events, 0.0 us)
Async XLA Ops:
  1.3 1.9 %copy-start = (bf16[2048,768]{1,0:T(8,128)(2,1)S(1)}, bf16[2048,768]{1,0:T(8,128)(2,1)}, u32[]{:S(2)}) copy-start(bf16[2048,768]{1,0:T(8,128)(2,1)} %raw_hbm.1) | copy-start | bytes 9437188
  3.2 0.7 copy-start.1
  6.7 21.0 %collective-permute-start.2 = (bf16[2048,768]{1,0:T(8,128)(2,1)S(1)}, bf16[2048,768]{1,0:T(8,128)(2,1)S(1)}, u32[]{:S(2)}, u32[]{:S(2)}) collective-permute-start(bf16[2048,768]{1,0:T(8,128)(2,1)S(1)} %get-tuple-element.52.refs_0_.xv), channel_id=1, source_target_pairs={{0,1},{1,0},{2,3},{3,2},{4,5},{5,4},{6,7},{7,6}} | collective-permute-start | bytes 9437192 | tf_op jit(solution)/shard_map/ppermute | solution.py:284
  7.5 20.3 %collective-permute-start.1 = (f32[40,128]{1,0:T(8,128)S(1)}, f32[40,128]{1,0:T(8,128)S(1)}, u32[]{:S(2)}, u32[]{:S(2)}) collective-permute-start(f32[40,128]{1,0:T(8,128)S(1)} %get-tuple-element.54.refs_2_.my_info), channel_id=1, source_target_pairs={{0,1},{1,0},{2,3},{3,2},{4,5},{5,4},{6,7},{7,6}} | collective-permute-start | bytes 61448 | tf_op jit(solution)/shard_map/ppermute | solution.py:279
  7.5 31.9 %collective-permute-start = (f32[40,128]{1,0:T(8,128)S(1)}, f32[40,128]{1,0:T(8,128)S(1)}, u32[]{:S(2)}, u32[]{:S(2)}) collective-permute-start(f32[40,128]{1,0:T(8,128)S(1)} %get-tuple-element.54.refs_2_.my_info), channel_id=1, source_target_pairs={{0,2},{1,3},{2,0},{3,1},{4,6},{5,7},{6,4},{7,5}} | collective-permute-start | bytes 61448 | tf_op jit(solution)/shard_map/ppermute | solution.py:278
  8.8 30.6 %collective-permute-start.8 = (bf16[256,768]{1,0:T(8,128)(2,1)S(1)}, bf16[256,768]{1,0:T(8,128)(2,1)S(1)}, u32[]{:S(2)}, u32[]{:S(2)}) collective-permute-start(bf16[256,768]{1,0:T(8,128)(2,1)S(1)} %slice_select_fusion), channel_id=1, source_target_pairs={{0,2},{1,3},{2,0},{3,1},{4,6},{5,7},{6,4},{7,5}} | collective-permute-start | bytes 1179656 | tf_op jit(solution)/shard_map/ppermute | solution.py:276
  9.3 35.7 %collective-permute-start.7 = (bf16[512,768]{1,0:T(8,128)(2,1)S(1)}, bf16[512,768]{1,0:T(8,128)(2,1)S(1)}, u32[]{:S(2)}, u32[]{:S(2)}) collective-permute-start(bf16[512,768]{1,0:T(8,128)(2,1)S(1)} %get-tuple-element.102), channel_id=1, source_target_pairs={{0,2},{1,3},{2,0},{3,1},{4,6},{5,7},{6,4},{7,5}} | collective-permute-start | bytes 2359304 | tf_op jit(solution)/shard_map/ppermute | solution.py:282
  39.4 3.2 %collective-permute-start.9 = (bf16[256,768]{1,0:T(8,128)(2,1)S(1)}, bf16[256,768]{1,0:T(8,128)(2,1)S(1)}, u32[]{:S(2)}, u32[]{:S(2)}) collective-permute-start(bf16[256,768]{1,0:T(8,128)(2,1)S(1)} %collective-permute-done.8.refs_4_), channel_id=1, source_target_pairs={{0,1},{1,0},{2,3},{3,2},{4,5},{5,4},{6,7},{7,6}} | collective-permute-start | bytes 1179656 | tf_op jit(solution)/shard_map/ppermute | solution.py:294
  40.2 2.4 %collective-permute-start.4 = (f32[40,128]{1,0:T(8,128)S(1)}, f32[40,128]{1,0:T(8,128)S(1)}, u32[]{:S(2)}, u32[]{:S(2)}) collective-permute-start(f32[40,128]{1,0:T(8,128)S(1)} %collective-permute-done.refs_3_), channel_id=1, source_target_pairs={{0,1},{1,0},{2,3},{3,2},{4,5},{5,4},{6,7},{7,6}} | collective-permute-start | bytes 61448 | tf_op jit(solution)/shard_map/ppermute | solution.py:289
  45.0 2.4 %collective-permute-start.10 = (bf16[512,768]{1,0:T(8,128)(2,1)S(1)}, bf16[512,768]{1,0:T(8,128)(2,1)S(1)}, u32[]{:S(2)}, u32[]{:S(2)}) collective-permute-start(bf16[512,768]{1,0:T(8,128)(2,1)S(1)} %collective-permute-done.7.refs_4_), channel_id=1, source_target_pairs={{0,1},{1,0},{2,3},{3,2},{4,5},{5,4},{6,7},{7,6}} | collective-permute-start | bytes 2359304 | tf_op jit(solution)/shard_map/ppermute | solution.py:294
  45.5 19.1 %collective-permute-start.6 = (bf16[512,768]{1,0:T(8,128)(2,1)S(1)}, bf16[512,768]{1,0:T(8,128)(2,1)S(1)}, u32[]{:S(2)}, u32[]{:S(2)}) collective-permute-start(bf16[512,768]{1,0:T(8,128)(2,1)S(1)} %get-tuple-element.103), channel_id=1, source_target_pairs={{0,2},{1,3},{2,0},{3,1},{4,6},{5,7},{6,4},{7,5}} | collective-permute-start | bytes 2359304 | tf_op jit(solution)/shard_map/ppermute | solution.py:282
  64.5 2.8 %collective-permute-start.11 = (bf16[512,768]{1,0:T(8,128)(2,1)S(1)}, bf16[512,768]{1,0:T(8,128)(2,1)S(1)}, u32[]{:S(2)}, u32[]{:S(2)}) collective-permute-start(bf16[512,768]{1,0:T(8,128)(2,1)S(1)} %collective-permute-done.6.refs_4_), channel_id=1, source_target_pairs={{0,1},{1,0},{2,3},{3,2},{4,5},{5,4},{6,7},{7,6}} | collective-permute-start | bytes 2359304 | tf_op jit(solution)/shard_map/ppermute | solution.py:294
  65.4 19.1 %collective-permute-start.5 = (bf16[512,768]{1,0:T(8,128)(2,1)S(1)}, bf16[512,768]{1,0:T(8,128)(2,1)S(1)}, u32[]{:S(2)}, u32[]{:S(2)}) collective-permute-start(bf16[512,768]{1,0:T(8,128)(2,1)S(1)} %get-tuple-element.104), channel_id=1, source_target_pairs={{0,2},{1,3},{2,0},{3,1},{4,6},{5,7},{6,4},{7,5}} | collective-permute-start | bytes 2359304 | tf_op jit(solution)/shard_map/ppermute | solution.py:282
  84.5 2.8 %collective-permute-start.12 = (bf16[512,768]{1,0:T(8,128)(2,1)S(1)}, bf16[512,768]{1,0:T(8,128)(2,1)S(1)}, u32[]{:S(2)}, u32[]{:S(2)}) collective-permute-start(bf16[512,768]{1,0:T(8,128)(2,1)S(1)} %collective-permute-done.5.refs_4_), channel_id=1, source_target_pairs={{0,1},{1,0},{2,3},{3,2},{4,5},{5,4},{6,7},{7,6}} | collective-permute-start | bytes 2359304 | tf_op jit(solution)/shard_map/ppermute | solution.py:294
  85.4 10.7 %collective-permute-start.3 = (bf16[256,768]{1,0:T(8,128)(2,1)S(1)}, bf16[256,768]{1,0:T(8,128)(2,1)S(1)}, u32[]{:S(2)}, u32[]{:S(2)}) collective-permute-start(bf16[256,768]{1,0:T(8,128)(2,1)S(1)} %slice.15), channel_id=1, source_target_pairs={{0,2},{1,3},{2,0},{3,1},{4,6},{5,7},{6,4},{7,5}} | collective-permute-start | bytes 1179656 | tf_op jit(solution)/shard_map/ppermute | solution.py:282
  96.1 2.2 %collective-permute-start.13 = (bf16[256,768]{1,0:T(8,128)(2,1)S(1)}, bf16[256,768]{1,0:T(8,128)(2,1)S(1)}, u32[]{:S(2)}, u32[]{:S(2)}) collective-permute-start(bf16[256,768]{1,0:T(8,128)(2,1)S(1)} %collective-permute-done.3.refs_4_), channel_id=1, source_target_pairs={{0,1},{1,0},{2,3},{3,2},{4,5},{5,4},{6,7},{7,6}} | collective-permute-start | bytes 1179656 | tf_op jit(solution)/shard_map/ppermute | solution.py:294
  99.8 6.1 %collective-permute-start.14 = (f32[8,128]{1,0:T(8,128)S(1)}, f32[8,128]{1,0:T(8,128)S(1)}, u32[]{:S(2)}, u32[]{:S(2)}) collective-permute-start(f32[8,128]{1,0:T(8,128)S(1)} %get-tuple-element.101), channel_id=1, source_target_pairs={{0,2},{1,3},{2,0},{3,1},{4,6},{5,7},{6,4},{7,5}} | collective-permute-start | bytes 12296 | tf_op jit(solution)/shard_map/ppermute | solution.py:304
  100.8 5.0 %collective-permute-start.15 = (f32[8,128]{1,0:T(8,128)S(1)}, f32[8,128]{1,0:T(8,128)S(1)}, u32[]{:S(2)}, u32[]{:S(2)}) collective-permute-start(f32[8,128]{1,0:T(8,128)S(1)} %get-tuple-element.101), channel_id=1, source_target_pairs={{0,1},{1,0},{2,3},{3,2},{4,5},{5,4},{6,7},{7,6}} | collective-permute-start | bytes 12296 | tf_op jit(solution)/shard_map/ppermute | solution.py:304
  100.9 5.0 %collective-permute-start.16 = (f32[8,128]{1,0:T(8,128)S(1)}, f32[8,128]{1,0:T(8,128)S(1)}, u32[]{:S(2)}, u32[]{:S(2)}) collective-permute-start(f32[8,128]{1,0:T(8,128)S(1)} %get-tuple-element.101), channel_id=1, source_target_pairs={{0,3},{1,2},{2,1},{3,0},{4,7},{5,6},{6,5},{7,4}} | collective-permute-start | bytes 12296 | tf_op jit(solution)/shard_map/ppermute | solution.py:304

commit v8 on v7

--- a/solution.py
+++ b/solution.py
@@ -19,10 +19,6 @@
 
 def count_of(info_ref):
     return jnp.max(info_ref[info_ref.shape[0] - 8:, :]).astype(jnp.int32)
-
-
-def live_tiles(info_ref):
-    return (count_of(info_ref) + FINISH_TILE - 1) // FINISH_TILE
 
 
 def prep_kernel(kappa, raw_hbm, q_hbm, count_ref, xv, rowv, info, forces, zeros, q_ref, sem, in_sems):
@@ -194,9 +190,9 @@
         name='last')(*ins)
 
 
-def finish_kernel(inv_len2, xv, tv, sv, wv, cols, my_info, blank, forces, buf, out_sems):
+def finish_kernel(inv_len2, xv, tv, sv, wv, cols, count_ref, blank, forces, buf, out_sems):
     del blank
-    num = live_tiles(my_info)
+    num = (count_ref[0] + FINISH_TILE - 1) // FINISH_TILE
 
     def out(i):
         return pltpu.make_async_copy(
@@ -229,7 +225,7 @@
     return pl.pallas_call(
         functools.partial(finish_kernel, 1.0 / width),
         out_shape=jax.ShapeDtypeStruct((rows, width), F32),
-        in_specs=[VMEM_SPEC] * (len(ins) - 1) + [HBM_SPEC], out_specs=HBM_SPEC,
+        in_specs=[VMEM_SPEC] * (len(ins) - 2) + [pl.BlockSpec(memory_space=pltpu.SMEM), HBM_SPEC], out_specs=HBM_SPEC,
         scratch_shapes=[pltpu.VMEM((4, FINISH_TILE, width), F32), pltpu.SemaphoreType.DMA((4,))],
         input_output_aliases={len(ins) - 1: 0},
         compiler_params=pltpu.CompilerParams(vmem_limit_bytes=VMEM_LIMIT),
@@ -260,7 +256,7 @@
         input_output_aliases={} if first else {len(ins) - 2: 0, len(ins) - 1: 1}, **common)(*ins)
 
 
-PIECES = (256, 512, 512, 512, 256)
+PIECES = (512, 512, 512, 256, 256)
 
 
 def solution(mesh):
@@ -302,7 +298,7 @@
         total = part
         for perm in (cross_perm, pair_perm, diag_perm):
             total = total + lax.ppermute(part, 'row', perm)
-        forces = finish(x, t_sum, s_sum, w_last, relay, info, blank)
+        forces = finish(x, t_sum, s_sum, w_last, relay, counts, blank)
         return forces, (0.5 * jnp.sum(total)).reshape(1)
 
     row_spec = P(('sys', 'row'), None)

time: 108 us -> 113 us (1.046)
  waiting for transfers between devices: 37.4 us -> 41.8 us
    ppermute x4, waiting for transfers between devices: 31.1 us -> 36.2 us  [per_device(): arrived.append(lax.ppermute(x[off:off + size], 'row', cross_perm))]
    pallas_call x11, Pallas kernels: 46.3 us -> 47.5 us  [step(): pl.pallas_call(kernel, out_shape=[pltpu.VMEM((rows, width), F32), pltpu.V...]
    ppermute x4, starting transfers between devices: 1.24 us -> 0.07 us  [per_device(): arrived.append(lax.ppermute(x[off:off + size], 'row', cross_perm))]
  transfers between devices with their start and end apart: 17 -> 17, of which waited for: 7 -> 8; matrix products, arithmetic and copies ran while one was open for 0% -> 0% of each run, Pallas kernels for 46% -> 45%
where the time goes in v8:
time: 113 us
  Pallas kernels  55.1 us (49%)
  waiting for transfers between devices  41.8 us (37%)
  starting transfers between devices  9 us (8%)
  between operations  3.28 us (3%)
  local copies, waits for them, and re-layouts  2.73 us (2%)
    pallas_call x11, Pallas kernels, step(): pl.pallas_call(kernel, out_shape=[pltpu.VMEM((rows, width), F32), pltpu.V...  47.5 us
    ppermute x4, waiting for transfers between devices, per_device(): arrived.append(lax.ppermute(x[off:off + size], 'row', cross_perm))  36.2 us
    ppermute x5, waiting for transfers between devices, per_device(): relay = lax.ppermute(piece, 'row', pair_perm)  5.63 us
    ppermute x5, starting transfers between devices, per_device(): relay = lax.ppermute(piece, 'row', pair_perm)  4 us
    pallas_call x1, Pallas kernels, finish(): pl.pallas_call(functools.partial(finish_kernel, 1.0 / width), out_shape=j...  3.27 us
    pallas_call x1, Pallas kernels, prep(): pl.pallas_call(functools.partial(prep_kernel, LOG2E * 0.5 / width), out_s...  2.87 us
    ppermute x3, starting transfers between devices, per_device(): total = total + lax.ppermute(part, 'row', perm)  2.65 us
    unnamed x4, local copies, waits for them, and re-layouts  2.58 us
  transfers between devices with their start and end apart: 17, of which 8 were waited for; matrix products, arithmetic and copies ran while one was open for 0% of the time, Pallas kernels for 45%

profile of v8, /device:TPU:5, one launch (start us, length us, event | category | flops | bytes accessed | tf_op | source)
XLA Modules:
  0.0 112.7 jit_solution(285842922830393151)
XLA Ops:
  1.3 1.9 %copy-done = bf16[2048,768]{1,0:T(8,128)(2,1)S(1)} copy-done((bf16[2048,768]{1,0:T(8,128)(2,1)S(1)}, bf16[2048,768]{1,0:T(8,128)(2,1)}, u32[]{:S(2)}) %copy-start) | copy-done | bytes 3145752
  3.2 0.7 copy-done.1
  3.9 2.9 %prep.1 = (bf16[2048,768]{1,0:T(8,128)(2,1)S(1)}, f32[2,2048,128]{2,1,0:T(8,128)S(1)}, f32[40,128]{1,0:T(8,128)S(1)}, f32[2048,768]{1,0:T(8,128)}) custom-call(bf16[2048,768]{1,0:T(8,128)(2,1)S(1)} %copy-done, f32[16,128]{1,0:T(8,128)S(1)} %bitcast.4, s32[1]{0:T(128)} %copy.49.count_ref), custom_call_target="tpu_custom_call" | custom-call | tf_op jit(solution)/shard_map/prep/pallas_call | solution.py:81
  6.7 0.7 collective-permute-start.2
  7.5 0.0 collective-permute-start.1
  7.5 1.2 %collective-permute-start = (f32[40,128]{1,0:T(8,128)S(1)}, f32[40,128]{1,0:T(8,128)S(1)}, u32[]{:S(2)}, u32[]{:S(2)}) collective-permute-start(f32[40,128]{1,0:T(8,128)S(1)} %get-tuple-element.54.refs_2_), channel_id=1, source_target_pairs={{0,2},{1,3},{2,0},{3,1},{4,6},{5,7},{6,4},{7,5}} | collective-permute-start | bytes 61448 | tf_op jit(solution)/shard_map/ppermute | solution.py:274
  8.7 0.1 slice_select_fusion
  8.8 0.3 collective-permute-start.8
  9.1 17.2 %step_0_16.2 = (f32[2048,768]{1,0:T(8,128)S(1)}, f32[2048,128]{1,0:T(8,128)S(1)}) custom-call(bf16[2048,768]{1,0:T(8,128)(2,1)S(1)} %get-tuple-element.52.refs_0_.xv, f32[2,2048,128]{2,1,0:T(8,128)S(1)} %get-tuple-element.53.refs_1_.rowv, f32[40,128]{1,0:T(8,128)S(1)} %get-tuple-element.54.refs_2_), custom_call_target="tpu_custom_call" | custom-call | flops 7730940928 | bytes 1572864 | tf_op jit(solution)/shard_map/step_0_16/pallas_call | solution.py:252
  26.3 0.0 collective-permute-done.1.refs_3_
  26.3 11.5 %step_0_16.3 = (f32[2048,768]{1,0:T(8,128)S(1)}, f32[2048,128]{1,0:T(8,128)S(1)}) custom-call(bf16[2048,768]{1,0:T(8,128)(2,1)S(1)} %get-tuple-element.52.refs_0_.xv, f32[2,2048,128]{2,1,0:T(8,128)S(1)} %get-tuple-element.53.refs_1_.rowv, f32[40,128]{1,0:T(8,128)S(1)} %get-tuple-element.54.refs_2_, ...), custom_call_target="tpu_custom_call", output_to_operand_aliasing={{0}: (5, {}), {1}: (6, {})} | custom-call | flops 7730940928 | bytes 1572864 | tf_op jit(solution)/shard_map/step_0_16/pallas_call | solution.py:252
  37.8 0.0 collective-permute-done.refs_3_
  37.8 0.5 collective-permute-start.9
  38.4 0.1 fusion
  38.5 0.0 collective-permute-start.7
  38.5 0.0 collective-permute-start.4
  38.6 3.9 %step_0_4.2 = (f32[2048,768]{1,0:T(8,128)S(1)}, f32[2048,128]{1,0:T(8,128)S(1)}) custom-call(bf16[2048,768]{1,0:T(8,128)(2,1)S(1)} %get-tuple-element.52.refs_0_.xv, f32[2,2048,128]{2,1,0:T(8,128)S(1)} %get-tuple-element.53.refs_1_.rowv, f32[40,128]{1,0:T(8,128)S(1)} %get-tuple-element.54.refs_2_, ...), custom_call_target="tpu_custom_call", output_to_operand_aliasing={{0}: (5, {}), {1}: (6, {})} | custom-call | flops 1932735232 | bytes 1572864 | tf_op jit(solution)/shard_map/step_0_4/pallas_call | solution.py:252
  42.5 0.0 collective-permute-done.4.refs_3_.src_info
  42.5 4.1 %step_0_4.3 = (f32[2048,768]{1,0:T(8,128)S(1)}, f32[2048,128]{1,0:T(8,128)S(1)}) custom-call(bf16[2048,768]{1,0:T(8,128)(2,1)S(1)} %get-tuple-element.52.refs_0_.xv, f32[2,2048,128]{2,1,0:T(8,128)S(1)} %get-tuple-element.53.refs_1_.rowv, f32[40,128]{1,0:T(8,128)S(1)} %get-tuple-element.54.refs_2_, ...), custom_call_target="tpu_custom_call", output_to_operand_aliasing={{0}: (5, {}), {1}: (6, {})} | custom-call | flops 1932735232 | bytes 1572864 | tf_op jit(solution)/shard_map/step_0_4/pallas_call | solution.py:252
  46.6 11.0 %collective-permute-done.7.refs_4_ = bf16[512,768]{1,0:T(8,128)(2,1)S(1)} collective-permute-done((bf16[512,768]{1,0:T(8,128)(2,1)S(1)}, bf16[512,768]{1,0:T(8,128)(2,1)S(1)}, u32[]{:S(2)}, u32[]{:S(2)}) %collective-permute-start.7) | collective-permute-done | bytes 786464 | tf_op jit(solution)/shard_map/ppermute | solution.py:278
  57.6 0.9 collective-permute-start.10
  58.5 0.0 collective-permute-start.6
  58.5 0.1 step_4_4.2
  58.6 1.8 %collective-permute-done.10.refs_4_ = bf16[512,768]{1,0:T(8,128)(2,1)S(1)} collective-permute-done((bf16[512,768]{1,0:T(8,128)(2,1)S(1)}, bf16[512,768]{1,0:T(8,128)(2,1)S(1)}, u32[]{:S(2)}, u32[]{:S(2)}) %collective-permute-start.10) | collective-permute-done | bytes 786464 | tf_op jit(solution)/shard_map/ppermute | solution.py:290
  60.4 3.9 %step_4_4.3 = (f32[2048,768]{1,0:T(8,128)S(1)}, f32[2048,128]{1,0:T(8,128)S(1)}) custom-call(bf16[2048,768]{1,0:T(8,128)(2,1)S(1)} %get-tuple-element.52.refs_0_.xv, f32[2,2048,128]{2,1,0:T(8,128)S(1)} %get-tuple-element.53.refs_1_.rowv, f32[40,128]{1,0:T(8,128)S(1)} %get-tuple-element.54.refs_2_, ...), custom_call_target="tpu_custom_call", output_to_operand_aliasing={{0}: (5, {}), {1}: (6, {})} | custom-call | flops 1932735232 | bytes 1572864 | tf_op jit(solution)/shard_map/step_4_4/pallas_call | solution.py:252
  64.3 13.3 %collective-permute-done.6.refs_4_ = bf16[512,768]{1,0:T(8,128)(2,1)S(1)} collective-permute-done((bf16[512,768]{1,0:T(8,128)(2,1)S(1)}, bf16[512,768]{1,0:T(8,128)(2,1)S(1)}, u32[]{:S(2)}, u32[]{:S(2)}) %collective-permute-start.6) | collective-permute-done | bytes 786464 | tf_op jit(solution)/shard_map/ppermute | solution.py:278
  77.6 0.9 collective-permute-start.11
  78.4 0.1 fusion.1
  78.5 0.0 collective-permute-start.5
  78.5 0.4 step_8_4.2
  78.9 1.5 %collective-permute-done.11.refs_4_ = bf16[512,768]{1,0:T(8,128)(2,1)S(1)} collective-permute-done((bf16[512,768]{1,0:T(8,128)(2,1)S(1)}, bf16[512,768]{1,0:T(8,128)(2,1)S(1)}, u32[]{:S(2)}, u32[]{:S(2)}) %collective-permute-start.11) | collective-permute-done | bytes 786464 | tf_op jit(solution)/shard_map/ppermute | solution.py:290
  80.3 3.9 %step_8_4.3 = (f32[2048,768]{1,0:T(8,128)S(1)}, f32[2048,128]{1,0:T(8,128)S(1)}) custom-call(bf16[2048,768]{1,0:T(8,128)(2,1)S(1)} %get-tuple-element.52.refs_0_.xv, f32[2,2048,128]{2,1,0:T(8,128)S(1)} %get-tuple-element.53.refs_1_.rowv, f32[40,128]{1,0:T(8,128)S(1)} %get-tuple-element.54.refs_2_, ...), custom_call_target="tpu_custom_call", output_to_operand_aliasing={{0}: (5, {}), {1}: (6, {})} | custom-call | flops 1932735232 | bytes 1572864 | tf_op jit(solution)/shard_map/step_8_4/pallas_call | solution.py:252
  84.2 4.9 %collective-permute-done.5.refs_4_ = bf16[256,768]{1,0:T(8,128)(2,1)S(1)} collective-permute-done((bf16[256,768]{1,0:T(8,128)(2,1)S(1)}, bf16[256,768]{1,0:T(8,128)(2,1)S(1)}, u32[]{:S(2)}, u32[]{:S(2)}) %collective-permute-start.5) | collective-permute-done | bytes 393248 | tf_op jit(solution)/shard_map/ppermute | solution.py:278
  89.2 0.9 collective-permute-start.12
  90.0 0.0 collective-permute-start.3
  90.0 0.1 step_12_2.2
  90.2 1.2 %collective-permute-done.12.refs_4_ = bf16[256,768]{1,0:T(8,128)(2,1)S(1)} collective-permute-done((bf16[256,768]{1,0:T(8,128)(2,1)S(1)}, bf16[256,768]{1,0:T(8,128)(2,1)S(1)}, u32[]{:S(2)}, u32[]{:S(2)}) %collective-permute-start.12) | collective-permute-done | bytes 393248 | tf_op jit(solution)/shard_map/ppermute | solution.py:290
  91.4 2.3 %step_12_2.3 = (f32[2048,768]{1,0:T(8,128)S(1)}, f32[2048,128]{1,0:T(8,128)S(1)}) custom-call(bf16[2048,768]{1,0:T(8,128)(2,1)S(1)} %get-tuple-element.52.refs_0_.xv, f32[2,2048,128]{2,1,0:T(8,128)S(1)} %get-tuple-element.53.refs_1_.rowv, f32[40,128]{1,0:T(8,128)S(1)} %get-tuple-element.54.refs_2_, ...), custom_call_target="tpu_custom_call", output_to_operand_aliasing={{0}: (5, {}), {1}: (6, {})} | custom-call | flops 966367616 | bytes 1572864 | tf_op jit(solution)/shard_map/step_12_2/pallas_call | solution.py:252
  93.7 7.0 %collective-permute-done.3.refs_4_ = bf16[256,768]{1,0:T(8,128)(2,1)S(1)} collective-permute-done((bf16[256,768]{1,0:T(8,128)(2,1)S(1)}, bf16[256,768]{1,0:T(8,128)(2,1)S(1)}, u32[]{:S(2)}, u32[]{:S(2)}) %collective-permute-start.3) | collective-permute-done | bytes 393248 | tf_op jit(solution)/shard_map/ppermute | solution.py:278
  100.7 0.9 collective-permute-start.13
  101.6 0.1 step_14_2.1
  101.7 1.2 %collective-permute-done.13.cols = bf16[256,768]{1,0:T(8,128)(2,1)S(1)} collective-permute-done((bf16[256,768]{1,0:T(8,128)(2,1)S(1)}, bf16[256,768]{1,0:T(8,128)(2,1)S(1)}, u32[]{:S(2)}, u32[]{:S(2)}) %collective-permute-start.13) | collective-permute-done | bytes 393248 | tf_op jit(solution)/shard_map/ppermute | solution.py:290
  102.9 1.4 %last.1 = (f32[2048,128]{1,0:T(8,128)S(1)}, bf16[2048,256]{1,0:T(8,128)(2,1)S(1)}, f32[8,128]{1,0:T(8,128)S(1)}) custom-call(bf16[2048,768]{1,0:T(8,128)(2,1)S(1)} %get-tuple-element.52.refs_0_.xv, f32[2,2048,128]{2,1,0:T(8,128)S(1)} %get-tuple-element.53.refs_1_.rowv, ...), custom_call_target="tpu_custom_call", output_to_operand_aliasing={{0}: (4, {})} | custom-call | flops 805306368 | bytes 1572864 | tf_op jit(solution)/shard_map/last/pallas_call | solution.py:183
  104.4 1.0 collective-permute-start.14
  105.4 0.0 collective-permute-start.15
  105.4 1.6 %collective-permute-start.16 = (f32[8,128]{1,0:T(8,128)S(1)}, f32[8,128]{1,0:T(8,128)S(1)}, u32[]{:S(2)}, u32[]{:S(2)}) collective-permute-start(f32[8,128]{1,0:T(8,128)S(1)} %get-tuple-element.101), channel_id=1, source_target_pairs={{0,3},{1,2},{2,1},{3,0},{4,7},{5,6},{6,5},{7,4}} | collective-permute-start | bytes 12296 | tf_op jit(solution)/shard_map/ppermute | solution.py:300
  107.0 3.3 %finish.1 = f32[2048,768]{1,0:T(8,128)} custom-call(bf16[2048,768]{1,0:T(8,128)(2,1)S(1)} %get-tuple-element.52.refs_0_.xv, f32[2048,768]{1,0:T(8,128)S(1)} %get-tuple-element.96.tv, f32[2048,128]{1,0:T(8,128)S(1)} %get-tuple-element.98.sv, bf16[2048,256]{1,0:T(8,128)(2,1)S(1)} %get-tuple-element.99.wv, ...), custom_call_target="tpu_custom_call", output_to_operand_aliasing={{}: (6, {})} | custom-call | flops 1572864000 | bytes 6291456 | tf_op jit(solution)/shard_map/finish/pallas_call | solution.py:225
  110.3 0.6 add_reduce_fusion
  (9 shorter events, 0.0 us)
Async XLA Ops:
  1.3 1.9 %copy-start = (bf16[2048,768]{1,0:T(8,128)(2,1)S(1)}, bf16[2048,768]{1,0:T(8,128)(2,1)}, u32[]{:S(2)}) copy-start(bf16[2048,768]{1,0:T(8,128)(2,1)} %raw_hbm.1) | copy-start | bytes 9437188
  3.2 0.7 copy-start.1
  6.7 19.6 %collective-permute-start.2 = (bf16[2048,768]{1,0:T(8,128)(2,1)S(1)}, bf16[2048,768]{1,0:T(8,128)(2,1)S(1)}, u32[]{:S(2)}, u32[]{:S(2)}) collective-permute-start(bf16[2048,768]{1,0:T(8,128)(2,1)S(1)} %get-tuple-element.52.refs_0_.xv), channel_id=1, source_target_pairs={{0,1},{1,0},{2,3},{3,2},{4,5},{5,4},{6,7},{7,6}} | collective-permute-start | bytes 9437192 | tf_op jit(solution)/shard_map/ppermute | solution.py:280
  7.5 18.9 %collective-permute-start.1 = (f32[40,128]{1,0:T(8,128)S(1)}, f32[40,128]{1,0:T(8,128)S(1)}, u32[]{:S(2)}, u32[]{:S(2)}) collective-permute-start(f32[40,128]{1,0:T(8,128)S(1)} %get-tuple-element.54.refs_2_), channel_id=1, source_target_pairs={{0,1},{1,0},{2,3},{3,2},{4,5},{5,4},{6,7},{7,6}} | collective-permute-start | bytes 61448 | tf_op jit(solution)/shard_map/ppermute | solution.py:275
  7.5 30.3 %collective-permute-start = (f32[40,128]{1,0:T(8,128)S(1)}, f32[40,128]{1,0:T(8,128)S(1)}, u32[]{:S(2)}, u32[]{:S(2)}) collective-permute-start(f32[40,128]{1,0:T(8,128)S(1)} %get-tuple-element.54.refs_2_), channel_id=1, source_target_pairs={{0,2},{1,3},{2,0},{3,1},{4,6},{5,7},{6,4},{7,5}} | collective-permute-start | bytes 61448 | tf_op jit(solution)/shard_map/ppermute | solution.py:274
  8.8 29.0 %collective-permute-start.8 = (bf16[512,768]{1,0:T(8,128)(2,1)S(1)}, bf16[512,768]{1,0:T(8,128)(2,1)S(1)}, u32[]{:S(2)}, u32[]{:S(2)}) collective-permute-start(bf16[512,768]{1,0:T(8,128)(2,1)S(1)} %slice_select_fusion), channel_id=1, source_target_pairs={{0,2},{1,3},{2,0},{3,1},{4,6},{5,7},{6,4},{7,5}} | collective-permute-start | bytes 2359304 | tf_op jit(solution)/shard_map/ppermute | solution.py:272
  37.8 4.7 %collective-permute-start.9 = (bf16[512,768]{1,0:T(8,128)(2,1)S(1)}, bf16[512,768]{1,0:T(8,128)(2,1)S(1)}, u32[]{:S(2)}, u32[]{:S(2)}) collective-permute-start(bf16[512,768]{1,0:T(8,128)(2,1)S(1)} %collective-permute-done.8.refs_4_), channel_id=1, source_target_pairs={{0,1},{1,0},{2,3},{3,2},{4,5},{5,4},{6,7},{7,6}} | collective-permute-start | bytes 2359304 | tf_op jit(solution)/shard_map/ppermute | solution.py:290
  38.5 19.1 %collective-permute-start.7 = (bf16[512,768]{1,0:T(8,128)(2,1)S(1)}, bf16[512,768]{1,0:T(8,128)(2,1)S(1)}, u32[]{:S(2)}, u32[]{:S(2)}) collective-permute-start(bf16[512,768]{1,0:T(8,128)(2,1)S(1)} %get-tuple-element.102), channel_id=1, source_target_pairs={{0,2},{1,3},{2,0},{3,1},{4,6},{5,7},{6,4},{7,5}} | collective-permute-start | bytes 2359304 | tf_op jit(solution)/shard_map/ppermute | solution.py:278
  38.5 4.0 %collective-permute-start.4 = (f32[40,128]{1,0:T(8,128)S(1)}, f32[40,128]{1,0:T(8,128)S(1)}, u32[]{:S(2)}, u32[]{:S(2)}) collective-permute-start(f32[40,128]{1,0:T(8,128)S(1)} %collective-permute-done.refs_3_), channel_id=1, source_target_pairs={{0,1},{1,0},{2,3},{3,2},{4,5},{5,4},{6,7},{7,6}} | collective-permute-start | bytes 61448 | tf_op jit(solution)/shard_map/ppermute | solution.py:285
  57.6 2.8 %collective-permute-start.10 = (bf16[512,768]{1,0:T(8,128)(2,1)S(1)}, bf16[512,768]{1,0:T(8,128)(2,1)S(1)}, u32[]{:S(2)}, u32[]{:S(2)}) collective-permute-start(bf16[512,768]{1,0:T(8,128)(2,1)S(1)} %collective-permute-done.7.refs_4_), channel_id=1, source_target_pairs={{0,1},{1,0},{2,3},{3,2},{4,5},{5,4},{6,7},{7,6}} | collective-permute-start | bytes 2359304 | tf_op jit(solution)/shard_map/ppermute | solution.py:290
  58.5 19.1 %collective-permute-start.6 = (bf16[512,768]{1,0:T(8,128)(2,1)S(1)}, bf16[512,768]{1,0:T(8,128)(2,1)S(1)}, u32[]{:S(2)}, u32[]{:S(2)}) collective-permute-start(bf16[512,768]{1,0:T(8,128)(2,1)S(1)} %get-tuple-element.103), channel_id=1, source_target_pairs={{0,2},{1,3},{2,0},{3,1},{4,6},{5,7},{6,4},{7,5}} | collective-permute-start | bytes 2359304 | tf_op jit(solution)/shard_map/ppermute | solution.py:278
  77.6 2.8 %collective-permute-start.11 = (bf16[512,768]{1,0:T(8,128)(2,1)S(1)}, bf16[512,768]{1,0:T(8,128)(2,1)S(1)}, u32[]{:S(2)}, u32[]{:S(2)}) collective-permute-start(bf16[512,768]{1,0:T(8,128)(2,1)S(1)} %collective-permute-done.6.refs_4_), channel_id=1, source_target_pairs={{0,1},{1,0},{2,3},{3,2},{4,5},{5,4},{6,7},{7,6}} | collective-permute-start | bytes 2359304 | tf_op jit(solution)/shard_map/ppermute | solution.py:290
  78.5 10.7 %collective-permute-start.5 = (bf16[256,768]{1,0:T(8,128)(2,1)S(1)}, bf16[256,768]{1,0:T(8,128)(2,1)S(1)}, u32[]{:S(2)}, u32[]{:S(2)}) collective-permute-start(bf16[256,768]{1,0:T(8,128)(2,1)S(1)} %get-tuple-element.104), channel_id=1, source_target_pairs={{0,2},{1,3},{2,0},{3,1},{4,6},{5,7},{6,4},{7,5}} | collective-permute-start | bytes 1179656 | tf_op jit(solution)/shard_map/ppermute | solution.py:278
  89.2 2.2 %collective-permute-start.12 = (bf16[256,768]{1,0:T(8,128)(2,1)S(1)}, bf16[256,768]{1,0:T(8,128)(2,1)S(1)}, u32[]{:S(2)}, u32[]{:S(2)}) collective-permute-start(bf16[256,768]{1,0:T(8,128)(2,1)S(1)} %collective-permute-done.5.refs_4_), channel_id=1, source_target_pairs={{0,1},{1,0},{2,3},{3,2},{4,5},{5,4},{6,7},{7,6}} | collective-permute-start | bytes 1179656 | tf_op jit(solution)/shard_map/ppermute | solution.py:290
  90.0 10.7 %collective-permute-start.3 = (bf16[256,768]{1,0:T(8,128)(2,1)S(1)}, bf16[256,768]{1,0:T(8,128)(2,1)S(1)}, u32[]{:S(2)}, u32[]{:S(2)}) collective-permute-start(bf16[256,768]{1,0:T(8,128)(2,1)S(1)} %get-tuple-element.105), channel_id=1, source_target_pairs={{0,2},{1,3},{2,0},{3,1},{4,6},{5,7},{6,4},{7,5}} | collective-permute-start | bytes 1179656 | tf_op jit(solution)/shard_map/ppermute | solution.py:278
  100.7 2.2 %collective-permute-start.13 = (bf16[256,768]{1,0:T(8,128)(2,1)S(1)}, bf16[256,768]{1,0:T(8,128)(2,1)S(1)}, u32[]{:S(2)}, u32[]{:S(2)}) collective-permute-start(bf16[256,768]{1,0:T(8,128)(2,1)S(1)} %collective-permute-done.3.refs_4_), channel_id=1, source_target_pairs={{0,1},{1,0},{2,3},{3,2},{4,5},{5,4},{6,7},{7,6}} | collective-permute-start | bytes 1179656 | tf_op jit(solution)/shard_map/ppermute | solution.py:290
  104.4 5.9 %collective-permute-start.14 = (f32[8,128]{1,0:T(8,128)S(1)}, f32[8,128]{1,0:T(8,128)S(1)}, u32[]{:S(2)}, u32[]{:S(2)}) collective-permute-start(f32[8,128]{1,0:T(8,128)S(1)} %get-tuple-element.101), channel_id=1, source_target_pairs={{0,2},{1,3},{2,0},{3,1},{4,6},{5,7},{6,4},{7,5}} | collective-permute-start | bytes 12296 | tf_op jit(solution)/shard_map/ppermute | solution.py:300
  105.4 4.9 %collective-permute-start.15 = (f32[8,128]{1,0:T(8,128)S(1)}, f32[8,128]{1,0:T(8,128)S(1)}, u32[]{:S(2)}, u32[]{:S(2)}) collective-permute-start(f32[8,128]{1,0:T(8,128)S(1)} %get-tuple-element.101), channel_id=1, source_target_pairs={{0,1},{1,0},{2,3},{3,2},{4,5},{5,4},{6,7},{7,6}} | collective-permute-start | bytes 12296 | tf_op jit(solution)/shard_map/ppermute | solution.py:300
  105.4 4.9 %collective-permute-start.16 = (f32[8,128]{1,0:T(8,128)S(1)}, f32[8,128]{1,0:T(8,128)S(1)}, u32[]{:S(2)}, u32[]{:S(2)}) collective-permute-start(f32[8,128]{1,0:T(8,128)S(1)} %get-tuple-element.101), channel_id=1, source_target_pairs={{0,3},{1,2},{2,1},{3,0},{4,7},{5,6},{6,5},{7,4}} | collective-permute-start | bytes 12296 | tf_op jit(solution)/shard_map/ppermute | solution.py:300
